TPU v7x, 32 devices: a whole 2x2x4 slice. The times are simulated.
32 devices in a mesh: seq: 16 (over z, x, core), exp: 2 (over y).
Axes of the slice: x: 2, y: 2, z: 4, core: 2. Of those that a mesh axis runs over, the one named last changes fastest.
Arguments:
- queries: bfloat16 [6144, 1536], P('seq', 'exp'), may hold values from -120 to 120
- key_heads: bfloat16 [6144, 1536], P('seq', 'exp'), may hold values from -6 to 6
- value_heads: bfloat16 [6144, 1024], P('seq', 'exp'), may hold values from -6 to 6
- block_layout: int32 [48, 16], P('seq'), may hold values from 0 to 21, as said below
- out_weight: bfloat16 [1024, 2048], P('exp'), may hold values from -0.1875 to 0.1875
- norm_gain: float32 [2048], replicated, may hold values from 0.5 to 1.5
- expert_ids: int32 [6144, 1], P(('seq', 'exp')), may hold values from 0 to 1; in each aligned block of 192 rows (0 to 191, 192 to 383, ...) at most 144 rows name the same one
- route_weight: float32 [6144, 1], P(('seq', 'exp')), may hold values from 0.1 to 1
- gate_weight: bfloat16 [2, 2048, 704], P('exp'), may hold values from -0.125 to 0.125
- up_weight: bfloat16 [2, 2048, 704], P('exp'), may hold values from -0.125 to 0.125
- down_weight: bfloat16 [2, 704, 2048], P('exp'), may hold values from -0.21875 to 0.21875
Outputs:
- layer_out: bfloat16 [6144, 2048], P(('seq', 'exp'))
Inputs may be any that keep to these rules, and one draw needn't show every extreme that they name: `block_layout`: each row holds the offset 0 and 15 other distinct offsets. `expert_ids`: among the 192 tokens of one device in the expert layer (aligned blocks of rows) at most 144 name the same expert.
All inputs are finite; a program needn't handle non-finite values.
Results may differ from a plain program's by a relative error of at most 0.02.
Values may be sent and summed in bfloat16 or wider, within the bound.
No kernel may reach another device: no remote copies, remote signals or barrier semaphores. Data moves between devices by JAX's collectives and lax.ppermute only.
A program may use at most 128 MiB of HBM per device.

v0:
```python
import functools

import jax
import jax.numpy as jnp
from jax import lax
from jax.experimental import pallas as pl
from jax.experimental.pallas import tpu as pltpu
from jax.sharding import PartitionSpec as P


QK = 192
VD = 128
BLK = 128
SPAN = 22
NEG = -1e30
LOG2E = 1.4426950408889634
F32 = jnp.float32
BF16 = jnp.bfloat16
MIB = 1 << 20


def ceil_to(value, step):
    return -(-value // step) * step


def vmem():
    return pl.BlockSpec(memory_space=pltpu.VMEM)


def params(mib):
    return pltpu.CompilerParams(vmem_limit_bytes=mib * MIB)


def anywhere():
    return pl.BlockSpec(memory_space=pl.ANY)


def in_hbm(array):
    return pltpu.with_memory_space_constraint(array, pltpu.HBM)


def pack_kv_kernel(group, k_ref, v_ref, *refs):
    outs, (k_buf, kt, sem) = refs[:group], refs[group:]
    own = lax.axis_index("seq") % group
    tokens = k_ref.shape[0]
    blocks = tokens // BLK
    loads = []
    for t in range(blocks):
        rows = slice(t * BLK, (t + 1) * BLK)
        loads.append(pltpu.make_async_copy(k_ref.at[rows, :], k_buf.at[rows, :], sem.at[t]))
    stores = []
    for d in range(group):
        cols = pl.ds(pl.multiple_of((own ^ d) * VD, VD), VD)
        for t in range(blocks):
            rows = slice(t * BLK, (t + 1) * BLK)
            stores.append(
                pltpu.make_async_copy(
                    v_ref.at[rows, cols], outs[d].at[QK : QK + VD, rows], sem.at[blocks * (d + 1) + t]
                )
            )
    for copy in loads + stores:
        copy.start()
    for t in range(blocks):
        rows = slice(t * BLK, (t + 1) * BLK)
        loads[t].wait()
        kt[:, rows] = k_buf[rows, :].T
    for d in range(group):
        outs[d][:QK, :] = kt[pl.ds(pl.multiple_of((own ^ d) * QK, 16), QK), :]
    for copy in stores:
        copy.wait()


def pack_kv(k, v, group):
    tokens = k.shape[0]
    return pl.pallas_call(
        functools.partial(pack_kv_kernel, group),
        out_shape=[pltpu.VMEM((QK + VD, tokens), BF16)] * group,
        in_specs=[anywhere(), anywhere()],
        out_specs=[vmem()] * group,
        scratch_shapes=[
            pltpu.VMEM(k.shape, BF16),
            pltpu.VMEM((k.shape[1], tokens), BF16),
            pltpu.SemaphoreType.DMA(((group + 1) * (tokens // BLK),)),
        ],
        compiler_params=params(8),
        cost_estimate=pl.CostEstimate(flops=1 << 20, transcendentals=0, bytes_accessed=1 << 20),
        name="pack_kv",
    )(in_hbm(k), in_hbm(v))


def pack_q_kernel(group, phases, layout_hbm, q_ref, w_ref, down_ref, after_ref, *refs):
    outs, (w_out, down_out), (layout_ref, q_buf, qt, sem) = refs[:group], refs[group : group + 2], refs[group + 2 :]
    seq = lax.axis_index("seq")
    own, plane = seq % group, seq // group
    tokens = q_ref.shape[0]
    blocks, chosen = layout_ref.shape
    plane_blocks = group * blocks
    aug = outs[0].shape[0] - QK
    width, quarter = w_out.shape[1], down_out.shape[1]
    loads = []
    for t in range(tokens // BLK):
        rows = slice(t * BLK, (t + 1) * BLK)
        loads.append(pltpu.make_async_copy(q_ref.at[rows, :], q_buf.at[rows, :], sem.at[t]))
    layout_load = pltpu.make_async_copy(layout_hbm, layout_ref, sem.at[blocks])
    down_load = pltpu.make_async_copy(
        down_ref.at[0, :, pl.ds(pl.multiple_of(own * quarter, 128), quarter)], down_out, sem.at[blocks + 1]
    )
    w_load = pltpu.make_async_copy(
        w_ref.at[:, pl.ds(pl.multiple_of((seq % 2) * width, 128), width)], w_out, sem.at[blocks + 2]
    )
    for copy in [layout_load] + loads + [down_load, w_load]:
        copy.start()
    row = lax.broadcasted_iota(jnp.int32, (aug, BLK), 0)
    phase = jnp.zeros_like(row)
    for p in range(1, phases):
        phase = phase + (row >= p * plane_blocks).astype(jnp.int32)
    exists = (phase <= plane) & (row < phases * plane_blocks)
    layout_load.wait()
    for t in range(tokens // BLK):
        rows = slice(t * BLK, (t + 1) * BLK)
        offset = own * blocks + t + 2 * plane_blocks * phase - row
        hit = offset == layout_ref[t, 0]
        for c in range(1, chosen):
            hit = hit | (offset == layout_ref[t, c])
        mask = jnp.where(hit & exists, F32(0.0), F32(NEG)).astype(BF16)
        for d in range(group):
            outs[d][QK:, rows] = mask
        loads[t].wait()
        qt[:, rows] = q_buf[rows, :].T
    for d in range(group):
        outs[d][:QK, :] = qt[pl.ds(pl.multiple_of((own ^ d) * QK, 16), QK), :]
    down_load.wait()
    w_load.wait()


def pack_q(q, layout, w, down, earlier, group, phases):
    tokens = q.shape[0]
    aug = ceil_to(phases * group * layout.shape[0], 16)
    w_part = pltpu.VMEM((w.shape[0], w.shape[1] // 2), BF16)
    down_part = pltpu.VMEM((down.shape[1], down.shape[2] // group), BF16)
    return pl.pallas_call(
        functools.partial(pack_q_kernel, group, phases),
        out_shape=[pltpu.VMEM((QK + aug, tokens), BF16)] * group + [w_part, down_part],
        in_specs=[anywhere()] * 5,
        out_specs=[vmem()] * (group + 2),
        scratch_shapes=[
            pltpu.SMEM(layout.shape, jnp.int32),
            pltpu.VMEM(q.shape, BF16),
            pltpu.VMEM((q.shape[1], tokens), BF16),
            pltpu.SemaphoreType.DMA((layout.shape[0] + 3,)),
        ],
        compiler_params=params(8),
        cost_estimate=pl.CostEstimate(flops=1 << 20, transcendentals=0, bytes_accessed=1 << 20),
        name="pack_q",
    )(in_hbm(layout), in_hbm(q), in_hbm(w), in_hbm(down), earlier)


def select_index(values, own):
    picked = jnp.int32(values[0])
    for at in range(1, len(values)):
        picked = jnp.where(own == at, jnp.int32(values[at]), picked)
    return picked


def attend_kernel(group, tables, phase, first, last, shards_seen, rows_step, *refs):
    refs = list(refs)

    def take(count):
        taken = refs[:count]
        del refs[:count]
        return taken

    if first:
        q_in = take(group)
    else:
        q_ref, m_in, acc_in = take(3)
    kv_refs = take(len(tables))
    if first:
        q_ref, m_out, acc_out = take(3)
    elif last:
        outs = take(2 * group)
        context = refs.pop()
    else:
        m_out, acc_out = take(2)
    kaug, vaug, s_ref = refs
    own = lax.axis_index("seq") % group
    tokens = kv_refs[0].shape[1]
    blocks = tokens // BLK
    aug = kaug.shape[0] - QK
    scale = F32(QK**-0.5 * LOG2E)
    if first:
        depth = q_in[0].shape[0]
        for d in range(group):
            for t in range(blocks):
                rows = slice(d * tokens + t * BLK, d * tokens + (t + 1) * BLK)
                q_ref[rows, :depth] = q_in[d][:, t * BLK : (t + 1) * BLK].T
                if depth < q_ref.shape[1]:
                    q_ref[rows, depth:] = jnp.zeros((BLK, q_ref.shape[1] - depth), BF16)
    row = lax.broadcasted_iota(jnp.int32, (aug, BLK), 0)
    at = 0
    for (count, table), ref in zip(tables, kv_refs):
        for c in range(count):
            base = c * (QK + VD)
            kaug[:QK, at * tokens : (at + 1) * tokens] = ref[base : base + QK, :]
            shard = select_index(table[c], own)
            for t in range(blocks):
                part = slice(at * tokens + t * BLK, at * tokens + (t + 1) * BLK)
                here = (phase * group + shard) * blocks + t
                kaug[QK:, part] = jnp.where(row == here, F32(1.0), F32(0.0)).astype(BF16)
                vaug[part, :VD] = ref[base + QK : base + QK + VD, t * BLK : (t + 1) * BLK]
                vaug[part, VD:] = jnp.ones((BLK, VD), BF16)
            at += 1

    def step(rows, slot, diagonal):
        s_now = s_ref.at[slot]
        s_now[...] = jnp.dot(q_ref[rows, :], kaug[...], preferred_element_type=F32)
        if first:
            lower = lax.broadcasted_iota(jnp.int32, (BLK, BLK), 0) >= lax.broadcasted_iota(
                jnp.int32, (BLK, BLK), 1
            )
            for t in range(rows_step // BLK):
                tile = (slice(t * BLK, (t + 1) * BLK), slice(diagonal + t * BLK, diagonal + (t + 1) * BLK))
                s_now[tile] = jnp.where(lower, s_now[tile], F32(NEG))
        peak = jnp.max(s_now[...], axis=1, keepdims=True)
        if not first:
            before = m_in[rows, :1]
            peak = jnp.maximum(peak, before)
        weights = jnp.exp2((s_now[...] - peak) * scale).astype(BF16)
        acc = jnp.dot(weights, vaug[...], preferred_element_type=F32)
        if not first:
            acc = acc + acc_in[rows, :] * jnp.exp2((before - peak) * scale)
        if last:
            context[rows, :] = (acc[:, :VD] / acc[:, VD:]).astype(BF16)
        else:
            m_out[rows, :] = jnp.broadcast_to(peak, (rows_step, m_out.shape[1]))
            acc_out[rows, :] = acc

    per = tokens // rows_step
    count = 0
    for shard in range(group):
        for r in range(per):
            if first:
                start = shard * tokens + r * rows_step
                step(slice(start, start + rows_step), count % 2, start)
                count += 1
                continue
            rows = pl.ds(pl.multiple_of((own ^ shard) * tokens + r * rows_step, rows_step), rows_step)
            if shard in shards_seen:
                step(rows, count % 2, 0)
                count += 1
            elif last:
                context[rows, :] = (acc_in[rows, :VD] / acc_in[rows, VD:]).astype(BF16)
    if last:
        half = tokens // 2
        part = lax.axis_index("exp")
        for d in range(group):
            outs[d][...] = context[d * tokens : (d + 1) * tokens, :]
            at = pl.multiple_of(d * tokens + part * half, 16)
            outs[group + d][...] = context[pl.ds(at, half), :]


def attend(group, tables, phase, kv, q_in=None, state=None, last=False, shards_seen=(), rows_step=128):
    first = state is None
    tokens = kv[0].shape[1]
    total = group * tokens
    keys = sum(count for count, _ in tables) * tokens
    depth = q_in[0].shape[0] if first else state[0].shape[1]
    depth = ceil_to(depth, 128)
    outs = [pltpu.VMEM((total, 128), F32), pltpu.VMEM((total, 2 * VD), F32)]
    scratch = [
        pltpu.VMEM((depth, keys), BF16),
        pltpu.VMEM((keys, 2 * VD), BF16),
        pltpu.VMEM((2, rows_step, keys), F32),
    ]
    aliases = {}
    if first:
        inputs = list(q_in)
        outs = [pltpu.VMEM((total, depth), BF16)] + outs
    elif last:
        inputs = list(state)
        outs = [pltpu.VMEM((tokens, VD), BF16)] * group + [pltpu.VMEM((tokens // 2, VD), BF16)] * group
        scratch = scratch + [pltpu.VMEM((total, VD), BF16)]
    else:
        inputs = list(state)
        aliases = {1: 0, 2: 1}
    inputs = inputs + list(kv)
    queries = total if first else len(shards_seen) * tokens
    return pl.pallas_call(
        functools.partial(attend_kernel, group, tables, phase, first, last, shards_seen, rows_step),
        out_shape=outs,
        in_specs=[vmem()] * len(inputs),
        out_specs=[vmem()] * len(outs),
        scratch_shapes=scratch,
        input_output_aliases=aliases,
        compiler_params=params(20),
        cost_estimate=pl.CostEstimate(
            flops=4 * queries * keys * 256, transcendentals=queries * keys, bytes_accessed=1 << 20
        ),
    )(*inputs)


def gather_kernel(group, plan, *refs):
    parts, outs = refs[: -len(plan)], refs[-len(plan) :]
    own = lax.axis_index("seq") % group
    size = QK + VD
    for g in range(group):

        @pl.when(own == g)
        def _():
            for out, places in zip(outs, plan):
                for at, place in enumerate(places):
                    part, c = place[g]
                    out[at * size : (at + 1) * size, :] = parts[part][c * size : (c + 1) * size, :]


def gather(group, plan, parts):
    outs = [pltpu.VMEM((len(p) * (QK + VD), parts[0].shape[1]), BF16) for p in plan]
    return pl.pallas_call(
        functools.partial(gather_kernel, group, plan),
        out_shape=outs,
        in_specs=[vmem()] * len(parts),
        out_specs=[vmem()] * len(outs),
        compiler_params=params(8),
        cost_estimate=pl.CostEstimate(flops=1 << 20, transcendentals=0, bytes_accessed=1 << 20),
    )(*parts)


def own_tokens_kernel(group, *refs):
    pieces, out_ref = refs[:group], refs[group]
    half = pieces[0].shape[0] // 2
    rows = pl.ds(pl.multiple_of((1 - lax.axis_index("exp")) * half, 16), half)
    for d in range(group):
        out_ref[d * half : (d + 1) * half, :] = pieces[d][rows, :]


def own_tokens(pieces):
    group = len(pieces)
    return pl.pallas_call(
        functools.partial(own_tokens_kernel, group),
        out_shape=pltpu.VMEM((group * pieces[0].shape[0] // 2, pieces[0].shape[1]), BF16),
        in_specs=[vmem()] * group,
        out_specs=vmem(),
        compiler_params=params(8),
        cost_estimate=pl.CostEstimate(flops=1 << 20, transcendentals=0, bytes_accessed=1 << 20),
        name="own_tokens",
    )(*pieces)


def pack_columns(ref, value):
    ref[: value.shape[0], :] = value[:, :128]
    rest = value[:, 128:]
    half = value.shape[0] // 2
    ref[value.shape[0] :, :] = jnp.concatenate([rest[:half], rest[half:]], axis=1)


def unpack_columns(ref, rows):
    rest = ref[rows:, :]
    return jnp.concatenate(
        [ref[:rows, :], jnp.concatenate([rest[:, :64], rest[:, 64:]], axis=0)], axis=1
    )


def hidden_kernel(group, mine, eps, *refs):
    pieces, refs = refs[: group + (1 if mine else group)], refs[group + (1 if mine else group) :]
    w_own, w_same, w_swap, gain, gate_w, up_w = refs[:6]
    refs = refs[6:]
    if mine:
        ids, down_own, attended_ref, partial_ref, ctx, att = refs
    else:
        hidden_ref, ctx, att = refs
    seq, part = lax.axis_index("seq"), lax.axis_index("exp")
    own = seq % group
    side = seq % 2
    rows_here = ctx.shape[0]
    which = part if mine else 1 - part
    rows = pl.ds(pl.multiple_of(which * rows_here, 16), rows_here)
    half = group * VD
    for d in range(group):
        at = pl.multiple_of((own ^ d) * VD, VD)
        ctx[:, pl.ds(at, VD)] = pieces[d][rows, :]
        if mine:
            ctx[:, pl.ds(half + at, VD)] = pieces[group][d * rows_here : (d + 1) * rows_here, :]
        else:
            ctx[:, pl.ds(half + at, VD)] = pieces[group + d][...]
    width = w_own.shape[1] // 2
    for at, ref in ((side, w_same), (1 - side, w_swap)):
        cols = pl.ds(pl.multiple_of(at * width, 128), width)
        att[:, cols] = jnp.dot(ctx[:, :half], w_own[:, cols], preferred_element_type=F32) + jnp.dot(
            ctx[:, half:], ref[...], preferred_element_type=F32
        )
    attended = att[...]
    rescale = lax.rsqrt(jnp.mean(attended * attended, axis=1, keepdims=True) + F32(eps))
    normed = (attended * rescale * gain[...]).astype(BF16)
    across = (((1,), (1,)), ((), ()))
    gate = lax.dot_general(gate_w[0], normed, across, preferred_element_type=F32)
    up = lax.dot_general(up_w[0], normed, across, preferred_element_type=F32)
    hidden = (gate * jax.nn.sigmoid(gate) * up).astype(BF16)
    if mine:
        attended_ref[...] = attended
        routed = jnp.where(ids[...] == part, hidden.astype(F32), jnp.zeros(hidden.shape, F32)).astype(BF16)
        partial_ref[...] = jnp.dot(routed.T, down_own[0], preferred_element_type=F32)
    else:
        pack_columns(hidden_ref, hidden)


def hidden_part(group, pieces, w_own, w_same, w_swap, gain, gate_w, up_w, *extra):
    mine = bool(extra)
    rows = pieces[0].shape[0] // 2
    width = w_own.shape[1]
    inner = gate_w.shape[1]
    inputs = list(pieces) + [w_own, w_same, w_swap, gain, gate_w, up_w] + list(extra)
    if mine:
        outs = [pltpu.VMEM((rows, width), F32)] * 2
    else:
        outs = [pltpu.VMEM((inner * rows // 128, 128), BF16)]
    return pl.pallas_call(
        functools.partial(hidden_kernel, group, mine, 1e-06),
        out_shape=outs,
        in_specs=[vmem()] * len(inputs),
        out_specs=[vmem()] * len(outs),
        scratch_shapes=[pltpu.VMEM((rows, 2 * group * VD), BF16), pltpu.VMEM((rows, width), F32)],
        compiler_params=params(24),
        cost_estimate=pl.CostEstimate(
            flops=2 * rows * width * (2 * group * VD + 2 * inner), transcendentals=rows * inner, bytes_accessed=1 << 20
        ),
        name="hidden_own" if mine else "hidden_peer",
    )(*inputs)


def combine_kernel(group, attended, partial, hid_peer, ids, weight, *refs):
    down, out_ref = refs[:group], refs[group]
    own = lax.axis_index("seq") % group
    here = ids[...] == lax.axis_index("exp")
    hidden = unpack_columns(hid_peer, down[0].shape[0]).astype(F32)
    other = jnp.where(here, jnp.zeros(hidden.shape, F32), hidden).astype(BF16).T
    column = jnp.broadcast_to(weight[...], (128, weight.shape[1])).T[:, :1]
    width = out_ref.shape[1] // group
    for d in range(group):
        cols = pl.ds(pl.multiple_of((own ^ d) * width, 128), width)
        result = partial[:, cols] + jnp.dot(other, down[d][...], preferred_element_type=F32)
        result = result.astype(BF16).astype(F32)
        out_ref[:, cols] = (attended[:, cols] + column * result).astype(BF16)


def combine(group, attended, partial, hid_peer, ids, weight, down):
    inputs = [attended, partial, hid_peer, ids, weight] + list(down)
    return pl.pallas_call(
        functools.partial(combine_kernel, group),
        out_shape=jax.ShapeDtypeStruct(attended.shape, BF16),
        in_specs=[vmem()] * len(inputs),
        out_specs=vmem(),
        compiler_params=params(20),
        cost_estimate=pl.CostEstimate(flops=1 << 20, transcendentals=0, bytes_accessed=1 << 20),
        name="combine",
    )(*inputs)


def after(values, *earlier):
    return lax.optimization_barrier((tuple(values), earlier))[0]


def shards(
    queries,
    key_heads,
    value_heads,
    block_layout,
    out_weight,
    norm_gain,
    expert_ids,
    route_weight,
    gate_weight,
    up_weight,
    down_weight,
):
    peers = lax.axis_size("seq")
    group = value_heads.shape[1] // VD
    blocks = queries.shape[0] // BLK
    plane_blocks = group * blocks
    phases = 1 + -(-(SPAN - 1) // plane_blocks)

    def swap(array, d):
        return lax.ppermute(array, "seq", [(i, i ^ d) for i in range(peers)])

    def across(array):
        return lax.ppermute(array, "exp", [(0, 1), (1, 0)])

    def swap_across(array, d):
        pairs = [(2 * i + e, 2 * (i ^ d) + 1 - e) for i in range(peers) for e in range(2)]
        return lax.ppermute(array, ("seq", "exp"), pairs)

    def forward(array):
        return lax.ppermute(array, "seq", [(i, i + group) for i in range(peers - group)])

    def needed(hop):
        return [
            shard
            for shard in range(group)
            if (shard + 1) * blocks - 1 >= plane_blocks * hop - (SPAN - 1)
        ]

    kv = pack_kv(key_heads, value_heads, group)
    held = [kv[0]] + [swap(kv[d], d) for d in range(1, group)]
    *qs, w_part, down_part = pack_q(
        queries, block_layout, out_weight, down_weight, kv[0], group, phases
    )
    qs = [qs[0]] + [swap(qs[d], d) for d in range(1, group)]
    down0 = across(down_part)
    w_same = across(w_part)

    tables = tuple((1, (tuple(g ^ d for g in range(group)),)) for d in range(group))
    early = group // 2
    joined = gather(group, (tuple(((d, 0),) * group for d in range(early)),), held[:early])[0]
    q_aug, peak, acc = attend(group, tables, 0, held, q_in=qs)
    (down0,) = after((down0,), peak)
    down2 = swap(down0, 2)

    tables = ((early, tuple(tables[d][1][0] for d in range(early))),) + tables[early:]
    parts = [joined] + held[early:]
    for hop in range(1, phases):
        if hop > 1:
            wanted = needed(hop)
            flat = [(at, c, table[c]) for at, (count, table) in enumerate(tables) for c in range(count)]
            chains = []
            for g in range(group):
                there = sorted((f for f in flat if f[2][g] in wanted), key=lambda f: -f[2][g])
                head = [f for f in there if f[0] == 0][:1]
                chains.append(head + [f for f in there if f not in head])
            plans = [
                ((tuple((chains[g][k][0], chains[g][k][1]) for g in range(group)),),) for k in range(len(wanted))
            ]
            tables = tuple(
                (1, (tuple(chains[g][k][2][g] for g in range(group)),)) for k in range(len(wanted))
            )
            parts = [gather(group, plan, parts[:1] if k == 0 else parts)[0] for k, plan in enumerate(plans)]
        parts = [forward(part) for part in parts]

        def seen(those):
            highest = max(max(table[c]) for count, table in those for c in range(count))
            limit = highest * blocks + blocks - 1 + SPAN - 1 - plane_blocks * hop
            return tuple(shard for shard in range(group) if shard * blocks <= limit)

        state = (q_aug, peak, acc)
        if hop < phases - 1:
            peak, acc = attend(group, tables, hop, parts, state=state, shards_seen=seen(tables))
        else:
            peak, acc = attend(
                group, tables[:-1], hop, parts[:-1], state=state, shards_seen=seen(tables[:-1])
            )
            down0, down2 = after((down0, down2), peak)
            down1 = swap(down0, 1)
            down3 = swap(down2, 1)
            context = attend(
                group,
                tables[-1:],
                hop,
                parts[-1:],
                state=(q_aug, peak, acc),
                last=True,
                shards_seen=seen(tables[-1:]),
            )
    (w_same,) = after((w_same,), context[0])
    w_swap = swap(w_same, 1)
    whole, first = context[:group], context[group:]
    same = [whole[0]] + [swap(whole[d], d) for d in range(1, group)]
    other = [across(first[0])] + [swap_across(first[d], d) for d in range(1, group)]
    mine = [across(own_tokens(same))]
    gain = norm_gain.reshape(1, -1)
    weights = (out_weight, w_same, w_swap, gain, gate_weight.swapaxes(1, 2), up_weight.swapaxes(1, 2))
    ids = expert_ids.reshape(1, -1)
    (hid_out,) = hidden_part(group, same + other, *weights)
    hid_peer = across(hid_out)
    attended, partial = hidden_part(group, same + mine, *weights, ids, down_weight)
    return combine(
        group, attended, partial, hid_peer, ids, route_weight.reshape(1, -1), (down0, down1, down2, down3)
    )


def solution(mesh):
    in_specs = (
        P("seq", "exp"),
        P("seq", "exp"),
        P("seq", "exp"),
        P("seq", None),
        P("exp", None),
        P(),
        P(("seq", "exp"), None),
        P(("seq", "exp"), None),
        P("exp", None, None),
        P("exp", None, None),
        P("exp", None, None),
    )
    out_specs = P(("seq", "exp"), None)

    return jax.shard_map(shards, mesh=mesh, in_specs=in_specs, out_specs=out_specs, check_vma=False)
```

profile of v0, /device:TPU:0, one launch (start us, length us, event | category | flops | bytes accessed | tf_op | source)
XLA Modules:
  0.0 109.4 jit_solution(7339232091989976997)
XLA Ops:
  0.0 1.4 %pack_kv.1 = (bf16[320,384]{1,0:T(8,128)(2,1)S(1)}, bf16[320,384]{1,0:T(8,128)(2,1)S(1)}, bf16[320,384]{1,0:T(8,128)(2,1)S(1)}, bf16[320,384]{1,0:T(8,128)(2,1)S(1)}) custom-call(bf16[384,768]{1,0:T(8,128)(2,1)} %k_ref.1, bf16[384,512]{1,0:T(8,128)(2,1)} %v_ref.1), custom_call_target="tpu_custom_call" | custom-call | flops 1048576 | bytes 1048576 | tf_op jit(solution)/shard_map/pack_kv/pallas_call | solution.py:75
  1.5 0.6 collective-permute-start.3
  2.0 2.6 %collective-permute-start.4 = (bf16[320,384]{1,0:T(8,128)(2,1)S(1)}, bf16[320,384]{1,0:T(8,128)(2,1)S(1)}, u32[]{:S(2)}, u32[]{:S(2)}) collective-permute-start(bf16[320,384]{1,0:T(8,128)(2,1)S(1)} %get-tuple-element.42), channel_id=1, source_target_pairs={{0,4},{2,6},{4,0},{6,2},{8,12},{10,14},{12,8},{14,10},{16,20},{18,... | collective-permute-start | bytes 737288 | tf_op jit(solution)/shard_map/ppermute | solution.py:482
  4.6 0.0 collective-permute-start.5
  4.6 0.0 collective-permute-done.3.refs_5_.refs_1_
  4.6 0.1 shard_map.110
  4.7 3.8 %collective-permute-start.6 = (bf16[640,384]{1,0:T(8,128)(2,1)S(1)}, bf16[640,384]{1,0:T(8,128)(2,1)S(1)}, u32[]{:S(2)}, u32[]{:S(2)}) collective-permute-start(bf16[640,384]{1,0:T(8,128)(2,1)S(1)} %shard_map.110), channel_id=1, source_target_pairs={{0,8},{2,10},{4,12},{6,14},{8,16},{10,18},{12,20},{14,22},{16,24},... | collective-permute-start | bytes 1474568 | tf_op jit(solution)/shard_map/ppermute | solution.py:492
  8.4 1.8 %pack_q.1 = (bf16[240,384]{1,0:T(8,128)(2,1)S(1)}, bf16[240,384]{1,0:T(8,128)(2,1)S(1)}, bf16[240,384]{1,0:T(8,128)(2,1)S(1)}, bf16[240,384]{1,0:T(8,128)(2,1)S(...) custom-call(s32[3,16]{1,0:T(4,128)} %layout_hbm.1, bf16[384,768]{1,0:T(8,128)(2,1)} %q_ref.1, ...), custom_call_target="tpu_custom_call" | custom-call | flops 1048576 | bytes 1048576 | tf_op jit(solution)/shard_map/pack_q/pallas_call | solution.py:141
  10.3 1.6 %collective-permute-start.23 = (bf16[704,512]{1,0:T(8,128)(2,1)S(1)}, bf16[704,512]{1,0:T(8,128)(2,1)S(1)}, u32[]{:S(2)}, u32[]{:S(2)}) collective-permute-start(bf16[704,512]{1,0:T(8,128)(2,1)S(1)} %get-tuple-element.63), channel_id=1, source_target_pairs={{0,1},{1,0},{2,3},{3,2},{4,5},{5,4},{6,7},{7,6},{8,9},{9,8},{10,11... | collective-permute-start | bytes 2162696 | tf_op jit(solution)/shard_map/ppermute | solution.py:485
  11.8 0.5 collective-permute-start.16
  12.4 0.0 collective-permute-done.4.refs_6_
  12.4 3.5 %collective-permute-start.7 = (bf16[320,384]{1,0:T(8,128)(2,1)S(1)}, bf16[320,384]{1,0:T(8,128)(2,1)S(1)}, u32[]{:S(2)}, u32[]{:S(2)}) collective-permute-start(bf16[320,384]{1,0:T(8,128)(2,1)S(1)} %collective-permute-done.4.refs_6_), channel_id=1, source_target_pairs={{0,8},{2,10},{4,12},{6,14},{8,16},{10,18},{12,20},{14,22},{16,24},... | collective-permute-start | bytes 737288 | tf_op jit(solution)/shard_map/ppermute | solution.py:492
  15.8 0.3 collective-permute-done.5.refs_7_
  16.1 3.5 %collective-permute-start.8 = (bf16[320,384]{1,0:T(8,128)(2,1)S(1)}, bf16[320,384]{1,0:T(8,128)(2,1)S(1)}, u32[]{:S(2)}, u32[]{:S(2)}) collective-permute-start(bf16[320,384]{1,0:T(8,128)(2,1)S(1)} %collective-permute-done.5.refs_7_), channel_id=1, source_target_pairs={{0,8},{2,10},{4,12},{6,14},{8,16},{10,18},{12,20},{14,22},{16,24},... | collective-permute-start | bytes 737288 | tf_op jit(solution)/shard_map/ppermute | solution.py:492
  19.6 5.7 %collective-permute-done.7.refs_4_.refs_1_ = bf16[320,384]{1,0:T(8,128)(2,1)S(1)} collective-permute-done((bf16[320,384]{1,0:T(8,128)(2,1)S(1)}, bf16[320,384]{1,0:T(8,128)(2,1)S(1)}, u32[]{:S(2)}, u32[]{:S(2)}) %collective-permute-start.7) | collective-permute-done | bytes 245792 | tf_op jit(solution)/shard_map/ppermute | solution.py:492
  25.3 0.0 collective-permute-start
  25.3 4.6 %collective-permute-done.8.refs_5_.refs_2_ = bf16[320,384]{1,0:T(8,128)(2,1)S(1)} collective-permute-done((bf16[320,384]{1,0:T(8,128)(2,1)S(1)}, bf16[320,384]{1,0:T(8,128)(2,1)S(1)}, u32[]{:S(2)}, u32[]{:S(2)}) %collective-permute-start.8) | collective-permute-done | bytes 245792 | tf_op jit(solution)/shard_map/ppermute | solution.py:492
  29.9 1.5 %collective-permute-start.1 = (bf16[240,384]{1,0:T(8,128)(2,1)S(1)}, bf16[240,384]{1,0:T(8,128)(2,1)S(1)}, u32[]{:S(2)}, u32[]{:S(2)}) collective-permute-start(bf16[240,384]{1,0:T(8,128)(2,1)S(1)} %get-tuple-element.39), channel_id=1, source_target_pairs={{0,4},{2,6},{4,0},{6,2},{8,12},{10,14},{12,8},{14,10},{16,20},{18,... | collective-permute-start | bytes 552968 | tf_op jit(solution)/shard_map/ppermute | solution.py:482
  31.4 0.0 collective-permute-done.6.refs_3_.refs_0_
  31.4 0.0 collective-permute-start.2
  31.5 0.1 shard_map.113
  31.5 4.4 %collective-permute-start.9 = (bf16[320,384]{1,0:T(8,128)(2,1)S(1)}, bf16[320,384]{1,0:T(8,128)(2,1)S(1)}, u32[]{:S(2)}, u32[]{:S(2)}) collective-permute-start(bf16[320,384]{1,0:T(8,128)(2,1)S(1)} %shard_map.112), channel_id=1, source_target_pairs={{0,8},{2,10},{4,12},{6,14},{8,16},{10,18},{12,20},{14,22},{16,24},... | collective-permute-start | bytes 737288 | tf_op jit(solution)/shard_map/ppermute | solution.py:492
  35.9 1.5 %collective-permute-done.1.refs_2_ = bf16[240,384]{1,0:T(8,128)(2,1)S(1)} collective-permute-done((bf16[240,384]{1,0:T(8,128)(2,1)S(1)}, bf16[240,384]{1,0:T(8,128)(2,1)S(1)}, u32[]{:S(2)}, u32[]{:S(2)}) %collective-permute-start.1) | collective-permute-done | bytes 184352 | tf_op jit(solution)/shard_map/ppermute | solution.py:482
  37.4 4.4 %collective-permute-start.10 = (bf16[320,384]{1,0:T(8,128)(2,1)S(1)}, bf16[320,384]{1,0:T(8,128)(2,1)S(1)}, u32[]{:S(2)}, u32[]{:S(2)}) collective-permute-start(bf16[320,384]{1,0:T(8,128)(2,1)S(1)} %shard_map.113), channel_id=1, source_target_pairs={{0,8},{2,10},{4,12},{6,14},{8,16},{10,18},{12,20},{14,22},{16,24},... | collective-permute-start | bytes 737288 | tf_op jit(solution)/shard_map/ppermute | solution.py:492
  41.8 0.0 collective-permute-done.2.refs_3_
  41.8 3.6 %shard_map.109 = (bf16[1536,256]{1,0:T(8,128)(2,1)S(1)}, f32[1536,128]{1,0:T(8,128)S(1)}, f32[1536,256]{1,0:T(8,128)S(1)}) custom-call(bf16[240,384]{1,0:T(8,128)(2,1)S(1)} %get-tuple-element.37.refs_0_, bf16[240,384]{1,0:T(8,128)(2,1)S(1)} %collective-permute-done.refs_1_, bf16[240,384]{1,0:T(8,128)(2,1)S(1)} %collective-permute-done.1.refs_2_, ...), custom_call_target="tpu_custom_call" | custom-call | flops 2415919104 | bytes 1048576 | tf_op jit(solution)/shard_map/pallas_call | solution.py:288
  45.5 0.0 collective-permute-done.23.refs_0_
  45.5 0.1 shard_map.115
  45.6 3.7 %collective-permute-start.11 = (bf16[320,384]{1,0:T(8,128)(2,1)S(1)}, bf16[320,384]{1,0:T(8,128)(2,1)S(1)}, u32[]{:S(2)}, u32[]{:S(2)}) collective-permute-start(bf16[320,384]{1,0:T(8,128)(2,1)S(1)} %shard_map.115), channel_id=1, source_target_pairs={{0,8},{2,10},{4,12},{6,14},{8,16},{10,18},{12,20},{14,22},{16,24},... | collective-permute-start | bytes 737288 | tf_op jit(solution)/shard_map/ppermute | solution.py:492
  49.2 0.0 copy-start.3
  49.3 3.9 %shard_map.111 = (f32[1536,128]{1,0:T(8,128)S(1)}, f32[1536,256]{1,0:T(8,128)S(1)}) custom-call(bf16[1536,256]{1,0:T(8,128)(2,1)S(1)} %get-tuple-element.44.refs_0_, f32[1536,128]{1,0:T(8,128)S(1)} %get-tuple-element.45.refs_1_, f32[1536,256]{1,0:T(8,128)S(1)} %get-tuple-element.46.refs_2_, ...), custom_call_target="tpu_custom_call", output_to_operand_aliasing={{0}: (1, {}), {1}: (2, {})} | custom-call | flops 2415919104 | bytes 1048576 | tf_op jit(solution)/shard_map/pallas_call | solution.py:288
  53.2 0.0 collective-permute-done.10.refs_4_
  53.2 0.0 copy-start.2
  53.2 1.8 %shard_map.114 = (f32[1536,128]{1,0:T(8,128)S(1)}, f32[1536,256]{1,0:T(8,128)S(1)}) custom-call(bf16[1536,256]{1,0:T(8,128)(2,1)S(1)} %get-tuple-element.44.refs_0_, f32[1536,128]{1,0:T(8,128)S(1)} %get-tuple-element.47.refs_1_, f32[1536,256]{1,0:T(8,128)S(1)} %get-tuple-element.48.refs_2_, ...), custom_call_target="tpu_custom_call", output_to_operand_aliasing={{0}: (1, {}), {1}: (2, {})} | custom-call | flops 905969664 | bytes 1048576 | tf_op jit(solution)/shard_map/pallas_call | solution.py:288
  55.1 0.0 copy-start
  55.1 0.0 copy-start.4
  55.1 1.7 %shard_map.116 = (bf16[384,128]{1,0:T(8,128)(2,1)S(1)}, bf16[384,128]{1,0:T(8,128)(2,1)S(1)}, bf16[384,128]{1,0:T(8,128)(2,1)S(1)}, bf16[384,128]{1,0:T(8,128)(2...) custom-call(bf16[1536,256]{1,0:T(8,128)(2,1)S(1)} %get-tuple-element, ...), custom_call_target="tpu_custom_call" | custom-call | flops 301989888 | bytes 1048576 | tf_op jit(solution)/shard_map/pallas_call | solution.py:288
  56.8 0.0 collective-permute-done.16.refs_6_.refs_9_
  56.8 0.1 collective-permute-start.17
  56.9 1.6 %collective-permute-start.24 = (bf16[704,512]{1,0:T(8,128)(2,1)S(1)}, bf16[704,512]{1,0:T(8,128)(2,1)S(1)}, u32[]{:S(2)}, u32[]{:S(2)}) collective-permute-start(bf16[704,512]{1,0:T(8,128)(2,1)S(1)} %collective-permute-done.23.refs_0_), channel_id=1, source_target_pairs={{0,4},{2,6},{4,0},{6,2},{8,12},{10,14},{12,8},{14,10},{16,20},{18,... | collective-permute-start | bytes 2162696 | tf_op jit(solution)/shard_map/ppermute | solution.py:482
  58.4 17.0 %collective-permute-done.24.refs_2_ = bf16[704,512]{1,0:T(8,128)(2,1)S(1)} collective-permute-done((bf16[704,512]{1,0:T(8,128)(2,1)S(1)}, bf16[704,512]{1,0:T(8,128)(2,1)S(1)}, u32[]{:S(2)}, u32[]{:S(2)}) %collective-permute-start.24) | collective-permute-done | bytes 720928 | tf_op jit(solution)/shard_map/ppermute | solution.py:482
  75.4 0.5 collective-permute-start.26
  75.9 1.5 %collective-permute-start.18 = (bf16[192,128]{1,0:T(8,128)(2,1)S(1)}, bf16[192,128]{1,0:T(8,128)(2,1)S(1)}, u32[]{:S(2)}, u32[]{:S(2)}) collective-permute-start(bf16[192,128]{1,0:T(8,128)(2,1)S(1)} %get-tuple-element.59), channel_id=1, source_target_pairs={{0,1},{1,0},{2,3},{3,2},{4,5},{5,4},{6,7},{7,6},{8,9},{9,8},{10,11... | collective-permute-start | bytes 147464 | tf_op jit(solution)/shard_map/ppermute | solution.py:485
  77.5 0.0 collective-permute-start.12
  77.5 2.6 %collective-permute-done.18.refs_4_ = bf16[192,128]{1,0:T(8,128)(2,1)S(1)} collective-permute-done((bf16[192,128]{1,0:T(8,128)(2,1)S(1)}, bf16[192,128]{1,0:T(8,128)(2,1)S(1)}, u32[]{:S(2)}, u32[]{:S(2)}) %collective-permute-start.18) | collective-permute-done | bytes 49184 | tf_op jit(solution)/shard_map/ppermute | solution.py:485
  80.0 0.0 collective-permute-start.19
  80.0 4.0 %collective-permute-done.19.refs_5_ = bf16[192,128]{1,0:T(8,128)(2,1)S(1)} collective-permute-done((bf16[192,128]{1,0:T(8,128)(2,1)S(1)}, bf16[192,128]{1,0:T(8,128)(2,1)S(1)}, u32[]{:S(2)}, u32[]{:S(2)}) %collective-permute-start.19) | collective-permute-done | bytes 49184 | tf_op jit(solution)/shard_map/ppermute | solution.py:489
  84.0 1.5 %collective-permute-start.13 = (bf16[384,128]{1,0:T(8,128)(2,1)S(1)}, bf16[384,128]{1,0:T(8,128)(2,1)S(1)}, u32[]{:S(2)}, u32[]{:S(2)}) collective-permute-start(bf16[384,128]{1,0:T(8,128)(2,1)S(1)} %get-tuple-element.53), channel_id=1, source_target_pairs={{0,4},{2,6},{4,0},{6,2},{8,12},{10,14},{12,8},{14,10},{16,20},{18,... | collective-permute-start | bytes 294920 | tf_op jit(solution)/shard_map/ppermute | solution.py:482
  85.5 3.7 %collective-permute-done.13.refs_2_ = bf16[384,128]{1,0:T(8,128)(2,1)S(1)} collective-permute-done((bf16[384,128]{1,0:T(8,128)(2,1)S(1)}, bf16[384,128]{1,0:T(8,128)(2,1)S(1)}, u32[]{:S(2)}, u32[]{:S(2)}) %collective-permute-start.13) | collective-permute-done | bytes 98336 | tf_op jit(solution)/shard_map/ppermute | solution.py:482
  89.1 2.5 %collective-permute-start.20 = (bf16[192,128]{1,0:T(8,128)(2,1)S(1)}, bf16[192,128]{1,0:T(8,128)(2,1)S(1)}, u32[]{:S(2)}, u32[]{:S(2)}) collective-permute-start(bf16[192,128]{1,0:T(8,128)(2,1)S(1)} %get-tuple-element.61), channel_id=1, source_target_pairs={{0,5},{1,4},{2,7},{3,6},{4,1},{5,0},{6,3},{7,2},{8,13},{9,12},{10,... | collective-permute-start | bytes 147464 | tf_op jit(solution)/shard_map/ppermute | solution.py:489
  91.6 0.0 collective-permute-done.14.refs_3_
  91.6 0.5 collective-permute-start.21
  92.1 2.0 %collective-permute-done.20.refs_6_ = bf16[192,128]{1,0:T(8,128)(2,1)S(1)} collective-permute-done((bf16[192,128]{1,0:T(8,128)(2,1)S(1)}, bf16[192,128]{1,0:T(8,128)(2,1)S(1)}, u32[]{:S(2)}, u32[]{:S(2)}) %collective-permute-start.20) | collective-permute-done | bytes 49184 | tf_op jit(solution)/shard_map/ppermute | solution.py:489
  94.1 0.7 collective-permute-start.15
  94.8 1.5 %collective-permute-done.21.refs_7_ = bf16[192,128]{1,0:T(8,128)(2,1)S(1)} collective-permute-done((bf16[192,128]{1,0:T(8,128)(2,1)S(1)}, bf16[192,128]{1,0:T(8,128)(2,1)S(1)}, u32[]{:S(2)}, u32[]{:S(2)}) %collective-permute-start.21) | collective-permute-done | bytes 49184 | tf_op jit(solution)/shard_map/ppermute | solution.py:489
  96.3 0.0 copy-start.1
  96.3 0.0 copy-start.5
  96.3 3.1 %hidden_peer.1 = bf16[1056,128]{1,0:T(8,128)(2,1)S(1)} custom-call(bf16[384,128]{1,0:T(8,128)(2,1)S(1)} %get-tuple-element.51.refs_0_, bf16[384,128]{1,0:T(8,128)(2,1)S(1)} %collective-permute-done.12.refs_1_, bf16[384,128]{1,0:T(8,128)(2,1)S(1)} %collective-permute-done.13.refs_2_, bf16[384,128]{1,0:T(8,128)(2,1)S(1)} %collective-permute-done.14.refs_3_, ...), custom_call_target="tpu_custom_call" | custom-call | flops 1912602624 | bytes 1048576 | tf_op jit(solution)/shard_map/hidden_peer/pallas_call | solution.py:416
  99.4 0.8 collective-permute-start.22
  100.2 0.0 copy-start.6
  100.2 3.8 %hidden_own.1 = (f32[192,2048]{1,0:T(8,128)S(1)}, f32[192,2048]{1,0:T(8,128)S(1)}) custom-call(bf16[384,128]{1,0:T(8,128)(2,1)S(1)} %get-tuple-element.51.refs_0_, bf16[384,128]{1,0:T(8,128)(2,1)S(1)} %collective-permute-done.12.refs_1_, bf16[384,128]{1,0:T(8,128)(2,1)S(1)} %collective-permute-done.13.refs_2_, ...), custom_call_target="tpu_custom_call" | custom-call | flops 1912602624 | bytes 1048576 | tf_op jit(solution)/shard_map/hidden_own/pallas_call | solution.py:416
  104.0 0.0 collective-permute-done.26.refs_3_
  104.0 3.5 %collective-permute-done.22.hid_peer = bf16[1056,128]{1,0:T(8,128)(2,1)S(1)} collective-permute-done((bf16[1056,128]{1,0:T(8,128)(2,1)S(1)}, bf16[1056,128]{1,0:T(8,128)(2,1)S(1)}, u32[]{:S(2)}, u32[]{:S(2)}) %collective-permute-start.22) | collective-permute-done | bytes 270368 | tf_op jit(solution)/shard_map/ppermute | solution.py:485
  107.5 1.9 %combine.1 = bf16[192,2048]{1,0:T(8,128)(2,1)} custom-call(f32[192,2048]{1,0:T(8,128)S(1)} %get-tuple-element.57.attended, f32[192,2048]{1,0:T(8,128)S(1)} %get-tuple-element.58.partial, bf16[1056,128]{1,0:T(8,128)(2,1)S(1)} %collective-permute-done.22.hid_peer, s32[1,192]{1,0:T(1,128)S(1)} %bitcast.12, f32[1,192]{1,0:T(1,128)S(1)} %bitcast.13, ...), custom_call_target="tpu_custom_call" | custom-call | flops 1048576 | bytes 1048576 | tf_op jit(solution)/shard_map/combine/pallas_call | solution.py:447
  (18 shorter events, 0.1 us)
Async XLA Ops:
  1.5 3.2 %collective-permute-start.3 = (bf16[320,384]{1,0:T(8,128)(2,1)S(1)}, bf16[320,384]{1,0:T(8,128)(2,1)S(1)}, u32[]{:S(2)}, u32[]{:S(2)}) collective-permute-start(bf16[320,384]{1,0:T(8,128)(2,1)S(1)} %get-tuple-element.41), channel_id=1, source_target_pairs={{0,2},{2,0},{4,6},{6,4},{8,10},{10,8},{12,14},{14,12},{16,18},{18,... | collective-permute-start | bytes 737288 | tf_op jit(solution)/shard_map/ppermute | solution.py:482
  2.0 10.3 %collective-permute-start.4 = (bf16[320,384]{1,0:T(8,128)(2,1)S(1)}, bf16[320,384]{1,0:T(8,128)(2,1)S(1)}, u32[]{:S(2)}, u32[]{:S(2)}) collective-permute-start(bf16[320,384]{1,0:T(8,128)(2,1)S(1)} %get-tuple-element.42), channel_id=1, source_target_pairs={{0,4},{2,6},{4,0},{6,2},{8,12},{10,14},{12,8},{14,10},{16,20},{18,... | collective-permute-start | bytes 737288 | tf_op jit(solution)/shard_map/ppermute | solution.py:482
  4.6 11.6 %collective-permute-start.5 = (bf16[320,384]{1,0:T(8,128)(2,1)S(1)}, bf16[320,384]{1,0:T(8,128)(2,1)S(1)}, u32[]{:S(2)}, u32[]{:S(2)}) collective-permute-start(bf16[320,384]{1,0:T(8,128)(2,1)S(1)} %get-tuple-element.43), channel_id=1, source_target_pairs={{0,6},{2,4},{4,2},{6,0},{8,14},{10,12},{12,10},{14,8},{16,22},{18,... | collective-permute-start | bytes 737288 | tf_op jit(solution)/shard_map/ppermute | solution.py:482
  4.7 26.7 %collective-permute-start.6 = (bf16[640,384]{1,0:T(8,128)(2,1)S(1)}, bf16[640,384]{1,0:T(8,128)(2,1)S(1)}, u32[]{:S(2)}, u32[]{:S(2)}) collective-permute-start(bf16[640,384]{1,0:T(8,128)(2,1)S(1)} %shard_map.110), channel_id=1, source_target_pairs={{0,8},{2,10},{4,12},{6,14},{8,16},{10,18},{12,20},{14,22},{16,24},... | collective-permute-start | bytes 1474568 | tf_op jit(solution)/shard_map/ppermute | solution.py:492
  10.3 35.2 %collective-permute-start.23 = (bf16[704,512]{1,0:T(8,128)(2,1)S(1)}, bf16[704,512]{1,0:T(8,128)(2,1)S(1)}, u32[]{:S(2)}, u32[]{:S(2)}) collective-permute-start(bf16[704,512]{1,0:T(8,128)(2,1)S(1)} %get-tuple-element.63), channel_id=1, source_target_pairs={{0,1},{1,0},{2,3},{3,2},{4,5},{5,4},{6,7},{7,6},{8,9},{9,8},{10,11... | collective-permute-start | bytes 2162696 | tf_op jit(solution)/shard_map/ppermute | solution.py:485
  11.8 44.9 %collective-permute-start.16 = (bf16[512,1024]{1,0:T(8,128)(2,1)S(1)}, bf16[512,1024]{1,0:T(8,128)(2,1)S(1)}, u32[]{:S(2)}, u32[]{:S(2)}) collective-permute-start(bf16[512,1024]{1,0:T(8,128)(2,1)S(1)} %get-tuple-element.55), channel_id=1, source_target_pairs={{0,1},{1,0},{2,3},{3,2},{4,5},{5,4},{6,7},{7,6},{8,9},{9,8},{10,11... | collective-permute-start | bytes 3145736 | tf_op jit(solution)/shard_map/ppermute | solution.py:485
  12.4 12.9 %collective-permute-start.7 = (bf16[320,384]{1,0:T(8,128)(2,1)S(1)}, bf16[320,384]{1,0:T(8,128)(2,1)S(1)}, u32[]{:S(2)}, u32[]{:S(2)}) collective-permute-start(bf16[320,384]{1,0:T(8,128)(2,1)S(1)} %collective-permute-done.4.refs_6_), channel_id=1, source_target_pairs={{0,8},{2,10},{4,12},{6,14},{8,16},{10,18},{12,20},{14,22},{16,24},... | collective-permute-start | bytes 737288 | tf_op jit(solution)/shard_map/ppermute | solution.py:492
  16.1 13.8 %collective-permute-start.8 = (bf16[320,384]{1,0:T(8,128)(2,1)S(1)}, bf16[320,384]{1,0:T(8,128)(2,1)S(1)}, u32[]{:S(2)}, u32[]{:S(2)}) collective-permute-start(bf16[320,384]{1,0:T(8,128)(2,1)S(1)} %collective-permute-done.5.refs_7_), channel_id=1, source_target_pairs={{0,8},{2,10},{4,12},{6,14},{8,16},{10,18},{12,20},{14,22},{16,24},... | collective-permute-start | bytes 737288 | tf_op jit(solution)/shard_map/ppermute | solution.py:492
  25.3 6.2 %collective-permute-start = (bf16[240,384]{1,0:T(8,128)(2,1)S(1)}, bf16[240,384]{1,0:T(8,128)(2,1)S(1)}, u32[]{:S(2)}, u32[]{:S(2)}) collective-permute-start(bf16[240,384]{1,0:T(8,128)(2,1)S(1)} %get-tuple-element.38), channel_id=1, source_target_pairs={{0,2},{2,0},{4,6},{6,4},{8,10},{10,8},{12,14},{14,12},{16,18},{18,... | collective-permute-start | bytes 552968 | tf_op jit(solution)/shard_map/ppermute | solution.py:482
  29.9 7.5 %collective-permute-start.1 = (bf16[240,384]{1,0:T(8,128)(2,1)S(1)}, bf16[240,384]{1,0:T(8,128)(2,1)S(1)}, u32[]{:S(2)}, u32[]{:S(2)}) collective-permute-start(bf16[240,384]{1,0:T(8,128)(2,1)S(1)} %get-tuple-element.39), channel_id=1, source_target_pairs={{0,4},{2,6},{4,0},{6,2},{8,12},{10,14},{12,8},{14,10},{16,20},{18,... | collective-permute-start | bytes 552968 | tf_op jit(solution)/shard_map/ppermute | solution.py:482
  31.4 10.4 %collective-permute-start.2 = (bf16[240,384]{1,0:T(8,128)(2,1)S(1)}, bf16[240,384]{1,0:T(8,128)(2,1)S(1)}, u32[]{:S(2)}, u32[]{:S(2)}) collective-permute-start(bf16[240,384]{1,0:T(8,128)(2,1)S(1)} %get-tuple-element.40), channel_id=1, source_target_pairs={{0,6},{2,4},{4,2},{6,0},{8,14},{10,12},{12,10},{14,8},{16,22},{18,... | collective-permute-start | bytes 552968 | tf_op jit(solution)/shard_map/ppermute | solution.py:482
  31.5 21.7 %collective-permute-start.9 = (bf16[320,384]{1,0:T(8,128)(2,1)S(1)}, bf16[320,384]{1,0:T(8,128)(2,1)S(1)}, u32[]{:S(2)}, u32[]{:S(2)}) collective-permute-start(bf16[320,384]{1,0:T(8,128)(2,1)S(1)} %shard_map.112), channel_id=1, source_target_pairs={{0,8},{2,10},{4,12},{6,14},{8,16},{10,18},{12,20},{14,22},{16,24},... | collective-permute-start | bytes 737288 | tf_op jit(solution)/shard_map/ppermute | solution.py:492
  37.4 15.8 %collective-permute-start.10 = (bf16[320,384]{1,0:T(8,128)(2,1)S(1)}, bf16[320,384]{1,0:T(8,128)(2,1)S(1)}, u32[]{:S(2)}, u32[]{:S(2)}) collective-permute-start(bf16[320,384]{1,0:T(8,128)(2,1)S(1)} %shard_map.113), channel_id=1, source_target_pairs={{0,8},{2,10},{4,12},{6,14},{8,16},{10,18},{12,20},{14,22},{16,24},... | collective-permute-start | bytes 737288 | tf_op jit(solution)/shard_map/ppermute | solution.py:492
  45.6 9.5 %collective-permute-start.11 = (bf16[320,384]{1,0:T(8,128)(2,1)S(1)}, bf16[320,384]{1,0:T(8,128)(2,1)S(1)}, u32[]{:S(2)}, u32[]{:S(2)}) collective-permute-start(bf16[320,384]{1,0:T(8,128)(2,1)S(1)} %shard_map.115), channel_id=1, source_target_pairs={{0,8},{2,10},{4,12},{6,14},{8,16},{10,18},{12,20},{14,22},{16,24},... | collective-permute-start | bytes 737288 | tf_op jit(solution)/shard_map/ppermute | solution.py:492
  49.2 47.1 %copy-start.3 = (bf16[1,2048,704]{1,2,0:T(8,128)(2,1)S(1)}, bf16[1,2048,704]{1,2,0:T(8,128)(2,1)}, u32[]{:S(2)}) copy-start(bf16[1,2048,704]{1,2,0:T(8,128)(2,1)} %param.20) | copy-start | bytes 8650756
  53.2 43.1 %copy-start.2 = (bf16[1,2048,704]{1,2,0:T(8,128)(2,1)S(1)}, bf16[1,2048,704]{1,2,0:T(8,128)(2,1)}, u32[]{:S(2)}) copy-start(bf16[1,2048,704]{1,2,0:T(8,128)(2,1)} %param.19) | copy-start | bytes 8650756
  55.1 41.2 %copy-start = (bf16[512,2048]{1,0:T(8,128)(2,1)S(1)}, bf16[512,2048]{1,0:T(8,128)(2,1)}, u32[]{:S(2)}) copy-start(bf16[512,2048]{1,0:T(8,128)(2,1)} %refs_8_.1) | copy-start | bytes 6291460
  55.1 41.2 %copy-start.4 = (f32[2048]{0:T(1024)S(1)}, f32[2048]{0:T(1024)}, u32[]{:S(2)}) copy-start(f32[2048]{0:T(1024)} %param.16) | copy-start | bytes 24580
  56.8 39.5 %collective-permute-start.17 = (bf16[512,1024]{1,0:T(8,128)(2,1)S(1)}, bf16[512,1024]{1,0:T(8,128)(2,1)S(1)}, u32[]{:S(2)}, u32[]{:S(2)}) collective-permute-start(bf16[512,1024]{1,0:T(8,128)(2,1)S(1)} %collective-permute-done.16.refs_6_.refs_9_), channel_id=1, source_target_pairs={{0,2},{2,0},{4,6},{6,4},{8,10},{10,8},{12,14},{14,12},{16,18},{18,... | collective-permute-start | bytes 3145736 | tf_op jit(solution)/shard_map/ppermute | solution.py:482
  56.9 18.5 %collective-permute-start.24 = (bf16[704,512]{1,0:T(8,128)(2,1)S(1)}, bf16[704,512]{1,0:T(8,128)(2,1)S(1)}, u32[]{:S(2)}, u32[]{:S(2)}) collective-permute-start(bf16[704,512]{1,0:T(8,128)(2,1)S(1)} %collective-permute-done.23.refs_0_), channel_id=1, source_target_pairs={{0,4},{2,6},{4,0},{6,2},{8,12},{10,14},{12,8},{14,10},{16,20},{18,... | collective-permute-start | bytes 2162696 | tf_op jit(solution)/shard_map/ppermute | solution.py:482
  75.4 28.6 %collective-permute-start.25 = (bf16[704,512]{1,0:T(8,128)(2,1)S(1)}, bf16[704,512]{1,0:T(8,128)(2,1)S(1)}, u32[]{:S(2)}, u32[]{:S(2)}) collective-permute-start(bf16[704,512]{1,0:T(8,128)(2,1)S(1)} %collective-permute-done.23.refs_0_), channel_id=1, source_target_pairs={{0,2},{2,0},{4,6},{6,4},{8,10},{10,8},{12,14},{14,12},{16,18},{18,... | collective-permute-start | bytes 2162696 | tf_op jit(solution)/shard_map/ppermute | solution.py:482
  75.4 28.6 %collective-permute-start.26 = (bf16[704,512]{1,0:T(8,128)(2,1)S(1)}, bf16[704,512]{1,0:T(8,128)(2,1)S(1)}, u32[]{:S(2)}, u32[]{:S(2)}) collective-permute-start(bf16[704,512]{1,0:T(8,128)(2,1)S(1)} %collective-permute-done.24.refs_2_), channel_id=1, source_target_pairs={{0,2},{2,0},{4,6},{6,4},{8,10},{10,8},{12,14},{14,12},{16,18},{18,... | collective-permute-start | bytes 2162696 | tf_op jit(solution)/shard_map/ppermute | solution.py:482
  75.9 4.1 %collective-permute-start.18 = (bf16[192,128]{1,0:T(8,128)(2,1)S(1)}, bf16[192,128]{1,0:T(8,128)(2,1)S(1)}, u32[]{:S(2)}, u32[]{:S(2)}) collective-permute-start(bf16[192,128]{1,0:T(8,128)(2,1)S(1)} %get-tuple-element.59), channel_id=1, source_target_pairs={{0,1},{1,0},{2,3},{3,2},{4,5},{5,4},{6,7},{7,6},{8,9},{9,8},{10,11... | collective-permute-start | bytes 147464 | tf_op jit(solution)/shard_map/ppermute | solution.py:485
  77.5 8.0 %collective-permute-start.12 = (bf16[384,128]{1,0:T(8,128)(2,1)S(1)}, bf16[384,128]{1,0:T(8,128)(2,1)S(1)}, u32[]{:S(2)}, u32[]{:S(2)}) collective-permute-start(bf16[384,128]{1,0:T(8,128)(2,1)S(1)} %get-tuple-element.52), channel_id=1, source_target_pairs={{0,2},{2,0},{4,6},{6,4},{8,10},{10,8},{12,14},{14,12},{16,18},{18,... | collective-permute-start | bytes 294920 | tf_op jit(solution)/shard_map/ppermute | solution.py:482
  80.0 4.0 %collective-permute-start.19 = (bf16[192,128]{1,0:T(8,128)(2,1)S(1)}, bf16[192,128]{1,0:T(8,128)(2,1)S(1)}, u32[]{:S(2)}, u32[]{:S(2)}) collective-permute-start(bf16[192,128]{1,0:T(8,128)(2,1)S(1)} %get-tuple-element.60), channel_id=1, source_target_pairs={{0,3},{1,2},{2,1},{3,0},{4,7},{5,6},{6,5},{7,4},{8,11},{9,10},{10,... | collective-permute-start | bytes 147464 | tf_op jit(solution)/shard_map/ppermute | solution.py:489
  84.0 5.2 %collective-permute-start.13 = (bf16[384,128]{1,0:T(8,128)(2,1)S(1)}, bf16[384,128]{1,0:T(8,128)(2,1)S(1)}, u32[]{:S(2)}, u32[]{:S(2)}) collective-permute-start(bf16[384,128]{1,0:T(8,128)(2,1)S(1)} %get-tuple-element.53), channel_id=1, source_target_pairs={{0,4},{2,6},{4,0},{6,2},{8,12},{10,14},{12,8},{14,10},{16,20},{18,... | collective-permute-start | bytes 294920 | tf_op jit(solution)/shard_map/ppermute | solution.py:482
  85.5 6.2 %collective-permute-start.14 = (bf16[384,128]{1,0:T(8,128)(2,1)S(1)}, bf16[384,128]{1,0:T(8,128)(2,1)S(1)}, u32[]{:S(2)}, u32[]{:S(2)}) collective-permute-start(bf16[384,128]{1,0:T(8,128)(2,1)S(1)} %get-tuple-element.54), channel_id=1, source_target_pairs={{0,6},{2,4},{4,2},{6,0},{8,14},{10,12},{12,10},{14,8},{16,22},{18,... | collective-permute-start | bytes 294920 | tf_op jit(solution)/shard_map/ppermute | solution.py:482
  89.1 5.0 %collective-permute-start.20 = (bf16[192,128]{1,0:T(8,128)(2,1)S(1)}, bf16[192,128]{1,0:T(8,128)(2,1)S(1)}, u32[]{:S(2)}, u32[]{:S(2)}) collective-permute-start(bf16[192,128]{1,0:T(8,128)(2,1)S(1)} %get-tuple-element.61), channel_id=1, source_target_pairs={{0,5},{1,4},{2,7},{3,6},{4,1},{5,0},{6,3},{7,2},{8,13},{9,12},{10,... | collective-permute-start | bytes 147464 | tf_op jit(solution)/shard_map/ppermute | solution.py:489
  91.6 4.7 %collective-permute-start.21 = (bf16[192,128]{1,0:T(8,128)(2,1)S(1)}, bf16[192,128]{1,0:T(8,128)(2,1)S(1)}, u32[]{:S(2)}, u32[]{:S(2)}) collective-permute-start(bf16[192,128]{1,0:T(8,128)(2,1)S(1)} %get-tuple-element.62), channel_id=1, source_target_pairs={{0,7},{1,6},{2,5},{3,4},{4,3},{5,2},{6,1},{7,0},{8,15},{9,14},{10,... | collective-permute-start | bytes 147464 | tf_op jit(solution)/shard_map/ppermute | solution.py:489
  94.1 6.1 %collective-permute-start.15 = (bf16[768,128]{1,0:T(8,128)(2,1)S(1)}, bf16[768,128]{1,0:T(8,128)(2,1)S(1)}, u32[]{:S(2)}, u32[]{:S(2)}) collective-permute-start(bf16[768,128]{1,0:T(8,128)(2,1)S(1)} %own_tokens.1), channel_id=1, source_target_pairs={{0,1},{1,0},{2,3},{3,2},{4,5},{5,4},{6,7},{7,6},{8,9},{9,8},{10,11... | collective-permute-start | bytes 589832 | tf_op jit(solution)/shard_map/ppermute | solution.py:485
  96.3 3.9 %copy-start.1 = (bf16[1,704,2048]{2,1,0:T(8,128)(2,1)S(1)}, bf16[1,704,2048]{2,1,0:T(8,128)(2,1)}, u32[]{:S(2)}) copy-start(bf16[1,704,2048]{2,1,0:T(8,128)(2,1)} %refs_12_.1) | copy-start | bytes 8650756
  96.3 3.9 %copy-start.5 = (s32[192,1]{0,1:T(1,128)S(1)}, s32[192,1]{0,1:T(1,128)}, u32[]{:S(2)}) copy-start(s32[192,1]{0,1:T(1,128)} %param.17) | copy-start | bytes 2308
  99.4 8.1 %collective-permute-start.22 = (bf16[1056,128]{1,0:T(8,128)(2,1)S(1)}, bf16[1056,128]{1,0:T(8,128)(2,1)S(1)}, u32[]{:S(2)}, u32[]{:S(2)}) collective-permute-start(bf16[1056,128]{1,0:T(8,128)(2,1)S(1)} %hidden_peer.1), channel_id=1, source_target_pairs={{0,1},{1,0},{2,3},{3,2},{4,5},{5,4},{6,7},{7,6},{8,9},{9,8},{10,11... | collective-permute-start | bytes 811016 | tf_op jit(solution)/shard_map/ppermute | solution.py:485
  100.2 7.3 %copy-start.6 = (f32[192,1]{0,1:T(1,128)S(1)}, f32[192,1]{0,1:T(1,128)}, u32[]{:S(2)}) copy-start(f32[192,1]{0,1:T(1,128)} %param.18) | copy-start | bytes 2308
where the time goes:
time: 110 us; the launch traced here: 109 us
  waiting for transfers between devices  46.3 us (42%)
  starting transfers between devices  39.4 us (36%)
  Pallas kernels  23.3 us (21%)
    ppermute x6, starting transfers between devices, forward(): lax.ppermute(array, 'seq', [(i, i + group) for i in range(peers - group)])  23.1 us
    ppermute x13, waiting for transfers between devices, swap(): return lax.ppermute(array, 'seq', [(i, i ^ d) for i in range(peers)])  22.5 us
    pallas_call x4, Pallas kernels, attend(): pl.pallas_call(functools.partial(attend_kernel, group, tables, phase, fir...  11.1 us
    ppermute x6, waiting for transfers between devices, forward(): lax.ppermute(array, 'seq', [(i, i + group) for i in range(peers - group)])  10.4 us
    ppermute x13, starting transfers between devices, swap(): return lax.ppermute(array, 'seq', [(i, i ^ d) for i in range(peers)])  8.25 us
    ppermute x3, waiting for transfers between devices, swap_across(): return lax.ppermute(array, ('seq', 'exp'), pairs)  7.47 us
    pallas_call x2, Pallas kernels, hidden_part(): pl.pallas_call(functools.partial(hidden_kernel, group, mine, 1e-06), out_...  6.81 us
    ppermute x5, waiting for transfers between devices, across(): return lax.ppermute(array, 'exp', [(0, 1), (1, 0)])  6.04 us
  transfers between devices with their start and end apart: 27, of which 11 were waited for; matrix products, arithmetic and copies ran while one was open for 0% of the time, Pallas kernels for 18%

commit v1 on v0

--- a/solution.py
+++ b/solution.py
@@ -17,6 +17,7 @@
 F32 = jnp.float32
 BF16 = jnp.bfloat16
 MIB = 1 << 20
+EXTRA = 16
 
 
 def ceil_to(value, step):
@@ -88,7 +89,7 @@
     )(in_hbm(k), in_hbm(v))
 
 
-def pack_q_kernel(group, phases, layout_hbm, q_ref, w_ref, down_ref, after_ref, *refs):
+def pack_q_kernel(group, phases, layout_hbm, q_ref, w_ref, down_ref, after_ref, ids_ref, *refs):
     outs, (w_out, down_out), (layout_ref, q_buf, qt, sem) = refs[:group], refs[group : group + 2], refs[group + 2 :]
     seq = lax.axis_index("seq")
     own, plane = seq % group, seq // group
@@ -106,7 +107,9 @@
         down_ref.at[0, :, pl.ds(pl.multiple_of(own * quarter, 128), quarter)], down_out, sem.at[blocks + 1]
     )
     w_load = pltpu.make_async_copy(
-        w_ref.at[:, pl.ds(pl.multiple_of((seq % 2) * width, 128), width)], w_out, sem.at[blocks + 2]
+        w_ref.at[:, pl.ds(pl.multiple_of((seq % 2) * width, 128), width)],
+        w_out.at[: w_ref.shape[0], :],
+        sem.at[blocks + 2],
     )
     for copy in [layout_load] + loads + [down_load, w_load]:
         copy.start()
@@ -115,6 +118,8 @@
     for p in range(1, phases):
         phase = phase + (row >= p * plane_blocks).astype(jnp.int32)
     exists = (phase <= plane) & (row < phases * plane_blocks)
+    ids = jnp.broadcast_to(ids_ref[...].astype(F32), (EXTRA, ids_ref.shape[1]))
+    w_out[w_ref.shape[0] :, : ids_ref.shape[1]] = ids.astype(BF16)
     layout_load.wait()
     for t in range(tokens // BLK):
         rows = slice(t * BLK, (t + 1) * BLK)
@@ -133,15 +138,15 @@
     w_load.wait()
 
 
-def pack_q(q, layout, w, down, earlier, group, phases):
+def pack_q(q, layout, w, down, earlier, ids, group, phases):
     tokens = q.shape[0]
     aug = ceil_to(phases * group * layout.shape[0], 16)
-    w_part = pltpu.VMEM((w.shape[0], w.shape[1] // 2), BF16)
+    w_part = pltpu.VMEM((w.shape[0] + EXTRA, w.shape[1] // 2), BF16)
     down_part = pltpu.VMEM((down.shape[1], down.shape[2] // group), BF16)
     return pl.pallas_call(
         functools.partial(pack_q_kernel, group, phases),
         out_shape=[pltpu.VMEM((QK + aug, tokens), BF16)] * group + [w_part, down_part],
-        in_specs=[anywhere()] * 5,
+        in_specs=[anywhere()] * 5 + [vmem()],
         out_specs=[vmem()] * (group + 2),
         scratch_shapes=[
             pltpu.SMEM(layout.shape, jnp.int32),
@@ -152,7 +157,7 @@
         compiler_params=params(8),
         cost_estimate=pl.CostEstimate(flops=1 << 20, transcendentals=0, bytes_accessed=1 << 20),
         name="pack_q",
-    )(in_hbm(layout), in_hbm(q), in_hbm(w), in_hbm(down), earlier)
+    )(in_hbm(layout), in_hbm(q), in_hbm(w), in_hbm(down), earlier, ids)
 
 
 def select_index(values, own):
@@ -346,18 +351,37 @@
     )(*pieces)
 
 
+def capacity_of(rows):
+    return 3 * rows // 4
+
+
+def slots_of(member, capacity):
+    tokens = member.shape[1]
+    before = lax.broadcasted_iota(jnp.int32, (tokens, tokens), 0) <= lax.broadcasted_iota(
+        jnp.int32, (tokens, tokens), 1
+    )
+    counted = jnp.dot(
+        jnp.broadcast_to(member, (16, tokens)).astype(BF16), before.astype(F32).astype(BF16), preferred_element_type=F32
+    )[:1]
+    slot = lax.broadcasted_iota(jnp.int32, (capacity, tokens), 0).astype(F32) + F32(1.0)
+    return jnp.where((slot == counted) & (member > F32(0.5)), F32(1.0), F32(0.0))
+
+
 def pack_columns(ref, value):
-    ref[: value.shape[0], :] = value[:, :128]
-    rest = value[:, 128:]
-    half = value.shape[0] // 2
-    ref[value.shape[0] :, :] = jnp.concatenate([rest[:half], rest[half:]], axis=1)
-
-
-def unpack_columns(ref, rows):
-    rest = ref[rows:, :]
-    return jnp.concatenate(
-        [ref[:rows, :], jnp.concatenate([rest[:, :64], rest[:, 64:]], axis=0)], axis=1
-    )
+    rows, width = value.shape
+    full = width // 128
+    for c in range(full):
+        ref[c * rows : (c + 1) * rows, :] = value[:, c * 128 : (c + 1) * 128].astype(BF16)
+    rest = value[:, full * 128 :]
+    half = rows // 2
+    ref[full * rows :, :] = jnp.concatenate([rest[:half], rest[half:]], axis=1).astype(BF16)
+
+
+def unpack_columns(ref, rows, width):
+    full = width // 128
+    rest = ref[full * rows :, :].astype(F32)
+    rest = jnp.concatenate([rest[:, :64], rest[:, 64:]], axis=0).astype(BF16)
+    return jnp.concatenate([ref[c * rows : (c + 1) * rows, :] for c in range(full)] + [rest], axis=1)
 
 
 def hidden_kernel(group, mine, eps, *refs):
@@ -365,7 +389,7 @@
     w_own, w_same, w_swap, gain, gate_w, up_w = refs[:6]
     refs = refs[6:]
     if mine:
-        ids, down_own, attended_ref, partial_ref, ctx, att = refs
+        ids, down_own, attended_ref, partial_ref, place_ref, ctx, att = refs
     else:
         hidden_ref, ctx, att = refs
     seq, part = lax.axis_index("seq"), lax.axis_index("exp")
@@ -386,7 +410,7 @@
     for at, ref in ((side, w_same), (1 - side, w_swap)):
         cols = pl.ds(pl.multiple_of(at * width, 128), width)
         att[:, cols] = jnp.dot(ctx[:, :half], w_own[:, cols], preferred_element_type=F32) + jnp.dot(
-            ctx[:, half:], ref[...], preferred_element_type=F32
+            ctx[:, half:], ref[:half, :], preferred_element_type=F32
         )
     attended = att[...]
     rescale = lax.rsqrt(jnp.mean(attended * attended, axis=1, keepdims=True) + F32(eps))
@@ -399,8 +423,14 @@
         attended_ref[...] = attended
         routed = jnp.where(ids[...] == part, hidden.astype(F32), jnp.zeros(hidden.shape, F32)).astype(BF16)
         partial_ref[...] = jnp.dot(routed.T, down_own[0], preferred_element_type=F32)
+        away = jnp.where(ids[...] == part, F32(0.0), F32(1.0))
+        place_ref[...] = slots_of(away, place_ref.shape[1]).T.astype(BF16)
     else:
-        pack_columns(hidden_ref, hidden)
+        arriving = w_same[half : half + 1, :rows_here].astype(F32)
+        member = jnp.where(arriving == part.astype(F32), F32(1.0), F32(0.0))
+        place = slots_of(member, capacity_of(rows_here)).astype(BF16)
+        chosen = lax.dot_general(place, hidden, across, preferred_element_type=F32)
+        pack_columns(hidden_ref, chosen)
 
 
 def hidden_part(group, pieces, w_own, w_same, w_swap, gain, gate_w, up_w, *extra):
@@ -410,9 +440,9 @@
     inner = gate_w.shape[1]
     inputs = list(pieces) + [w_own, w_same, w_swap, gain, gate_w, up_w] + list(extra)
     if mine:
-        outs = [pltpu.VMEM((rows, width), F32)] * 2
+        outs = [pltpu.VMEM((rows, width), F32)] * 2 + [pltpu.VMEM((rows, capacity_of(rows)), BF16)]
     else:
-        outs = [pltpu.VMEM((inner * rows // 128, 128), BF16)]
+        outs = [pltpu.VMEM((inner * capacity_of(rows) // 128, 128), BF16)]
     return pl.pallas_call(
         functools.partial(hidden_kernel, group, mine, 1e-06),
         out_shape=outs,
@@ -427,28 +457,34 @@
     )(*inputs)
 
 
-def combine_kernel(group, attended, partial, hid_peer, ids, weight, *refs):
-    down, out_ref = refs[:group], refs[group]
+def combine_kernel(group, attended, partial, place, hid_peer, weight, *refs):
+    down, out_ref, (result_ref, sem) = refs[:group], refs[group], refs[group + 1 :]
     own = lax.axis_index("seq") % group
-    here = ids[...] == lax.axis_index("exp")
-    hidden = unpack_columns(hid_peer, down[0].shape[0]).astype(F32)
-    other = jnp.where(here, jnp.zeros(hidden.shape, F32), hidden).astype(BF16).T
+    hidden = unpack_columns(hid_peer, place.shape[1], down[0].shape[0])
+    other = jnp.dot(place[...], hidden, preferred_element_type=F32).astype(BF16)
     column = jnp.broadcast_to(weight[...], (128, weight.shape[1])).T[:, :1]
     width = out_ref.shape[1] // group
+    copies = []
     for d in range(group):
         cols = pl.ds(pl.multiple_of((own ^ d) * width, 128), width)
         result = partial[:, cols] + jnp.dot(other, down[d][...], preferred_element_type=F32)
         result = result.astype(BF16).astype(F32)
-        out_ref[:, cols] = (attended[:, cols] + column * result).astype(BF16)
-
-
-def combine(group, attended, partial, hid_peer, ids, weight, down):
-    inputs = [attended, partial, hid_peer, ids, weight] + list(down)
+        here = slice(d * width, (d + 1) * width)
+        result_ref[:, here] = (attended[:, cols] + column * result).astype(BF16)
+        copies.append(pltpu.make_async_copy(result_ref.at[:, here], out_ref.at[:, cols], sem.at[d]))
+        copies[-1].start()
+    for copy in copies:
+        copy.wait()
+
+
+def combine(group, attended, partial, place, hid_peer, weight, down):
+    inputs = [attended, partial, place, hid_peer, weight] + list(down)
     return pl.pallas_call(
         functools.partial(combine_kernel, group),
         out_shape=jax.ShapeDtypeStruct(attended.shape, BF16),
         in_specs=[vmem()] * len(inputs),
-        out_specs=vmem(),
+        out_specs=anywhere(),
+        scratch_shapes=[pltpu.VMEM(attended.shape, BF16), pltpu.SemaphoreType.DMA((group,))],
         compiler_params=params(20),
         cost_estimate=pl.CostEstimate(flops=1 << 20, transcendentals=0, bytes_accessed=1 << 20),
         name="combine",
@@ -498,10 +534,11 @@
             if (shard + 1) * blocks - 1 >= plane_blocks * hop - (SPAN - 1)
         ]
 
+    ids = expert_ids.reshape(1, -1)
     kv = pack_kv(key_heads, value_heads, group)
     held = [kv[0]] + [swap(kv[d], d) for d in range(1, group)]
     *qs, w_part, down_part = pack_q(
-        queries, block_layout, out_weight, down_weight, kv[0], group, phases
+        queries, block_layout, out_weight, down_weight, kv[0], ids, group, phases
     )
     qs = [qs[0]] + [swap(qs[d], d) for d in range(1, group)]
     down0 = across(down_part)
@@ -546,9 +583,6 @@
             peak, acc = attend(
                 group, tables[:-1], hop, parts[:-1], state=state, shards_seen=seen(tables[:-1])
             )
-            down0, down2 = after((down0, down2), peak)
-            down1 = swap(down0, 1)
-            down3 = swap(down2, 1)
             context = attend(
                 group,
                 tables[-1:],
@@ -566,12 +600,14 @@
     mine = [across(own_tokens(same))]
     gain = norm_gain.reshape(1, -1)
     weights = (out_weight, w_same, w_swap, gain, gate_weight.swapaxes(1, 2), up_weight.swapaxes(1, 2))
-    ids = expert_ids.reshape(1, -1)
     (hid_out,) = hidden_part(group, same + other, *weights)
     hid_peer = across(hid_out)
-    attended, partial = hidden_part(group, same + mine, *weights, ids, down_weight)
+    down0, down2 = after((down0, down2), hid_out)
+    down1 = swap(down0, 1)
+    down3 = swap(down2, 1)
+    attended, partial, place = hidden_part(group, same + mine, *weights, ids, down_weight)
     return combine(
-        group, attended, partial, hid_peer, ids, route_weight.reshape(1, -1), (down0, down1, down2, down3)
+        group, attended, partial, place, hid_peer, route_weight.reshape(1, -1), (down0, down1, down2, down3)
     )
 
 

time: 110 us -> 108 us (0.982)
  waiting for transfers between devices: 46.3 us -> 44.5 us
    ppermute x13, waiting for transfers between devices: 22.5 us -> 6.89 us  [swap(): return lax.ppermute(array, 'seq', [(i, i ^ d) for i in range(peers)])]
    ppermute x3, waiting for transfers between devices: 7.47 us -> 14.4 us  [swap_across(): return lax.ppermute(array, ('seq', 'exp'), pairs)]
    ppermute x5, waiting for transfers between devices: 6.04 us -> 12.9 us  [across(): return lax.ppermute(array, 'exp', [(0, 1), (1, 0)])]
  transfers between devices with their start and end apart: 27 -> 27, of which waited for: 11 -> 11; matrix products, arithmetic and copies ran while one was open for 0% -> 0% of each run, Pallas kernels for 18% -> 19%
where the time goes in v1:
time: 108 us
  waiting for transfers between devices  44.5 us (41%)
  starting transfers between devices  39.7 us (37%)
  Pallas kernels  23.4 us (22%)
    ppermute x6, starting transfers between devices, forward(): lax.ppermute(array, 'seq', [(i, i + group) for i in range(peers - group)])  23.1 us
    ppermute x3, waiting for transfers between devices, swap_across(): return lax.ppermute(array, ('seq', 'exp'), pairs)  14.4 us
    ppermute x5, waiting for transfers between devices, across(): return lax.ppermute(array, 'exp', [(0, 1), (1, 0)])  12.9 us
    pallas_call x4, Pallas kernels, attend(): pl.pallas_call(functools.partial(attend_kernel, group, tables, phase, fir...  11.1 us
    ppermute x6, waiting for transfers between devices, forward(): lax.ppermute(array, 'seq', [(i, i + group) for i in range(peers - group)])  10.4 us
    ppermute x13, starting transfers between devices, swap(): return lax.ppermute(array, 'seq', [(i, i ^ d) for i in range(peers)])  8.96 us
    pallas_call x2, Pallas kernels, hidden_part(): pl.pallas_call(functools.partial(hidden_kernel, group, mine, 1e-06), out_...  7.15 us
    ppermute x13, waiting for transfers between devices, swap(): return lax.ppermute(array, 'seq', [(i, i ^ d) for i in range(peers)])  6.89 us
  transfers between devices with their start and end apart: 27, of which 11 were waited for; matrix products, arithmetic and copies ran while one was open for 0% of the time, Pallas kernels for 19%

profile of v1, /device:TPU:0, one launch (start us, length us, event | category | flops | bytes accessed | tf_op | source)
XLA Modules:
  0.0 108.2 jit_solution(16258896562120119575)
XLA Ops:
  0.0 1.5 %pack_kv.1 = (bf16[320,384]{1,0:T(8,128)(2,1)S(1)}, bf16[320,384]{1,0:T(8,128)(2,1)S(1)}, bf16[320,384]{1,0:T(8,128)(2,1)S(1)}, bf16[320,384]{1,0:T(8,128)(2,1)S(1)}) custom-call(bf16[384,768]{1,0:T(8,128)(2,1)} %k_ref.1, bf16[384,512]{1,0:T(8,128)(2,1)} %v_ref.1), custom_call_target="tpu_custom_call" | custom-call | flops 1048576 | bytes 1048576 | tf_op jit(solution)/shard_map/pack_kv/pallas_call | solution.py:76
  1.5 0.6 collective-permute-start.3
  2.0 2.6 %collective-permute-start.4 = (bf16[320,384]{1,0:T(8,128)(2,1)S(1)}, bf16[320,384]{1,0:T(8,128)(2,1)S(1)}, u32[]{:S(2)}, u32[]{:S(2)}) collective-permute-start(bf16[320,384]{1,0:T(8,128)(2,1)S(1)} %get-tuple-element.43), channel_id=1, source_target_pairs={{0,4},{2,6},{4,0},{6,2},{8,12},{10,14},{12,8},{14,10},{16,20},{18,... | collective-permute-start | bytes 737288 | tf_op jit(solution)/shard_map/ppermute | solution.py:518
  4.6 0.0 collective-permute-start.5
  4.6 0.0 collective-permute-done.3.refs_5_.refs_1_
  4.6 0.1 shard_map.110
  4.7 3.8 %collective-permute-start.6 = (bf16[640,384]{1,0:T(8,128)(2,1)S(1)}, bf16[640,384]{1,0:T(8,128)(2,1)S(1)}, u32[]{:S(2)}, u32[]{:S(2)}) collective-permute-start(bf16[640,384]{1,0:T(8,128)(2,1)S(1)} %shard_map.110), channel_id=1, source_target_pairs={{0,8},{2,10},{4,12},{6,14},{8,16},{10,18},{12,20},{14,22},{16,24},... | collective-permute-start | bytes 1474568 | tf_op jit(solution)/shard_map/ppermute | solution.py:528
  8.5 1.8 %pack_q.1 = (bf16[240,384]{1,0:T(8,128)(2,1)S(1)}, bf16[240,384]{1,0:T(8,128)(2,1)S(1)}, bf16[240,384]{1,0:T(8,128)(2,1)S(1)}, bf16[240,384]{1,0:T(8,128)(2,1)S(...) custom-call(s32[3,16]{1,0:T(4,128)} %layout_hbm.1, bf16[384,768]{1,0:T(8,128)(2,1)} %q_ref.1, ...), custom_call_target="tpu_custom_call" | custom-call | flops 1048576 | bytes 1048576 | tf_op jit(solution)/shard_map/pack_q/pallas_call | solution.py:146
  10.3 1.6 %collective-permute-start.16 = (bf16[528,1024]{1,0:T(8,128)(2,1)S(1)}, bf16[528,1024]{1,0:T(8,128)(2,1)S(1)}, u32[]{:S(2)}, u32[]{:S(2)}) collective-permute-start(bf16[528,1024]{1,0:T(8,128)(2,1)S(1)} %get-tuple-element.56), channel_id=1, source_target_pairs={{0,1},{1,0},{2,3},{3,2},{4,5},{5,4},{6,7},{7,6},{8,9},{9,8},{10,11... | collective-permute-start | bytes 3244040 | tf_op jit(solution)/shard_map/ppermute | solution.py:521
  11.9 0.5 collective-permute-start.23
  12.4 0.0 collective-permute-done.4.refs_6_
  12.4 3.5 %collective-permute-start.7 = (bf16[320,384]{1,0:T(8,128)(2,1)S(1)}, bf16[320,384]{1,0:T(8,128)(2,1)S(1)}, u32[]{:S(2)}, u32[]{:S(2)}) collective-permute-start(bf16[320,384]{1,0:T(8,128)(2,1)S(1)} %collective-permute-done.4.refs_6_), channel_id=1, source_target_pairs={{0,8},{2,10},{4,12},{6,14},{8,16},{10,18},{12,20},{14,22},{16,24},... | collective-permute-start | bytes 737288 | tf_op jit(solution)/shard_map/ppermute | solution.py:528
  15.8 0.3 collective-permute-done.5.refs_7_
  16.1 3.5 %collective-permute-start.8 = (bf16[320,384]{1,0:T(8,128)(2,1)S(1)}, bf16[320,384]{1,0:T(8,128)(2,1)S(1)}, u32[]{:S(2)}, u32[]{:S(2)}) collective-permute-start(bf16[320,384]{1,0:T(8,128)(2,1)S(1)} %collective-permute-done.5.refs_7_), channel_id=1, source_target_pairs={{0,8},{2,10},{4,12},{6,14},{8,16},{10,18},{12,20},{14,22},{16,24},... | collective-permute-start | bytes 737288 | tf_op jit(solution)/shard_map/ppermute | solution.py:528
  19.6 5.7 %collective-permute-done.7.refs_4_.refs_1_ = bf16[320,384]{1,0:T(8,128)(2,1)S(1)} collective-permute-done((bf16[320,384]{1,0:T(8,128)(2,1)S(1)}, bf16[320,384]{1,0:T(8,128)(2,1)S(1)}, u32[]{:S(2)}, u32[]{:S(2)}) %collective-permute-start.7) | collective-permute-done | bytes 245792 | tf_op jit(solution)/shard_map/ppermute | solution.py:528
  25.3 0.0 collective-permute-start
  25.3 4.6 %collective-permute-done.8.refs_5_.refs_2_ = bf16[320,384]{1,0:T(8,128)(2,1)S(1)} collective-permute-done((bf16[320,384]{1,0:T(8,128)(2,1)S(1)}, bf16[320,384]{1,0:T(8,128)(2,1)S(1)}, u32[]{:S(2)}, u32[]{:S(2)}) %collective-permute-start.8) | collective-permute-done | bytes 245792 | tf_op jit(solution)/shard_map/ppermute | solution.py:528
  29.9 1.5 %collective-permute-start.1 = (bf16[240,384]{1,0:T(8,128)(2,1)S(1)}, bf16[240,384]{1,0:T(8,128)(2,1)S(1)}, u32[]{:S(2)}, u32[]{:S(2)}) collective-permute-start(bf16[240,384]{1,0:T(8,128)(2,1)S(1)} %get-tuple-element.40), channel_id=1, source_target_pairs={{0,4},{2,6},{4,0},{6,2},{8,12},{10,14},{12,8},{14,10},{16,20},{18,... | collective-permute-start | bytes 552968 | tf_op jit(solution)/shard_map/ppermute | solution.py:518
  31.5 0.1 shard_map.113
  31.5 4.4 %collective-permute-start.9 = (bf16[320,384]{1,0:T(8,128)(2,1)S(1)}, bf16[320,384]{1,0:T(8,128)(2,1)S(1)}, u32[]{:S(2)}, u32[]{:S(2)}) collective-permute-start(bf16[320,384]{1,0:T(8,128)(2,1)S(1)} %shard_map.112), channel_id=1, source_target_pairs={{0,8},{2,10},{4,12},{6,14},{8,16},{10,18},{12,20},{14,22},{16,24},... | collective-permute-start | bytes 737288 | tf_op jit(solution)/shard_map/ppermute | solution.py:528
  36.0 1.5 %collective-permute-done.1.refs_2_ = bf16[240,384]{1,0:T(8,128)(2,1)S(1)} collective-permute-done((bf16[240,384]{1,0:T(8,128)(2,1)S(1)}, bf16[240,384]{1,0:T(8,128)(2,1)S(1)}, u32[]{:S(2)}, u32[]{:S(2)}) %collective-permute-start.1) | collective-permute-done | bytes 184352 | tf_op jit(solution)/shard_map/ppermute | solution.py:518
  37.5 4.4 %collective-permute-start.10 = (bf16[320,384]{1,0:T(8,128)(2,1)S(1)}, bf16[320,384]{1,0:T(8,128)(2,1)S(1)}, u32[]{:S(2)}, u32[]{:S(2)}) collective-permute-start(bf16[320,384]{1,0:T(8,128)(2,1)S(1)} %shard_map.113), channel_id=1, source_target_pairs={{0,8},{2,10},{4,12},{6,14},{8,16},{10,18},{12,20},{14,22},{16,24},... | collective-permute-start | bytes 737288 | tf_op jit(solution)/shard_map/ppermute | solution.py:528
  41.8 0.0 collective-permute-done.2.refs_3_
  41.9 3.7 %shard_map.109 = (bf16[1536,256]{1,0:T(8,128)(2,1)S(1)}, f32[1536,128]{1,0:T(8,128)S(1)}, f32[1536,256]{1,0:T(8,128)S(1)}) custom-call(bf16[240,384]{1,0:T(8,128)(2,1)S(1)} %get-tuple-element.38.refs_0_, bf16[240,384]{1,0:T(8,128)(2,1)S(1)} %collective-permute-done.refs_1_, bf16[240,384]{1,0:T(8,128)(2,1)S(1)} %collective-permute-done.1.refs_2_, ...), custom_call_target="tpu_custom_call" | custom-call | flops 2415919104 | bytes 1048576 | tf_op jit(solution)/shard_map/pallas_call | solution.py:293
  45.5 6.1 %collective-permute-done.23.refs_0_ = bf16[704,512]{1,0:T(8,128)(2,1)S(1)} collective-permute-done((bf16[704,512]{1,0:T(8,128)(2,1)S(1)}, bf16[704,512]{1,0:T(8,128)(2,1)S(1)}, u32[]{:S(2)}, u32[]{:S(2)}) %collective-permute-start.23) | collective-permute-done | bytes 720928 | tf_op jit(solution)/shard_map/ppermute | solution.py:521
  51.7 3.6 %collective-permute-start.11 = (bf16[320,384]{1,0:T(8,128)(2,1)S(1)}, bf16[320,384]{1,0:T(8,128)(2,1)S(1)}, u32[]{:S(2)}, u32[]{:S(2)}) collective-permute-start(bf16[320,384]{1,0:T(8,128)(2,1)S(1)} %shard_map.115), channel_id=1, source_target_pairs={{0,8},{2,10},{4,12},{6,14},{8,16},{10,18},{12,20},{14,22},{16,24},... | collective-permute-start | bytes 737288 | tf_op jit(solution)/shard_map/ppermute | solution.py:528
  55.3 0.0 copy-start.3
  55.4 3.9 %shard_map.111 = (f32[1536,128]{1,0:T(8,128)S(1)}, f32[1536,256]{1,0:T(8,128)S(1)}) custom-call(bf16[1536,256]{1,0:T(8,128)(2,1)S(1)} %get-tuple-element.45.refs_0_, f32[1536,128]{1,0:T(8,128)S(1)} %get-tuple-element.46.refs_1_, f32[1536,256]{1,0:T(8,128)S(1)} %get-tuple-element.47.refs_2_, ...), custom_call_target="tpu_custom_call", output_to_operand_aliasing={{0}: (1, {}), {1}: (2, {})} | custom-call | flops 2415919104 | bytes 1048576 | tf_op jit(solution)/shard_map/pallas_call | solution.py:293
  59.3 0.0 collective-permute-done.9.refs_3_
  59.3 0.0 collective-permute-done.10.refs_4_
  59.3 0.0 copy-start.2
  59.3 1.8 %shard_map.114 = (f32[1536,128]{1,0:T(8,128)S(1)}, f32[1536,256]{1,0:T(8,128)S(1)}) custom-call(bf16[1536,256]{1,0:T(8,128)(2,1)S(1)} %get-tuple-element.45.refs_0_, f32[1536,128]{1,0:T(8,128)S(1)} %get-tuple-element.48.refs_1_, f32[1536,256]{1,0:T(8,128)S(1)} %get-tuple-element.49.refs_2_, ...), custom_call_target="tpu_custom_call", output_to_operand_aliasing={{0}: (1, {}), {1}: (2, {})} | custom-call | flops 905969664 | bytes 1048576 | tf_op jit(solution)/shard_map/pallas_call | solution.py:293
  61.2 0.0 copy-start
  61.2 0.0 copy-start.4
  61.2 1.7 %shard_map.116 = (bf16[384,128]{1,0:T(8,128)(2,1)S(1)}, bf16[384,128]{1,0:T(8,128)(2,1)S(1)}, bf16[384,128]{1,0:T(8,128)(2,1)S(1)}, bf16[384,128]{1,0:T(8,128)(2...) custom-call(bf16[1536,256]{1,0:T(8,128)(2,1)S(1)} %get-tuple-element, ...), custom_call_target="tpu_custom_call" | custom-call | flops 301989888 | bytes 1048576 | tf_op jit(solution)/shard_map/pallas_call | solution.py:293
  62.9 0.1 collective-permute-start.17
  63.0 1.5 %collective-permute-start.24 = (bf16[704,512]{1,0:T(8,128)(2,1)S(1)}, bf16[704,512]{1,0:T(8,128)(2,1)S(1)}, u32[]{:S(2)}, u32[]{:S(2)}) collective-permute-start(bf16[704,512]{1,0:T(8,128)(2,1)S(1)} %collective-permute-done.23.refs_0_), channel_id=1, source_target_pairs={{0,4},{2,6},{4,0},{6,2},{8,12},{10,14},{12,8},{14,10},{16,20},{18,... | collective-permute-start | bytes 2162696 | tf_op jit(solution)/shard_map/ppermute | solution.py:518
  64.5 1.5 %collective-permute-start.18 = (bf16[192,128]{1,0:T(8,128)(2,1)S(1)}, bf16[192,128]{1,0:T(8,128)(2,1)S(1)}, u32[]{:S(2)}, u32[]{:S(2)}) collective-permute-start(bf16[192,128]{1,0:T(8,128)(2,1)S(1)} %get-tuple-element.61), channel_id=1, source_target_pairs={{0,1},{1,0},{2,3},{3,2},{4,5},{5,4},{6,7},{7,6},{8,9},{9,8},{10,11... | collective-permute-start | bytes 147464 | tf_op jit(solution)/shard_map/ppermute | solution.py:521
  66.0 0.0 collective-permute-start.19
  66.0 1.5 %collective-permute-start.20 = (bf16[192,128]{1,0:T(8,128)(2,1)S(1)}, bf16[192,128]{1,0:T(8,128)(2,1)S(1)}, u32[]{:S(2)}, u32[]{:S(2)}) collective-permute-start(bf16[192,128]{1,0:T(8,128)(2,1)S(1)} %get-tuple-element.63), channel_id=1, source_target_pairs={{0,5},{1,4},{2,7},{3,6},{4,1},{5,0},{6,3},{7,2},{8,13},{9,12},{10,... | collective-permute-start | bytes 147464 | tf_op jit(solution)/shard_map/ppermute | solution.py:525
  67.5 1.1 collective-permute-done.18.refs_4_
  68.6 0.4 collective-permute-start.21
  69.0 1.0 collective-permute-done.19.refs_5_
  70.0 0.7 collective-permute-start.12
  70.7 13.4 %collective-permute-done.20.refs_6_ = bf16[192,128]{1,0:T(8,128)(2,1)S(1)} collective-permute-done((bf16[192,128]{1,0:T(8,128)(2,1)S(1)}, bf16[192,128]{1,0:T(8,128)(2,1)S(1)}, u32[]{:S(2)}, u32[]{:S(2)}) %collective-permute-start.20) | collective-permute-done | bytes 49184 | tf_op jit(solution)/shard_map/ppermute | solution.py:525
  84.1 1.5 %collective-permute-start.13 = (bf16[384,128]{1,0:T(8,128)(2,1)S(1)}, bf16[384,128]{1,0:T(8,128)(2,1)S(1)}, u32[]{:S(2)}, u32[]{:S(2)}) collective-permute-start(bf16[384,128]{1,0:T(8,128)(2,1)S(1)} %get-tuple-element.54), channel_id=1, source_target_pairs={{0,4},{2,6},{4,0},{6,2},{8,12},{10,14},{12,8},{14,10},{16,20},{18,... | collective-permute-start | bytes 294920 | tf_op jit(solution)/shard_map/ppermute | solution.py:518
  85.5 0.0 collective-permute-done.21.refs_7_
  85.5 0.0 collective-permute-start.14
  85.5 0.0 collective-permute-done.12.refs_1_
  85.5 3.3 %collective-permute-done.13.refs_2_ = bf16[384,128]{1,0:T(8,128)(2,1)S(1)} collective-permute-done((bf16[384,128]{1,0:T(8,128)(2,1)S(1)}, bf16[384,128]{1,0:T(8,128)(2,1)S(1)}, u32[]{:S(2)}, u32[]{:S(2)}) %collective-permute-start.13) | collective-permute-done | bytes 98336 | tf_op jit(solution)/shard_map/ppermute | solution.py:518
  88.8 1.8 %collective-permute-done.14.refs_3_ = bf16[384,128]{1,0:T(8,128)(2,1)S(1)} collective-permute-done((bf16[384,128]{1,0:T(8,128)(2,1)S(1)}, bf16[384,128]{1,0:T(8,128)(2,1)S(1)}, u32[]{:S(2)}, u32[]{:S(2)}) %collective-permute-start.14) | collective-permute-done | bytes 98336 | tf_op jit(solution)/shard_map/ppermute | solution.py:518
  90.7 0.0 copy-start.1
  90.7 3.3 %hidden_peer.1 = bf16[792,128]{1,0:T(8,128)(2,1)S(1)} custom-call(bf16[384,128]{1,0:T(8,128)(2,1)S(1)} %get-tuple-element.52.refs_0_, bf16[384,128]{1,0:T(8,128)(2,1)S(1)} %collective-permute-done.12.refs_1_, bf16[384,128]{1,0:T(8,128)(2,1)S(1)} %collective-permute-done.13.refs_2_, bf16[384,128]{1,0:T(8,128)(2,1)S(1)} %collective-permute-done.14.refs_3_, ...), custom_call_target="tpu_custom_call" | custom-call | flops 1912602624 | bytes 1048576 | tf_op jit(solution)/shard_map/hidden_peer/pallas_call | solution.py:446
  93.9 0.0 collective-permute-done.24.refs_2_
  94.0 0.2 collective-permute-start.25
  94.1 0.4 collective-permute-start.26
  94.5 0.0 copy-start.6
  94.6 0.6 collective-permute-start.15
  95.1 1.5 %collective-permute-start.22 = (bf16[792,128]{1,0:T(8,128)(2,1)S(1)}, bf16[792,128]{1,0:T(8,128)(2,1)S(1)}, u32[]{:S(2)}, u32[]{:S(2)}) collective-permute-start(bf16[792,128]{1,0:T(8,128)(2,1)S(1)} %hidden_peer.1), channel_id=1, source_target_pairs={{0,1},{1,0},{2,3},{3,2},{4,5},{5,4},{6,7},{7,6},{8,9},{9,8},{10,11... | collective-permute-start | bytes 608264 | tf_op jit(solution)/shard_map/ppermute | solution.py:521
  96.7 5.7 %collective-permute-done.15.refs_4_ = bf16[768,128]{1,0:T(8,128)(2,1)S(1)} collective-permute-done((bf16[768,128]{1,0:T(8,128)(2,1)S(1)}, bf16[768,128]{1,0:T(8,128)(2,1)S(1)}, u32[]{:S(2)}, u32[]{:S(2)}) %collective-permute-start.15) | collective-permute-done | bytes 196640 | tf_op jit(solution)/shard_map/ppermute | solution.py:521
  102.4 3.9 %hidden_own.1 = (f32[192,2048]{1,0:T(8,128)S(1)}, f32[192,2048]{1,0:T(8,128)S(1)}, bf16[192,144]{1,0:T(8,128)(2,1)S(1)}) custom-call(bf16[384,128]{1,0:T(8,128)(2,1)S(1)} %get-tuple-element.52.refs_0_, bf16[384,128]{1,0:T(8,128)(2,1)S(1)} %collective-permute-done.12.refs_1_, bf16[384,128]{1,0:T(8,128)(2,1)S(1)} %collective-permute-done.13.refs_2_, ...), custom_call_target="tpu_custom_call" | custom-call | flops 1912602624 | bytes 1048576 | tf_op jit(solution)/shard_map/hidden_own/pallas_call | solution.py:446
  106.3 0.0 collective-permute-done.25.refs_1_
  106.3 0.0 collective-permute-done.26.refs_3_
  106.3 1.7 %combine.1 = bf16[192,2048]{1,0:T(8,128)(2,1)} custom-call(f32[192,2048]{1,0:T(8,128)S(1)} %get-tuple-element.58.attended, f32[192,2048]{1,0:T(8,128)S(1)} %get-tuple-element.59.partial, bf16[192,144]{1,0:T(8,128)(2,1)S(1)} %get-tuple-element.60.place, bf16[792,128]{1,0:T(8,128)(2,1)S(1)} %collective-permute-done.22.hid_peer, f32[1,192]{1,0:T(1,128)S(1)} %bitcast.13, ...), custom_call_target="tpu_custom_call" | custom-call | flops 1048576 | bytes 1048576 | tf_op jit(solution)/shard_map/combine/pallas_call | solution.py:482
  (18 shorter events, 0.1 us)
Async XLA Ops:
  0.0 8.5 %copy-start.5 = (s32[192,1]{0,1:T(1,128)S(1)}, s32[192,1]{0,1:T(1,128)}, u32[]{:S(2)}) copy-start(s32[192,1]{0,1:T(1,128)} %param.17) | copy-start | bytes 2308
  1.5 3.2 %collective-permute-start.3 = (bf16[320,384]{1,0:T(8,128)(2,1)S(1)}, bf16[320,384]{1,0:T(8,128)(2,1)S(1)}, u32[]{:S(2)}, u32[]{:S(2)}) collective-permute-start(bf16[320,384]{1,0:T(8,128)(2,1)S(1)} %get-tuple-element.42), channel_id=1, source_target_pairs={{0,2},{2,0},{4,6},{6,4},{8,10},{10,8},{12,14},{14,12},{16,18},{18,... | collective-permute-start | bytes 737288 | tf_op jit(solution)/shard_map/ppermute | solution.py:518
  2.0 10.4 %collective-permute-start.4 = (bf16[320,384]{1,0:T(8,128)(2,1)S(1)}, bf16[320,384]{1,0:T(8,128)(2,1)S(1)}, u32[]{:S(2)}, u32[]{:S(2)}) collective-permute-start(bf16[320,384]{1,0:T(8,128)(2,1)S(1)} %get-tuple-element.43), channel_id=1, source_target_pairs={{0,4},{2,6},{4,0},{6,2},{8,12},{10,14},{12,8},{14,10},{16,20},{18,... | collective-permute-start | bytes 737288 | tf_op jit(solution)/shard_map/ppermute | solution.py:518
  4.6 11.6 %collective-permute-start.5 = (bf16[320,384]{1,0:T(8,128)(2,1)S(1)}, bf16[320,384]{1,0:T(8,128)(2,1)S(1)}, u32[]{:S(2)}, u32[]{:S(2)}) collective-permute-start(bf16[320,384]{1,0:T(8,128)(2,1)S(1)} %get-tuple-element.44), channel_id=1, source_target_pairs={{0,6},{2,4},{4,2},{6,0},{8,14},{10,12},{12,10},{14,8},{16,22},{18,... | collective-permute-start | bytes 737288 | tf_op jit(solution)/shard_map/ppermute | solution.py:518
  4.7 26.7 %collective-permute-start.6 = (bf16[640,384]{1,0:T(8,128)(2,1)S(1)}, bf16[640,384]{1,0:T(8,128)(2,1)S(1)}, u32[]{:S(2)}, u32[]{:S(2)}) collective-permute-start(bf16[640,384]{1,0:T(8,128)(2,1)S(1)} %shard_map.110), channel_id=1, source_target_pairs={{0,8},{2,10},{4,12},{6,14},{8,16},{10,18},{12,20},{14,22},{16,24},... | collective-permute-start | bytes 1474568 | tf_op jit(solution)/shard_map/ppermute | solution.py:528
  10.3 52.6 %collective-permute-start.16 = (bf16[528,1024]{1,0:T(8,128)(2,1)S(1)}, bf16[528,1024]{1,0:T(8,128)(2,1)S(1)}, u32[]{:S(2)}, u32[]{:S(2)}) collective-permute-start(bf16[528,1024]{1,0:T(8,128)(2,1)S(1)} %get-tuple-element.56), channel_id=1, source_target_pairs={{0,1},{1,0},{2,3},{3,2},{4,5},{5,4},{6,7},{7,6},{8,9},{9,8},{10,11... | collective-permute-start | bytes 3244040 | tf_op jit(solution)/shard_map/ppermute | solution.py:521
  11.9 39.8 %collective-permute-start.23 = (bf16[704,512]{1,0:T(8,128)(2,1)S(1)}, bf16[704,512]{1,0:T(8,128)(2,1)S(1)}, u32[]{:S(2)}, u32[]{:S(2)}) collective-permute-start(bf16[704,512]{1,0:T(8,128)(2,1)S(1)} %get-tuple-element.65), channel_id=1, source_target_pairs={{0,1},{1,0},{2,3},{3,2},{4,5},{5,4},{6,7},{7,6},{8,9},{9,8},{10,11... | collective-permute-start | bytes 2162696 | tf_op jit(solution)/shard_map/ppermute | solution.py:521
  12.4 12.9 %collective-permute-start.7 = (bf16[320,384]{1,0:T(8,128)(2,1)S(1)}, bf16[320,384]{1,0:T(8,128)(2,1)S(1)}, u32[]{:S(2)}, u32[]{:S(2)}) collective-permute-start(bf16[320,384]{1,0:T(8,128)(2,1)S(1)} %collective-permute-done.4.refs_6_), channel_id=1, source_target_pairs={{0,8},{2,10},{4,12},{6,14},{8,16},{10,18},{12,20},{14,22},{16,24},... | collective-permute-start | bytes 737288 | tf_op jit(solution)/shard_map/ppermute | solution.py:528
  16.1 13.8 %collective-permute-start.8 = (bf16[320,384]{1,0:T(8,128)(2,1)S(1)}, bf16[320,384]{1,0:T(8,128)(2,1)S(1)}, u32[]{:S(2)}, u32[]{:S(2)}) collective-permute-start(bf16[320,384]{1,0:T(8,128)(2,1)S(1)} %collective-permute-done.5.refs_7_), channel_id=1, source_target_pairs={{0,8},{2,10},{4,12},{6,14},{8,16},{10,18},{12,20},{14,22},{16,24},... | collective-permute-start | bytes 737288 | tf_op jit(solution)/shard_map/ppermute | solution.py:528
  25.3 6.2 %collective-permute-start = (bf16[240,384]{1,0:T(8,128)(2,1)S(1)}, bf16[240,384]{1,0:T(8,128)(2,1)S(1)}, u32[]{:S(2)}, u32[]{:S(2)}) collective-permute-start(bf16[240,384]{1,0:T(8,128)(2,1)S(1)} %get-tuple-element.39), channel_id=1, source_target_pairs={{0,2},{2,0},{4,6},{6,4},{8,10},{10,8},{12,14},{14,12},{16,18},{18,... | collective-permute-start | bytes 552968 | tf_op jit(solution)/shard_map/ppermute | solution.py:518
  29.9 7.5 %collective-permute-start.1 = (bf16[240,384]{1,0:T(8,128)(2,1)S(1)}, bf16[240,384]{1,0:T(8,128)(2,1)S(1)}, u32[]{:S(2)}, u32[]{:S(2)}) collective-permute-start(bf16[240,384]{1,0:T(8,128)(2,1)S(1)} %get-tuple-element.40), channel_id=1, source_target_pairs={{0,4},{2,6},{4,0},{6,2},{8,12},{10,14},{12,8},{14,10},{16,20},{18,... | collective-permute-start | bytes 552968 | tf_op jit(solution)/shard_map/ppermute | solution.py:518
  31.4 10.4 %collective-permute-start.2 = (bf16[240,384]{1,0:T(8,128)(2,1)S(1)}, bf16[240,384]{1,0:T(8,128)(2,1)S(1)}, u32[]{:S(2)}, u32[]{:S(2)}) collective-permute-start(bf16[240,384]{1,0:T(8,128)(2,1)S(1)} %get-tuple-element.41), channel_id=1, source_target_pairs={{0,6},{2,4},{4,2},{6,0},{8,14},{10,12},{12,10},{14,8},{16,22},{18,... | collective-permute-start | bytes 552968 | tf_op jit(solution)/shard_map/ppermute | solution.py:518
  31.5 27.8 %collective-permute-start.9 = (bf16[320,384]{1,0:T(8,128)(2,1)S(1)}, bf16[320,384]{1,0:T(8,128)(2,1)S(1)}, u32[]{:S(2)}, u32[]{:S(2)}) collective-permute-start(bf16[320,384]{1,0:T(8,128)(2,1)S(1)} %shard_map.112), channel_id=1, source_target_pairs={{0,8},{2,10},{4,12},{6,14},{8,16},{10,18},{12,20},{14,22},{16,24},... | collective-permute-start | bytes 737288 | tf_op jit(solution)/shard_map/ppermute | solution.py:528
  37.5 21.9 %collective-permute-start.10 = (bf16[320,384]{1,0:T(8,128)(2,1)S(1)}, bf16[320,384]{1,0:T(8,128)(2,1)S(1)}, u32[]{:S(2)}, u32[]{:S(2)}) collective-permute-start(bf16[320,384]{1,0:T(8,128)(2,1)S(1)} %shard_map.113), channel_id=1, source_target_pairs={{0,8},{2,10},{4,12},{6,14},{8,16},{10,18},{12,20},{14,22},{16,24},... | collective-permute-start | bytes 737288 | tf_op jit(solution)/shard_map/ppermute | solution.py:528
  51.7 9.5 %collective-permute-start.11 = (bf16[320,384]{1,0:T(8,128)(2,1)S(1)}, bf16[320,384]{1,0:T(8,128)(2,1)S(1)}, u32[]{:S(2)}, u32[]{:S(2)}) collective-permute-start(bf16[320,384]{1,0:T(8,128)(2,1)S(1)} %shard_map.115), channel_id=1, source_target_pairs={{0,8},{2,10},{4,12},{6,14},{8,16},{10,18},{12,20},{14,22},{16,24},... | collective-permute-start | bytes 737288 | tf_op jit(solution)/shard_map/ppermute | solution.py:528
  55.3 35.3 %copy-start.3 = (bf16[1,2048,704]{1,2,0:T(8,128)(2,1)S(1)}, bf16[1,2048,704]{1,2,0:T(8,128)(2,1)}, u32[]{:S(2)}) copy-start(bf16[1,2048,704]{1,2,0:T(8,128)(2,1)} %param.20) | copy-start | bytes 8650756
  59.3 31.3 %copy-start.2 = (bf16[1,2048,704]{1,2,0:T(8,128)(2,1)S(1)}, bf16[1,2048,704]{1,2,0:T(8,128)(2,1)}, u32[]{:S(2)}) copy-start(bf16[1,2048,704]{1,2,0:T(8,128)(2,1)} %param.19) | copy-start | bytes 8650756
  61.2 29.5 %copy-start = (bf16[512,2048]{1,0:T(8,128)(2,1)S(1)}, bf16[512,2048]{1,0:T(8,128)(2,1)}, u32[]{:S(2)}) copy-start(bf16[512,2048]{1,0:T(8,128)(2,1)} %refs_8_.1) | copy-start | bytes 6291460
  61.2 29.5 %copy-start.4 = (f32[2048]{0:T(1024)S(1)}, f32[2048]{0:T(1024)}, u32[]{:S(2)}) copy-start(f32[2048]{0:T(1024)} %param.16) | copy-start | bytes 24580
  62.9 27.7 %collective-permute-start.17 = (bf16[528,1024]{1,0:T(8,128)(2,1)S(1)}, bf16[528,1024]{1,0:T(8,128)(2,1)S(1)}, u32[]{:S(2)}, u32[]{:S(2)}) collective-permute-start(bf16[528,1024]{1,0:T(8,128)(2,1)S(1)} %collective-permute-done.16.refs_6_.refs_9_), channel_id=1, source_target_pairs={{0,2},{2,0},{4,6},{6,4},{8,10},{10,8},{12,14},{14,12},{16,18},{18,... | collective-permute-start | bytes 3244040 | tf_op jit(solution)/shard_map/ppermute | solution.py:518
  63.0 31.0 %collective-permute-start.24 = (bf16[704,512]{1,0:T(8,128)(2,1)S(1)}, bf16[704,512]{1,0:T(8,128)(2,1)S(1)}, u32[]{:S(2)}, u32[]{:S(2)}) collective-permute-start(bf16[704,512]{1,0:T(8,128)(2,1)S(1)} %collective-permute-done.23.refs_0_), channel_id=1, source_target_pairs={{0,4},{2,6},{4,0},{6,2},{8,12},{10,14},{12,8},{14,10},{16,20},{18,... | collective-permute-start | bytes 2162696 | tf_op jit(solution)/shard_map/ppermute | solution.py:518
  64.5 4.1 %collective-permute-start.18 = (bf16[192,128]{1,0:T(8,128)(2,1)S(1)}, bf16[192,128]{1,0:T(8,128)(2,1)S(1)}, u32[]{:S(2)}, u32[]{:S(2)}) collective-permute-start(bf16[192,128]{1,0:T(8,128)(2,1)S(1)} %get-tuple-element.61), channel_id=1, source_target_pairs={{0,1},{1,0},{2,3},{3,2},{4,5},{5,4},{6,7},{7,6},{8,9},{9,8},{10,11... | collective-permute-start | bytes 147464 | tf_op jit(solution)/shard_map/ppermute | solution.py:521
  66.0 4.0 %collective-permute-start.19 = (bf16[192,128]{1,0:T(8,128)(2,1)S(1)}, bf16[192,128]{1,0:T(8,128)(2,1)S(1)}, u32[]{:S(2)}, u32[]{:S(2)}) collective-permute-start(bf16[192,128]{1,0:T(8,128)(2,1)S(1)} %get-tuple-element.62), channel_id=1, source_target_pairs={{0,3},{1,2},{2,1},{3,0},{4,7},{5,6},{6,5},{7,4},{8,11},{9,10},{10,... | collective-permute-start | bytes 147464 | tf_op jit(solution)/shard_map/ppermute | solution.py:525
  66.0 18.0 %collective-permute-start.20 = (bf16[192,128]{1,0:T(8,128)(2,1)S(1)}, bf16[192,128]{1,0:T(8,128)(2,1)S(1)}, u32[]{:S(2)}, u32[]{:S(2)}) collective-permute-start(bf16[192,128]{1,0:T(8,128)(2,1)S(1)} %get-tuple-element.63), channel_id=1, source_target_pairs={{0,5},{1,4},{2,7},{3,6},{4,1},{5,0},{6,3},{7,2},{8,13},{9,12},{10,... | collective-permute-start | bytes 147464 | tf_op jit(solution)/shard_map/ppermute | solution.py:525
  68.6 16.9 %collective-permute-start.21 = (bf16[192,128]{1,0:T(8,128)(2,1)S(1)}, bf16[192,128]{1,0:T(8,128)(2,1)S(1)}, u32[]{:S(2)}, u32[]{:S(2)}) collective-permute-start(bf16[192,128]{1,0:T(8,128)(2,1)S(1)} %get-tuple-element.64), channel_id=1, source_target_pairs={{0,7},{1,6},{2,5},{3,4},{4,3},{5,2},{6,1},{7,0},{8,15},{9,14},{10,... | collective-permute-start | bytes 147464 | tf_op jit(solution)/shard_map/ppermute | solution.py:525
  70.0 15.5 %collective-permute-start.12 = (bf16[384,128]{1,0:T(8,128)(2,1)S(1)}, bf16[384,128]{1,0:T(8,128)(2,1)S(1)}, u32[]{:S(2)}, u32[]{:S(2)}) collective-permute-start(bf16[384,128]{1,0:T(8,128)(2,1)S(1)} %get-tuple-element.53), channel_id=1, source_target_pairs={{0,2},{2,0},{4,6},{6,4},{8,10},{10,8},{12,14},{14,12},{16,18},{18,... | collective-permute-start | bytes 294920 | tf_op jit(solution)/shard_map/ppermute | solution.py:518
  84.1 4.8 %collective-permute-start.13 = (bf16[384,128]{1,0:T(8,128)(2,1)S(1)}, bf16[384,128]{1,0:T(8,128)(2,1)S(1)}, u32[]{:S(2)}, u32[]{:S(2)}) collective-permute-start(bf16[384,128]{1,0:T(8,128)(2,1)S(1)} %get-tuple-element.54), channel_id=1, source_target_pairs={{0,4},{2,6},{4,0},{6,2},{8,12},{10,14},{12,8},{14,10},{16,20},{18,... | collective-permute-start | bytes 294920 | tf_op jit(solution)/shard_map/ppermute | solution.py:518
  85.5 5.1 %collective-permute-start.14 = (bf16[384,128]{1,0:T(8,128)(2,1)S(1)}, bf16[384,128]{1,0:T(8,128)(2,1)S(1)}, u32[]{:S(2)}, u32[]{:S(2)}) collective-permute-start(bf16[384,128]{1,0:T(8,128)(2,1)S(1)} %get-tuple-element.55), channel_id=1, source_target_pairs={{0,6},{2,4},{4,2},{6,0},{8,14},{10,12},{12,10},{14,8},{16,22},{18,... | collective-permute-start | bytes 294920 | tf_op jit(solution)/shard_map/ppermute | solution.py:518
  90.7 11.7 %copy-start.1 = (bf16[1,704,2048]{2,1,0:T(8,128)(2,1)S(1)}, bf16[1,704,2048]{2,1,0:T(8,128)(2,1)}, u32[]{:S(2)}) copy-start(bf16[1,704,2048]{2,1,0:T(8,128)(2,1)} %refs_12_.1) | copy-start | bytes 8650756
  94.0 12.3 %collective-permute-start.25 = (bf16[704,512]{1,0:T(8,128)(2,1)S(1)}, bf16[704,512]{1,0:T(8,128)(2,1)S(1)}, u32[]{:S(2)}, u32[]{:S(2)}) collective-permute-start(bf16[704,512]{1,0:T(8,128)(2,1)S(1)} %collective-permute-done.23.refs_0_), channel_id=1, source_target_pairs={{0,2},{2,0},{4,6},{6,4},{8,10},{10,8},{12,14},{14,12},{16,18},{18,... | collective-permute-start | bytes 2162696 | tf_op jit(solution)/shard_map/ppermute | solution.py:518
  94.1 12.2 %collective-permute-start.26 = (bf16[704,512]{1,0:T(8,128)(2,1)S(1)}, bf16[704,512]{1,0:T(8,128)(2,1)S(1)}, u32[]{:S(2)}, u32[]{:S(2)}) collective-permute-start(bf16[704,512]{1,0:T(8,128)(2,1)S(1)} %collective-permute-done.24.refs_2_), channel_id=1, source_target_pairs={{0,2},{2,0},{4,6},{6,4},{8,10},{10,8},{12,14},{14,12},{16,18},{18,... | collective-permute-start | bytes 2162696 | tf_op jit(solution)/shard_map/ppermute | solution.py:518
  94.5 11.8 %copy-start.6 = (f32[192,1]{0,1:T(1,128)S(1)}, f32[192,1]{0,1:T(1,128)}, u32[]{:S(2)}) copy-start(f32[192,1]{0,1:T(1,128)} %param.18) | copy-start | bytes 2308
  94.6 7.8 %collective-permute-start.15 = (bf16[768,128]{1,0:T(8,128)(2,1)S(1)}, bf16[768,128]{1,0:T(8,128)(2,1)S(1)}, u32[]{:S(2)}, u32[]{:S(2)}) collective-permute-start(bf16[768,128]{1,0:T(8,128)(2,1)S(1)} %own_tokens.1), channel_id=1, source_target_pairs={{0,1},{1,0},{2,3},{3,2},{4,5},{5,4},{6,7},{7,6},{8,9},{9,8},{10,11... | collective-permute-start | bytes 589832 | tf_op jit(solution)/shard_map/ppermute | solution.py:521
  95.1 11.1 %collective-permute-start.22 = (bf16[792,128]{1,0:T(8,128)(2,1)S(1)}, bf16[792,128]{1,0:T(8,128)(2,1)S(1)}, u32[]{:S(2)}, u32[]{:S(2)}) collective-permute-start(bf16[792,128]{1,0:T(8,128)(2,1)S(1)} %hidden_peer.1), channel_id=1, source_target_pairs={{0,1},{1,0},{2,3},{3,2},{4,5},{5,4},{6,7},{7,6},{8,9},{9,8},{10,11... | collective-permute-start | bytes 608264 | tf_op jit(solution)/shard_map/ppermute | solution.py:521

commit v2 on v1

--- a/solution.py
+++ b/solution.py
@@ -76,7 +76,7 @@
     return pl.pallas_call(
         functools.partial(pack_kv_kernel, group),
         out_shape=[pltpu.VMEM((QK + VD, tokens), BF16)] * group,
-        in_specs=[anywhere(), anywhere()],
+        in_specs=[anywhere()] * 2,
         out_specs=[vmem()] * group,
         scratch_shapes=[
             pltpu.VMEM(k.shape, BF16),
@@ -89,37 +89,91 @@
     )(in_hbm(k), in_hbm(v))
 
 
-def pack_q_kernel(group, phases, layout_hbm, q_ref, w_ref, down_ref, after_ref, ids_ref, *refs):
-    outs, (w_out, down_out), (layout_ref, q_buf, qt, sem) = refs[:group], refs[group : group + 2], refs[group + 2 :]
+def cut_kernel(group, w_ref, down_ref, ids_ref, after_ref, w_out, down_out, ids_buf, sem):
+    seq = lax.axis_index("seq")
+    own = seq % group
+    width, quarter = w_out.shape[1], down_out.shape[1]
+    ids_load = pltpu.make_async_copy(ids_ref, ids_buf, sem.at[0])
+    copies = [
+        pltpu.make_async_copy(
+            down_ref.at[0, :, pl.ds(pl.multiple_of(own * quarter, 128), quarter)], down_out, sem.at[1]
+        ),
+        pltpu.make_async_copy(
+            w_ref.at[:, pl.ds(pl.multiple_of((seq % 2) * width, 128), width)],
+            w_out.at[: w_ref.shape[0], :],
+            sem.at[2],
+        ),
+    ]
+    for copy in [ids_load] + copies:
+        copy.start()
+    ids_load.wait()
+    ids = jnp.broadcast_to(ids_buf[...].astype(F32), (EXTRA, ids_buf.shape[1]))
+    w_out[w_ref.shape[0] :, : ids_buf.shape[1]] = ids.astype(BF16)
+    for copy in copies:
+        copy.wait()
+
+
+def cut(w, down, ids, earlier, group):
+    return pl.pallas_call(
+        functools.partial(cut_kernel, group),
+        out_shape=[
+            pltpu.VMEM((w.shape[0] + EXTRA, w.shape[1] // 2), BF16),
+            pltpu.VMEM((down.shape[1], down.shape[2] // group), BF16),
+        ],
+        in_specs=[anywhere()] * 4,
+        out_specs=[vmem()] * 2,
+        scratch_shapes=[pltpu.VMEM(ids.shape, jnp.int32), pltpu.SemaphoreType.DMA((3,))],
+        compiler_params=params(8),
+        cost_estimate=pl.CostEstimate(flops=1 << 20, transcendentals=0, bytes_accessed=1 << 20),
+        name="cut",
+    )(in_hbm(w), in_hbm(down), in_hbm(ids), earlier)
+
+
+def stage_kernel(*refs):
+    count = (len(refs) - 2) // 2
+    sem = refs[-1]
+    copies = [
+        pltpu.make_async_copy(refs[at], refs[count + 1 + at], sem.at[at]) for at in range(count)
+    ]
+    for copy in copies:
+        copy.start()
+    for copy in copies:
+        copy.wait()
+
+
+def stage(arrays, earlier):
+    return pl.pallas_call(
+        stage_kernel,
+        out_shape=[pltpu.VMEM(a.shape, a.dtype) for a in arrays],
+        in_specs=[anywhere()] * (len(arrays) + 1),
+        out_specs=[vmem()] * len(arrays),
+        scratch_shapes=[pltpu.SemaphoreType.DMA((len(arrays),))],
+        compiler_params=params(16),
+        cost_estimate=pl.CostEstimate(flops=1 << 20, transcendentals=0, bytes_accessed=1 << 20),
+        name="stage",
+    )(*[in_hbm(a) for a in arrays], earlier)
+
+
+def pack_q_kernel(group, phases, layout_hbm, q_ref, after_ref, *refs):
+    outs, (layout_ref, q_buf, qt, sem) = refs[:group], refs[group:]
     seq = lax.axis_index("seq")
     own, plane = seq % group, seq // group
     tokens = q_ref.shape[0]
     blocks, chosen = layout_ref.shape
     plane_blocks = group * blocks
     aug = outs[0].shape[0] - QK
-    width, quarter = w_out.shape[1], down_out.shape[1]
     loads = []
     for t in range(tokens // BLK):
         rows = slice(t * BLK, (t + 1) * BLK)
         loads.append(pltpu.make_async_copy(q_ref.at[rows, :], q_buf.at[rows, :], sem.at[t]))
     layout_load = pltpu.make_async_copy(layout_hbm, layout_ref, sem.at[blocks])
-    down_load = pltpu.make_async_copy(
-        down_ref.at[0, :, pl.ds(pl.multiple_of(own * quarter, 128), quarter)], down_out, sem.at[blocks + 1]
-    )
-    w_load = pltpu.make_async_copy(
-        w_ref.at[:, pl.ds(pl.multiple_of((seq % 2) * width, 128), width)],
-        w_out.at[: w_ref.shape[0], :],
-        sem.at[blocks + 2],
-    )
-    for copy in [layout_load] + loads + [down_load, w_load]:
+    for copy in [layout_load] + loads:
         copy.start()
     row = lax.broadcasted_iota(jnp.int32, (aug, BLK), 0)
     phase = jnp.zeros_like(row)
     for p in range(1, phases):
         phase = phase + (row >= p * plane_blocks).astype(jnp.int32)
     exists = (phase <= plane) & (row < phases * plane_blocks)
-    ids = jnp.broadcast_to(ids_ref[...].astype(F32), (EXTRA, ids_ref.shape[1]))
-    w_out[w_ref.shape[0] :, : ids_ref.shape[1]] = ids.astype(BF16)
     layout_load.wait()
     for t in range(tokens // BLK):
         rows = slice(t * BLK, (t + 1) * BLK)
@@ -134,30 +188,26 @@
         qt[:, rows] = q_buf[rows, :].T
     for d in range(group):
         outs[d][:QK, :] = qt[pl.ds(pl.multiple_of((own ^ d) * QK, 16), QK), :]
-    down_load.wait()
-    w_load.wait()
-
-
-def pack_q(q, layout, w, down, earlier, ids, group, phases):
+
+
+def pack_q(q, layout, earlier, group, phases):
     tokens = q.shape[0]
     aug = ceil_to(phases * group * layout.shape[0], 16)
-    w_part = pltpu.VMEM((w.shape[0] + EXTRA, w.shape[1] // 2), BF16)
-    down_part = pltpu.VMEM((down.shape[1], down.shape[2] // group), BF16)
     return pl.pallas_call(
         functools.partial(pack_q_kernel, group, phases),
-        out_shape=[pltpu.VMEM((QK + aug, tokens), BF16)] * group + [w_part, down_part],
-        in_specs=[anywhere()] * 5 + [vmem()],
-        out_specs=[vmem()] * (group + 2),
+        out_shape=[pltpu.VMEM((QK + aug, tokens), BF16)] * group,
+        in_specs=[anywhere()] * 3,
+        out_specs=[vmem()] * group,
         scratch_shapes=[
             pltpu.SMEM(layout.shape, jnp.int32),
             pltpu.VMEM(q.shape, BF16),
             pltpu.VMEM((q.shape[1], tokens), BF16),
-            pltpu.SemaphoreType.DMA((layout.shape[0] + 3,)),
+            pltpu.SemaphoreType.DMA((layout.shape[0] + 1,)),
         ],
         compiler_params=params(8),
         cost_estimate=pl.CostEstimate(flops=1 << 20, transcendentals=0, bytes_accessed=1 << 20),
         name="pack_q",
-    )(in_hbm(layout), in_hbm(q), in_hbm(w), in_hbm(down), earlier, ids)
+    )(in_hbm(layout), in_hbm(q), earlier)
 
 
 def select_index(values, own):
@@ -167,7 +217,7 @@
     return picked
 
 
-def attend_kernel(group, tables, phase, first, last, shards_seen, rows_step, *refs):
+def attend_kernel(group, tables, phase, first, last, shards_seen, finish, rows_step, *refs):
     refs = list(refs)
 
     def take(count):
@@ -179,14 +229,18 @@
         q_in = take(group)
     else:
         q_ref, m_in, acc_in = take(3)
+        if last:
+            (ready,) = take(1)
     kv_refs = take(len(tables))
     if first:
         q_ref, m_out, acc_out = take(3)
     elif last:
         outs = take(2 * group)
-        context = refs.pop()
+        (context,) = take(1)
     else:
         m_out, acc_out = take(2)
+        if finish:
+            (context,) = take(1)
     kaug, vaug, s_ref = refs
     own = lax.axis_index("seq") % group
     tokens = kv_refs[0].shape[1]
@@ -216,7 +270,7 @@
                 vaug[part, VD:] = jnp.ones((BLK, VD), BF16)
             at += 1
 
-    def step(rows, slot, diagonal):
+    def step(rows, slot, diagonal, done):
         s_now = s_ref.at[slot]
         s_now[...] = jnp.dot(q_ref[rows, :], kaug[...], preferred_element_type=F32)
         if first:
@@ -234,7 +288,7 @@
         acc = jnp.dot(weights, vaug[...], preferred_element_type=F32)
         if not first:
             acc = acc + acc_in[rows, :] * jnp.exp2((before - peak) * scale)
-        if last:
+        if done:
             context[rows, :] = (acc[:, :VD] / acc[:, VD:]).astype(BF16)
         else:
             m_out[rows, :] = jnp.broadcast_to(peak, (rows_step, m_out.shape[1]))
@@ -246,14 +300,14 @@
         for r in range(per):
             if first:
                 start = shard * tokens + r * rows_step
-                step(slice(start, start + rows_step), count % 2, start)
+                step(slice(start, start + rows_step), count % 2, start, False)
                 count += 1
                 continue
             rows = pl.ds(pl.multiple_of((own ^ shard) * tokens + r * rows_step, rows_step), rows_step)
             if shard in shards_seen:
-                step(rows, count % 2, 0)
+                step(rows, count % 2, 0, shard in finish)
                 count += 1
-            elif last:
+            elif shard in finish:
                 context[rows, :] = (acc_in[rows, :VD] / acc_in[rows, VD:]).astype(BF16)
     if last:
         half = tokens // 2
@@ -264,7 +318,7 @@
             outs[group + d][...] = context[pl.ds(at, half), :]
 
 
-def attend(group, tables, phase, kv, q_in=None, state=None, last=False, shards_seen=(), rows_step=128):
+def attend(group, tables, phase, kv, q_in=None, state=None, last=False, shards_seen=(), finish=(), rows_step=128):
     first = state is None
     tokens = kv[0].shape[1]
     total = group * tokens
@@ -284,14 +338,17 @@
     elif last:
         inputs = list(state)
         outs = [pltpu.VMEM((tokens, VD), BF16)] * group + [pltpu.VMEM((tokens // 2, VD), BF16)] * group
-        scratch = scratch + [pltpu.VMEM((total, VD), BF16)]
+        outs = outs + [pltpu.VMEM((total, VD), BF16)]
+        aliases = {3: 2 * group}
     else:
         inputs = list(state)
         aliases = {1: 0, 2: 1}
+        if finish:
+            outs = outs + [pltpu.VMEM((total, VD), BF16)]
     inputs = inputs + list(kv)
     queries = total if first else len(shards_seen) * tokens
     return pl.pallas_call(
-        functools.partial(attend_kernel, group, tables, phase, first, last, shards_seen, rows_step),
+        functools.partial(attend_kernel, group, tables, phase, first, last, shards_seen, finish, rows_step),
         out_shape=outs,
         in_specs=[vmem()] * len(inputs),
         out_specs=[vmem()] * len(outs),
@@ -330,6 +387,31 @@
     )(*parts)
 
 
+def half_out_kernel(group, *refs):
+    pieces, (w_own, out_ref, ctx) = refs[:group], refs[group:]
+    own = lax.axis_index("seq") % group
+    for d in range(group):
+        ctx[:, pl.ds(pl.multiple_of((own ^ d) * VD, VD), VD)] = pieces[d][...]
+    out_ref[...] = jnp.dot(ctx[...], w_own[...], preferred_element_type=F32)
+
+
+def half_out(pieces, w_own):
+    group = len(pieces)
+    rows, width = pieces[0].shape[0], w_own.shape[1]
+    return pl.pallas_call(
+        functools.partial(half_out_kernel, group),
+        out_shape=pltpu.VMEM((rows, width), F32),
+        in_specs=[vmem()] * (group + 1),
+        out_specs=vmem(),
+        scratch_shapes=[pltpu.VMEM((rows, group * VD), BF16)],
+        compiler_params=params(16),
+        cost_estimate=pl.CostEstimate(
+            flops=2 * rows * width * group * VD, transcendentals=0, bytes_accessed=1 << 20
+        ),
+        name="half_out",
+    )(*pieces, w_own)
+
+
 def own_tokens_kernel(group, *refs):
     pieces, out_ref = refs[:group], refs[group]
     half = pieces[0].shape[0] // 2
@@ -385,9 +467,10 @@
 
 
 def hidden_kernel(group, mine, eps, *refs):
-    pieces, refs = refs[: group + (1 if mine else group)], refs[group + (1 if mine else group) :]
-    w_own, w_same, w_swap, gain, gate_w, up_w = refs[:6]
-    refs = refs[6:]
+    count = 1 if mine else group
+    partial_out, pieces, refs = refs[0], refs[1 : 1 + count], refs[1 + count :]
+    w_same, w_swap, gain, gate_w, up_w = refs[:5]
+    refs = refs[5:]
     if mine:
         ids, down_own, attended_ref, partial_ref, place_ref, ctx, att = refs
     else:
@@ -400,18 +483,12 @@
     rows = pl.ds(pl.multiple_of(which * rows_here, 16), rows_here)
     half = group * VD
     for d in range(group):
-        at = pl.multiple_of((own ^ d) * VD, VD)
-        ctx[:, pl.ds(at, VD)] = pieces[d][rows, :]
-        if mine:
-            ctx[:, pl.ds(half + at, VD)] = pieces[group][d * rows_here : (d + 1) * rows_here, :]
-        else:
-            ctx[:, pl.ds(half + at, VD)] = pieces[group + d][...]
-    width = w_own.shape[1] // 2
+        piece = pieces[0][d * rows_here : (d + 1) * rows_here, :] if mine else pieces[d][...]
+        ctx[:, pl.ds(pl.multiple_of((own ^ d) * VD, VD), VD)] = piece
+    width = att.shape[1] // 2
     for at, ref in ((side, w_same), (1 - side, w_swap)):
         cols = pl.ds(pl.multiple_of(at * width, 128), width)
-        att[:, cols] = jnp.dot(ctx[:, :half], w_own[:, cols], preferred_element_type=F32) + jnp.dot(
-            ctx[:, half:], ref[:half, :], preferred_element_type=F32
-        )
+        att[:, cols] = partial_out[rows, cols] + jnp.dot(ctx[...], ref[:half, :], preferred_element_type=F32)
     attended = att[...]
     rescale = lax.rsqrt(jnp.mean(attended * attended, axis=1, keepdims=True) + F32(eps))
     normed = (attended * rescale * gain[...]).astype(BF16)
@@ -433,12 +510,12 @@
         pack_columns(hidden_ref, chosen)
 
 
-def hidden_part(group, pieces, w_own, w_same, w_swap, gain, gate_w, up_w, *extra):
+def hidden_part(group, partial_out, pieces, w_same, w_swap, gain, gate_w, up_w, *extra):
     mine = bool(extra)
-    rows = pieces[0].shape[0] // 2
-    width = w_own.shape[1]
+    rows = partial_out.shape[0] // 2
+    width = partial_out.shape[1]
     inner = gate_w.shape[1]
-    inputs = list(pieces) + [w_own, w_same, w_swap, gain, gate_w, up_w] + list(extra)
+    inputs = [partial_out] + list(pieces) + [w_same, w_swap, gain, gate_w, up_w] + list(extra)
     if mine:
         outs = [pltpu.VMEM((rows, width), F32)] * 2 + [pltpu.VMEM((rows, capacity_of(rows)), BF16)]
     else:
@@ -448,7 +525,7 @@
         out_shape=outs,
         in_specs=[vmem()] * len(inputs),
         out_specs=[vmem()] * len(outs),
-        scratch_shapes=[pltpu.VMEM((rows, 2 * group * VD), BF16), pltpu.VMEM((rows, width), F32)],
+        scratch_shapes=[pltpu.VMEM((rows, group * VD), BF16), pltpu.VMEM((rows, width), F32)],
         compiler_params=params(24),
         cost_estimate=pl.CostEstimate(
             flops=2 * rows * width * (2 * group * VD + 2 * inner), transcendentals=rows * inner, bytes_accessed=1 << 20
@@ -525,7 +602,7 @@
         return lax.ppermute(array, ("seq", "exp"), pairs)
 
     def forward(array):
-        return lax.ppermute(array, "seq", [(i, i + group) for i in range(peers - group)])
+        return lax.ppermute(array, "seq", [(i, (i + group) % peers) for i in range(peers)])
 
     def needed(hop):
         return [
@@ -536,23 +613,22 @@
 
     ids = expert_ids.reshape(1, -1)
     kv = pack_kv(key_heads, value_heads, group)
+    w_part, down_part = cut(out_weight, down_weight, ids, kv[0], group)
     held = [kv[0]] + [swap(kv[d], d) for d in range(1, group)]
-    *qs, w_part, down_part = pack_q(
-        queries, block_layout, out_weight, down_weight, kv[0], ids, group, phases
-    )
+    qs = pack_q(queries, block_layout, kv[0], group, phases)
     qs = [qs[0]] + [swap(qs[d], d) for d in range(1, group)]
     down0 = across(down_part)
     w_same = across(w_part)
 
     tables = tuple((1, (tuple(g ^ d for g in range(group)),)) for d in range(group))
     early = group // 2
-    joined = gather(group, (tuple(((d, 0),) * group for d in range(early)),), held[:early])[0]
+    gate_now, up_now, out_now, down_now = stage(
+        (gate_weight.swapaxes(1, 2), up_weight.swapaxes(1, 2), out_weight, down_weight), held[-1]
+    )
     q_aug, peak, acc = attend(group, tables, 0, held, q_in=qs)
-    (down0,) = after((down0,), peak)
     down2 = swap(down0, 2)
 
-    tables = ((early, tuple(tables[d][1][0] for d in range(early))),) + tables[early:]
-    parts = [joined] + held[early:]
+    parts = held
     for hop in range(1, phases):
         if hop > 1:
             wanted = needed(hop)
@@ -560,7 +636,7 @@
             chains = []
             for g in range(group):
                 there = sorted((f for f in flat if f[2][g] in wanted), key=lambda f: -f[2][g])
-                head = [f for f in there if f[0] == 0][:1]
+                head = [f for f in there if f[0] < early][:1]
                 chains.append(head + [f for f in there if f not in head])
             plans = [
                 ((tuple((chains[g][k][0], chains[g][k][1]) for g in range(group)),),) for k in range(len(wanted))
@@ -568,7 +644,7 @@
             tables = tuple(
                 (1, (tuple(chains[g][k][2][g] for g in range(group)),)) for k in range(len(wanted))
             )
-            parts = [gather(group, plan, parts[:1] if k == 0 else parts)[0] for k, plan in enumerate(plans)]
+            parts = [gather(group, plan, parts[:early] if k == 0 else parts)[0] for k, plan in enumerate(plans)]
         parts = [forward(part) for part in parts]
 
         def seen(those):
@@ -580,32 +656,41 @@
         if hop < phases - 1:
             peak, acc = attend(group, tables, hop, parts, state=state, shards_seen=seen(tables))
         else:
-            peak, acc = attend(
-                group, tables[:-1], hop, parts[:-1], state=state, shards_seen=seen(tables[:-1])
+            late = seen(tables[-1:])
+            peak, acc, ready = attend(
+                group,
+                tables[:-1],
+                hop,
+                parts[:-1],
+                state=state,
+                shards_seen=seen(tables[:-1]),
+                finish=tuple(shard for shard in range(group) if shard not in late),
             )
             context = attend(
                 group,
                 tables[-1:],
                 hop,
                 parts[-1:],
-                state=(q_aug, peak, acc),
+                state=(q_aug, peak, acc, ready),
                 last=True,
-                shards_seen=seen(tables[-1:]),
+                shards_seen=late,
+                finish=late,
             )
     (w_same,) = after((w_same,), context[0])
     w_swap = swap(w_same, 1)
-    whole, first = context[:group], context[group:]
+    whole, first = context[:group], context[group : 2 * group]
     same = [whole[0]] + [swap(whole[d], d) for d in range(1, group)]
     other = [across(first[0])] + [swap_across(first[d], d) for d in range(1, group)]
     mine = [across(own_tokens(same))]
     gain = norm_gain.reshape(1, -1)
-    weights = (out_weight, w_same, w_swap, gain, gate_weight.swapaxes(1, 2), up_weight.swapaxes(1, 2))
-    (hid_out,) = hidden_part(group, same + other, *weights)
+    partial_out = half_out(same, out_now)
+    weights = (w_same, w_swap, gain, gate_now, up_now)
+    (hid_out,) = hidden_part(group, partial_out, other, *weights)
     hid_peer = across(hid_out)
     down0, down2 = after((down0, down2), hid_out)
     down1 = swap(down0, 1)
     down3 = swap(down2, 1)
-    attended, partial, place = hidden_part(group, same + mine, *weights, ids, down_weight)
+    attended, partial, place = hidden_part(group, partial_out, mine, *weights, ids, down_now)
     return combine(
         group, attended, partial, place, hid_peer, route_weight.reshape(1, -1), (down0, down1, down2, down3)
     )

time: 108 us -> 101 us (0.935)
  starting transfers between devices: 39.7 us -> 29.4 us
  Pallas kernels: 23.4 us -> 28.2 us
  waiting for transfers between devices: 44.5 us -> 42.6 us
    ppermute x6 -> x7, starting transfers between devices: 23.1 us -> 9.95 us  [forward(): lax.ppermute(array, 'seq', [(i, (i + group) % peers) for i in range(peers)])]
    ppermute x3, waiting for transfers between devices: 14.4 us -> 2.36 us  [swap_across(): return lax.ppermute(array, ('seq', 'exp'), pairs)]
    ppermute x6 -> x7, waiting for transfers between devices: 10.4 us -> 19.7 us  [forward(): lax.ppermute(array, 'seq', [(i, (i + group) % peers) for i in range(peers)])]
    pallas_call x0 -> x3, Pallas kernels: none -> 6.7 us  [the longest x1 4.17 us: stage(): pl.pallas_call(stage_kernel, out_shape=[pltpu.VMEM(a.shape, a.dtype) for...]
    ppermute x13, waiting for transfers between devices: 6.89 us -> 12.7 us  [swap(): return lax.ppermute(array, 'seq', [(i, i ^ d) for i in range(peers)])]
    ppermute x5, waiting for transfers between devices: 12.9 us -> 7.78 us  [across(): return lax.ppermute(array, 'exp', [(0, 1), (1, 0)])]
    ppermute x3, starting transfers between devices: 1.91 us -> 5.26 us  [swap_across(): return lax.ppermute(array, ('seq', 'exp'), pairs)]
  transfers between devices with their start and end apart: 27 -> 28, of which waited for: 11 -> 13; matrix products, arithmetic and copies ran while one was open for 0% -> 0% of each run, Pallas kernels for 19% -> 25%
where the time goes in v2:
time: 101 us; the launch traced here: 100 us
  waiting for transfers between devices  42.6 us (42%)
  starting transfers between devices  29.4 us (29%)
  Pallas kernels  28.2 us (28%)
    ppermute x7, waiting for transfers between devices, forward(): lax.ppermute(array, 'seq', [(i, (i + group) % peers) for i in range(peers)])  19.7 us
    ppermute x13, waiting for transfers between devices, swap(): return lax.ppermute(array, 'seq', [(i, i ^ d) for i in range(peers)])  12.7 us
    pallas_call x4, Pallas kernels, attend(): pl.pallas_call(functools.partial(attend_kernel, group, tables, phase, fir...  10.6 us
    ppermute x7, starting transfers between devices, forward(): lax.ppermute(array, 'seq', [(i, (i + group) % peers) for i in range(peers)])  9.95 us
    ppermute x13, starting transfers between devices, swap(): return lax.ppermute(array, 'seq', [(i, i ^ d) for i in range(peers)])  8.45 us
    ppermute x5, waiting for transfers between devices, across(): return lax.ppermute(array, 'exp', [(0, 1), (1, 0)])  7.78 us
    pallas_call x2, Pallas kernels, hidden_part(): pl.pallas_call(functools.partial(hidden_kernel, group, mine, 1e-06), out_...  6.3 us
    ppermute x5, starting transfers between devices, across(): return lax.ppermute(array, 'exp', [(0, 1), (1, 0)])  5.7 us
  transfers between devices with their start and end apart: 28, of which 13 were waited for; matrix products, arithmetic and copies ran while one was open for 0% of the time, Pallas kernels for 25%

profile of v2, /device:TPU:0, one launch (start us, length us, event | category | flops | bytes accessed | tf_op | source)
XLA Modules:
  0.0 100.5 jit_solution(10303928187835337746)
XLA Ops:
  0.0 1.4 %pack_kv.1 = (bf16[320,384]{1,0:T(8,128)(2,1)S(1)}, bf16[320,384]{1,0:T(8,128)(2,1)S(1)}, bf16[320,384]{1,0:T(8,128)(2,1)S(1)}, bf16[320,384]{1,0:T(8,128)(2,1)S(1)}) custom-call(bf16[384,768]{1,0:T(8,128)(2,1)} %k_ref.1, bf16[384,512]{1,0:T(8,128)(2,1)} %v_ref.1), custom_call_target="tpu_custom_call" | custom-call | flops 1048576 | bytes 1048576 | tf_op jit(solution)/shard_map/pack_kv/pallas_call | solution.py:76
  1.5 0.6 collective-permute-start.3
  2.0 2.6 %collective-permute-start.4 = (bf16[320,384]{1,0:T(8,128)(2,1)S(1)}, bf16[320,384]{1,0:T(8,128)(2,1)S(1)}, u32[]{:S(2)}, u32[]{:S(2)}) collective-permute-start(bf16[320,384]{1,0:T(8,128)(2,1)S(1)} %get-tuple-element.47), channel_id=1, source_target_pairs={{0,4},{2,6},{4,0},{6,2},{8,12},{10,14},{12,8},{14,10},{16,20},{18,... | collective-permute-start | bytes 737288 | tf_op jit(solution)/shard_map/ppermute | solution.py:595
  4.6 1.5 %cut.1 = (bf16[528,1024]{1,0:T(8,128)(2,1)S(1)}, bf16[704,512]{1,0:T(8,128)(2,1)S(1)}) custom-call(bf16[512,2048]{1,0:T(8,128)(2,1)} %w_ref.1, bf16[1,704,2048]{2,1,0:T(8,128)(2,1)} %down_ref.1, s32[1,192]{1,0:T(1,128)} %bitcast.7, bf16[320,384]{1,0:T(8,128)(2,1)S(1)} %get-tuple-element.41.after_ref.refs_4_), custom_call_target="tpu_custom_call" | custom-call | flops 1048576 | bytes 1048576 | tf_op jit(solution)/shard_map/cut/pallas_call | solution.py:117
  6.1 1.6 %collective-permute-start.17 = (bf16[528,1024]{1,0:T(8,128)(2,1)S(1)}, bf16[528,1024]{1,0:T(8,128)(2,1)S(1)}, u32[]{:S(2)}, u32[]{:S(2)}) collective-permute-start(bf16[528,1024]{1,0:T(8,128)(2,1)S(1)} %get-tuple-element.62), channel_id=1, source_target_pairs={{0,1},{1,0},{2,3},{3,2},{4,5},{5,4},{6,7},{7,6},{8,9},{9,8},{10,11... | collective-permute-start | bytes 3244040 | tf_op jit(solution)/shard_map/ppermute | solution.py:598
  7.6 0.0 collective-permute-start.5
  7.7 1.6 %collective-permute-start.6 = (bf16[320,384]{1,0:T(8,128)(2,1)S(1)}, bf16[320,384]{1,0:T(8,128)(2,1)S(1)}, u32[]{:S(2)}, u32[]{:S(2)}) collective-permute-start(bf16[320,384]{1,0:T(8,128)(2,1)S(1)} %get-tuple-element.41.after_ref.refs_4_), channel_id=1, source_target_pairs={{0,8},{2,10},{4,12},{6,14},{8,16},{10,18},{12,20},{14,22},{16,24},... | collective-permute-start | bytes 737288 | tf_op jit(solution)/shard_map/ppermute | solution.py:605
  9.2 0.0 collective-permute-done.3.refs_5_
  9.2 1.6 %collective-permute-start.7 = (bf16[320,384]{1,0:T(8,128)(2,1)S(1)}, bf16[320,384]{1,0:T(8,128)(2,1)S(1)}, u32[]{:S(2)}, u32[]{:S(2)}) collective-permute-start(bf16[320,384]{1,0:T(8,128)(2,1)S(1)} %collective-permute-done.3.refs_5_), channel_id=1, source_target_pairs={{0,8},{2,10},{4,12},{6,14},{8,16},{10,18},{12,20},{14,22},{16,24},... | collective-permute-start | bytes 737288 | tf_op jit(solution)/shard_map/ppermute | solution.py:605
  10.8 0.6 collective-permute-done.4.refs_6_
  11.4 2.1 %collective-permute-start.8 = (bf16[320,384]{1,0:T(8,128)(2,1)S(1)}, bf16[320,384]{1,0:T(8,128)(2,1)S(1)}, u32[]{:S(2)}, u32[]{:S(2)}) collective-permute-start(bf16[320,384]{1,0:T(8,128)(2,1)S(1)} %collective-permute-done.4.refs_6_), channel_id=1, source_target_pairs={{0,8},{2,10},{4,12},{6,14},{8,16},{10,18},{12,20},{14,22},{16,24},... | collective-permute-start | bytes 737288 | tf_op jit(solution)/shard_map/ppermute | solution.py:605
  13.5 2.6 %collective-permute-done.5.refs_7_.refs_4_ = bf16[320,384]{1,0:T(8,128)(2,1)S(1)} collective-permute-done((bf16[320,384]{1,0:T(8,128)(2,1)S(1)}, bf16[320,384]{1,0:T(8,128)(2,1)S(1)}, u32[]{:S(2)}, u32[]{:S(2)}) %collective-permute-start.5) | collective-permute-done | bytes 245792 | tf_op jit(solution)/shard_map/ppermute | solution.py:595
  16.1 1.5 %collective-permute-start.9 = (bf16[320,384]{1,0:T(8,128)(2,1)S(1)}, bf16[320,384]{1,0:T(8,128)(2,1)S(1)}, u32[]{:S(2)}, u32[]{:S(2)}) collective-permute-start(bf16[320,384]{1,0:T(8,128)(2,1)S(1)} %collective-permute-done.5.refs_7_.refs_4_), channel_id=1, source_target_pairs={{0,8},{2,10},{4,12},{6,14},{8,16},{10,18},{12,20},{14,22},{16,24},... | collective-permute-start | bytes 737288 | tf_op jit(solution)/shard_map/ppermute | solution.py:605
  17.7 1.3 %pack_q.1 = (bf16[240,384]{1,0:T(8,128)(2,1)S(1)}, bf16[240,384]{1,0:T(8,128)(2,1)S(1)}, bf16[240,384]{1,0:T(8,128)(2,1)S(1)}, bf16[240,384]{1,0:T(8,128)(2,1)S(1)}) custom-call(s32[3,16]{1,0:T(4,128)} %layout_hbm.1, bf16[384,768]{1,0:T(8,128)(2,1)} %q_ref.1, bf16[320,384]{1,0:T(8,128)(2,1)S(1)} %get-tuple-element.41.after_ref.refs_4_), custom_call_target="tpu_custom_call" | custom-call | flops 1048576 | bytes 1048576 | tf_op jit(solution)/shard_map/pack_q/pallas_call | solution.py:196
  19.0 0.0 collective-permute-done.6.refs_3_.refs_0_
  19.0 0.4 collective-permute-start
  19.5 4.1 %collective-permute-done.7.refs_4_.refs_1_ = bf16[320,384]{1,0:T(8,128)(2,1)S(1)} collective-permute-done((bf16[320,384]{1,0:T(8,128)(2,1)S(1)}, bf16[320,384]{1,0:T(8,128)(2,1)S(1)}, u32[]{:S(2)}, u32[]{:S(2)}) %collective-permute-start.7) | collective-permute-done | bytes 245792 | tf_op jit(solution)/shard_map/ppermute | solution.py:605
  23.6 1.5 %collective-permute-start.1 = (bf16[240,384]{1,0:T(8,128)(2,1)S(1)}, bf16[240,384]{1,0:T(8,128)(2,1)S(1)}, u32[]{:S(2)}, u32[]{:S(2)}) collective-permute-start(bf16[240,384]{1,0:T(8,128)(2,1)S(1)} %get-tuple-element.44), channel_id=1, source_target_pairs={{0,4},{2,6},{4,0},{6,2},{8,12},{10,14},{12,8},{14,10},{16,20},{18,... | collective-permute-start | bytes 552968 | tf_op jit(solution)/shard_map/ppermute | solution.py:595
  25.0 3.8 %collective-permute-done.8.refs_5_.refs_2_ = bf16[320,384]{1,0:T(8,128)(2,1)S(1)} collective-permute-done((bf16[320,384]{1,0:T(8,128)(2,1)S(1)}, bf16[320,384]{1,0:T(8,128)(2,1)S(1)}, u32[]{:S(2)}, u32[]{:S(2)}) %collective-permute-start.8) | collective-permute-done | bytes 245792 | tf_op jit(solution)/shard_map/ppermute | solution.py:605
  28.8 0.7 collective-permute-start.2
  29.5 4.3 %collective-permute-done.9.refs_6_.refs_3_ = bf16[320,384]{1,0:T(8,128)(2,1)S(1)} collective-permute-done((bf16[320,384]{1,0:T(8,128)(2,1)S(1)}, bf16[320,384]{1,0:T(8,128)(2,1)S(1)}, u32[]{:S(2)}, u32[]{:S(2)}) %collective-permute-start.9) | collective-permute-done | bytes 245792 | tf_op jit(solution)/shard_map/ppermute | solution.py:605
  33.8 0.5 collective-permute-start.24
  34.4 0.0 collective-permute-done.refs_1_
  34.4 0.1 collective-permute-start.10
  34.4 0.0 collective-permute-done.1.refs_2_
  34.5 1.3 %collective-permute-start.11 = (bf16[320,384]{1,0:T(8,128)(2,1)S(1)}, bf16[320,384]{1,0:T(8,128)(2,1)S(1)}, u32[]{:S(2)}, u32[]{:S(2)}) collective-permute-start(bf16[320,384]{1,0:T(8,128)(2,1)S(1)} %shard_map.112), channel_id=1, source_target_pairs={{0,8},{2,10},{4,12},{6,14},{8,16},{10,18},{12,20},{14,22},{16,24},... | collective-permute-start | bytes 737288 | tf_op jit(solution)/shard_map/ppermute | solution.py:605
  35.7 0.0 collective-permute-done.2.refs_3_
  35.7 3.6 %shard_map.109 = (bf16[1536,256]{1,0:T(8,128)(2,1)S(1)}, f32[1536,128]{1,0:T(8,128)S(1)}, f32[1536,256]{1,0:T(8,128)S(1)}) custom-call(bf16[240,384]{1,0:T(8,128)(2,1)S(1)} %get-tuple-element.42.refs_0_, bf16[240,384]{1,0:T(8,128)(2,1)S(1)} %collective-permute-done.refs_1_, bf16[240,384]{1,0:T(8,128)(2,1)S(1)} %collective-permute-done.1.refs_2_, ...), custom_call_target="tpu_custom_call" | custom-call | flops 2415919104 | bytes 1048576 | tf_op jit(solution)/shard_map/pallas_call | solution.py:350
  39.3 0.1 shard_map.114
  39.4 1.8 %collective-permute-start.12 = (bf16[320,384]{1,0:T(8,128)(2,1)S(1)}, bf16[320,384]{1,0:T(8,128)(2,1)S(1)}, u32[]{:S(2)}, u32[]{:S(2)}) collective-permute-start(bf16[320,384]{1,0:T(8,128)(2,1)S(1)} %shard_map.114), channel_id=1, source_target_pairs={{0,8},{2,10},{4,12},{6,14},{8,16},{10,18},{12,20},{14,22},{16,24},... | collective-permute-start | bytes 737288 | tf_op jit(solution)/shard_map/ppermute | solution.py:605
  41.2 3.7 %shard_map.110 = (f32[1536,128]{1,0:T(8,128)S(1)}, f32[1536,256]{1,0:T(8,128)S(1)}) custom-call(bf16[1536,256]{1,0:T(8,128)(2,1)S(1)} %get-tuple-element.49.refs_0_, f32[1536,128]{1,0:T(8,128)S(1)} %get-tuple-element.50.refs_1_, f32[1536,256]{1,0:T(8,128)S(1)} %get-tuple-element.51.refs_2_, ...), custom_call_target="tpu_custom_call", output_to_operand_aliasing={{0}: (1, {}), {1}: (2, {})} | custom-call | flops 2415919104 | bytes 1048576 | tf_op jit(solution)/shard_map/pallas_call | solution.py:350
  44.9 0.2 collective-permute-done.10.refs_3_
  45.1 5.3 %collective-permute-done.11.refs_4_ = bf16[320,384]{1,0:T(8,128)(2,1)S(1)} collective-permute-done((bf16[320,384]{1,0:T(8,128)(2,1)S(1)}, bf16[320,384]{1,0:T(8,128)(2,1)S(1)}, u32[]{:S(2)}, u32[]{:S(2)}) %collective-permute-start.11) | collective-permute-done | bytes 245792 | tf_op jit(solution)/shard_map/ppermute | solution.py:605
  50.3 1.8 %shard_map.113 = (f32[1536,128]{1,0:T(8,128)S(1)}, f32[1536,256]{1,0:T(8,128)S(1)}, bf16[1536,128]{1,0:T(8,128)(2,1)S(1)}) custom-call(bf16[1536,256]{1,0:T(8,128)(2,1)S(1)} %get-tuple-element.49.refs_0_, f32[1536,128]{1,0:T(8,128)S(1)} %get-tuple-element.52.refs_1_, ...), custom_call_target="tpu_custom_call", output_to_operand_aliasing={{0}: (1, {}), {1}: (2, {})} | custom-call | flops 905969664 | bytes 1048576 | tf_op jit(solution)/shard_map/pallas_call | solution.py:350
  52.1 2.1 %collective-permute-done.12.refs_4_ = bf16[320,384]{1,0:T(8,128)(2,1)S(1)} collective-permute-done((bf16[320,384]{1,0:T(8,128)(2,1)S(1)}, bf16[320,384]{1,0:T(8,128)(2,1)S(1)}, u32[]{:S(2)}, u32[]{:S(2)}) %collective-permute-start.12) | collective-permute-done | bytes 245792 | tf_op jit(solution)/shard_map/ppermute | solution.py:605
  54.2 1.5 %shard_map.115 = (bf16[384,128]{1,0:T(8,128)(2,1)S(1)}, bf16[384,128]{1,0:T(8,128)(2,1)S(1)}, bf16[384,128]{1,0:T(8,128)(2,1)S(1)}, bf16[384,128]{1,0:T(8,128)(2...) custom-call(bf16[1536,256]{1,0:T(8,128)(2,1)S(1)} %get-tuple-element, ...), custom_call_target="tpu_custom_call", output_to_operand_aliasing={{8}: (3, {})} | custom-call | flops 301989888 | bytes 1048576 | tf_op jit(solution)/shard_map/pallas_call | solution.py:350
  55.7 0.1 collective-permute-start.18
  55.8 0.0 collective-permute-done.24.refs_0_
  55.8 1.5 %collective-permute-start.25 = (bf16[704,512]{1,0:T(8,128)(2,1)S(1)}, bf16[704,512]{1,0:T(8,128)(2,1)S(1)}, u32[]{:S(2)}, u32[]{:S(2)}) collective-permute-start(bf16[704,512]{1,0:T(8,128)(2,1)S(1)} %collective-permute-done.24.refs_0_), channel_id=1, source_target_pairs={{0,4},{2,6},{4,0},{6,2},{8,12},{10,14},{12,8},{14,10},{16,20},{18,... | collective-permute-start | bytes 2162696 | tf_op jit(solution)/shard_map/ppermute | solution.py:595
  57.4 1.5 %collective-permute-start.19 = (bf16[192,128]{1,0:T(8,128)(2,1)S(1)}, bf16[192,128]{1,0:T(8,128)(2,1)S(1)}, u32[]{:S(2)}, u32[]{:S(2)}) collective-permute-start(bf16[192,128]{1,0:T(8,128)(2,1)S(1)} %get-tuple-element.70), channel_id=1, source_target_pairs={{0,1},{1,0},{2,3},{3,2},{4,5},{5,4},{6,7},{7,6},{8,9},{9,8},{10,11... | collective-permute-start | bytes 147464 | tf_op jit(solution)/shard_map/ppermute | solution.py:598
  58.9 0.0 collective-permute-start.13
  58.9 0.5 collective-permute-start.14
  59.4 2.0 %collective-permute-done.19.refs_1_ = bf16[192,128]{1,0:T(8,128)(2,1)S(1)} collective-permute-done((bf16[192,128]{1,0:T(8,128)(2,1)S(1)}, bf16[192,128]{1,0:T(8,128)(2,1)S(1)}, u32[]{:S(2)}, u32[]{:S(2)}) %collective-permute-start.19) | collective-permute-done | bytes 49184 | tf_op jit(solution)/shard_map/ppermute | solution.py:598
  61.5 4.2 %stage.1 = (bf16[1,704,2048]{2,1,0:T(8,128)(2,1)S(1)}, bf16[1,704,2048]{2,1,0:T(8,128)(2,1)S(1)}, bf16[512,2048]{1,0:T(8,128)(2,1)S(1)}, bf16[1,704,2048]{2,1,0:T(8,128)(2,1)S(1)}) custom-call(bf16[1,704,2048]{2,1,0:T(8,128)(2,1)} %bitcast.10, bf16[1,704,2048]{2,1,0:T(8,128)(2,1)} %bitcast.11, bf16[512,2048]{1,0:T(8,128)(2,1)} %w_ref.1, ...), custom_call_target="tpu_custom_call" | custom-call | flops 1048576 | bytes 1048576 | tf_op jit(solution)/shard_map/stage/pallas_call | solution.py:145
  65.6 0.0 collective-permute-done.13.refs_1_
  65.6 1.8 %collective-permute-start.20 = (bf16[192,128]{1,0:T(8,128)(2,1)S(1)}, bf16[192,128]{1,0:T(8,128)(2,1)S(1)}, u32[]{:S(2)}, u32[]{:S(2)}) collective-permute-start(bf16[192,128]{1,0:T(8,128)(2,1)S(1)} %get-tuple-element.71), channel_id=1, source_target_pairs={{0,3},{1,2},{2,1},{3,0},{4,7},{5,6},{6,5},{7,4},{8,11},{9,10},{10,... | collective-permute-start | bytes 147464 | tf_op jit(solution)/shard_map/ppermute | solution.py:602
  67.5 9.5 %collective-permute-done.14.refs_2_ = bf16[384,128]{1,0:T(8,128)(2,1)S(1)} collective-permute-done((bf16[384,128]{1,0:T(8,128)(2,1)S(1)}, bf16[384,128]{1,0:T(8,128)(2,1)S(1)}, u32[]{:S(2)}, u32[]{:S(2)}) %collective-permute-start.14) | collective-permute-done | bytes 98336 | tf_op jit(solution)/shard_map/ppermute | solution.py:595
  77.0 2.4 %collective-permute-start.21 = (bf16[192,128]{1,0:T(8,128)(2,1)S(1)}, bf16[192,128]{1,0:T(8,128)(2,1)S(1)}, u32[]{:S(2)}, u32[]{:S(2)}) collective-permute-start(bf16[192,128]{1,0:T(8,128)(2,1)S(1)} %get-tuple-element.72), channel_id=1, source_target_pairs={{0,5},{1,4},{2,7},{3,6},{4,1},{5,0},{6,3},{7,2},{8,13},{9,12},{10,... | collective-permute-start | bytes 147464 | tf_op jit(solution)/shard_map/ppermute | solution.py:602
  79.4 0.0 collective-permute-done.15.refs_3_
  79.4 1.0 collective-permute-start.22
  80.4 1.0 %half_out.1.refs_0_ = f32[384,2048]{1,0:T(8,128)S(1)} custom-call(bf16[384,128]{1,0:T(8,128)(2,1)S(1)} %get-tuple-element.57.refs_0_, bf16[384,128]{1,0:T(8,128)(2,1)S(1)} %collective-permute-done.13.refs_1_, bf16[384,128]{1,0:T(8,128)(2,1)S(1)} %collective-permute-done.14.refs_2_, bf16[384,128]{1,0:T(8,128)(2,1)S(1)} %collective-permute-done.15.refs_3_, ...), custom_call_target="tpu_custom_call" | custom-call | flops 805306368 | bytes 1048576 | tf_op jit(solution)/shard_map/half_out/pallas_call | solution.py:401
  81.5 0.0 collective-permute-done.20.refs_2_
  81.5 0.5 collective-permute-done.21.refs_3_
  82.0 1.9 %collective-permute-done.22.refs_4_ = bf16[192,128]{1,0:T(8,128)(2,1)S(1)} collective-permute-done((bf16[192,128]{1,0:T(8,128)(2,1)S(1)}, bf16[192,128]{1,0:T(8,128)(2,1)S(1)}, u32[]{:S(2)}, u32[]{:S(2)}) %collective-permute-start.22) | collective-permute-done | bytes 49184 | tf_op jit(solution)/shard_map/ppermute | solution.py:602
  83.9 0.0 collective-permute-done.18.refs_3_.refs_6_
  83.9 2.8 %hidden_peer.1 = bf16[792,128]{1,0:T(8,128)(2,1)S(1)} custom-call(f32[384,2048]{1,0:T(8,128)S(1)} %half_out.1.refs_0_, bf16[192,128]{1,0:T(8,128)(2,1)S(1)} %collective-permute-done.19.refs_1_, bf16[192,128]{1,0:T(8,128)(2,1)S(1)} %collective-permute-done.20.refs_2_, bf16[192,128]{1,0:T(8,128)(2,1)S(1)} %collective-permute-done.21.refs_3_, ...), custom_call_target="tpu_custom_call" | custom-call | flops 1912602624 | bytes 1048576 | tf_op jit(solution)/shard_map/hidden_peer/pallas_call | solution.py:523
  86.7 0.0 collective-permute-done.25.refs_2_
  86.7 0.1 collective-permute-start.26
  86.8 0.5 collective-permute-start.27
  87.3 1.0 collective-permute-start.16
  88.3 1.1 %collective-permute-start.23 = (bf16[792,128]{1,0:T(8,128)(2,1)S(1)}, bf16[792,128]{1,0:T(8,128)(2,1)S(1)}, u32[]{:S(2)}, u32[]{:S(2)}) collective-permute-start(bf16[792,128]{1,0:T(8,128)(2,1)S(1)} %hidden_peer.1), channel_id=1, source_target_pairs={{0,1},{1,0},{2,3},{3,2},{4,5},{5,4},{6,7},{7,6},{8,9},{9,8},{10,11... | collective-permute-start | bytes 608264 | tf_op jit(solution)/shard_map/ppermute | solution.py:598
  89.4 5.7 %collective-permute-done.16.refs_1_ = bf16[768,128]{1,0:T(8,128)(2,1)S(1)} collective-permute-done((bf16[768,128]{1,0:T(8,128)(2,1)S(1)}, bf16[768,128]{1,0:T(8,128)(2,1)S(1)}, u32[]{:S(2)}, u32[]{:S(2)}) %collective-permute-start.16) | collective-permute-done | bytes 196640 | tf_op jit(solution)/shard_map/ppermute | solution.py:598
  95.2 3.5 %hidden_own.1 = (f32[192,2048]{1,0:T(8,128)S(1)}, f32[192,2048]{1,0:T(8,128)S(1)}, bf16[192,144]{1,0:T(8,128)(2,1)S(1)}) custom-call(f32[384,2048]{1,0:T(8,128)S(1)} %half_out.1.refs_0_, bf16[768,128]{1,0:T(8,128)(2,1)S(1)} %collective-permute-done.16.refs_1_, bf16[528,1024]{1,0:T(8,128)(2,1)S(1)} %collective-permute-done.17.refs_2_.refs_5_, ...), custom_call_target="tpu_custom_call" | custom-call | flops 1912602624 | bytes 1048576 | tf_op jit(solution)/shard_map/hidden_own/pallas_call | solution.py:523
  98.7 1.7 %combine.1 = bf16[192,2048]{1,0:T(8,128)(2,1)} custom-call(f32[192,2048]{1,0:T(8,128)S(1)} %get-tuple-element.67.attended, f32[192,2048]{1,0:T(8,128)S(1)} %get-tuple-element.68.partial, bf16[192,144]{1,0:T(8,128)(2,1)S(1)} %get-tuple-element.69.place, bf16[792,128]{1,0:T(8,128)(2,1)S(1)} %collective-permute-done.23.hid_peer, f32[1,192]{1,0:T(1,128)S(1)} %bitcast.9, ...), custom_call_target="tpu_custom_call" | custom-call | flops 1048576 | bytes 1048576 | tf_op jit(solution)/shard_map/combine/pallas_call | solution.py:559
  (14 shorter events, 0.1 us)
Async XLA Ops:
  1.5 7.8 %collective-permute-start.3 = (bf16[320,384]{1,0:T(8,128)(2,1)S(1)}, bf16[320,384]{1,0:T(8,128)(2,1)S(1)}, u32[]{:S(2)}, u32[]{:S(2)}) collective-permute-start(bf16[320,384]{1,0:T(8,128)(2,1)S(1)} %get-tuple-element.46), channel_id=1, source_target_pairs={{0,2},{2,0},{4,6},{6,4},{8,10},{10,8},{12,14},{14,12},{16,18},{18,... | collective-permute-start | bytes 737288 | tf_op jit(solution)/shard_map/ppermute | solution.py:595
  2.0 9.4 %collective-permute-start.4 = (bf16[320,384]{1,0:T(8,128)(2,1)S(1)}, bf16[320,384]{1,0:T(8,128)(2,1)S(1)}, u32[]{:S(2)}, u32[]{:S(2)}) collective-permute-start(bf16[320,384]{1,0:T(8,128)(2,1)S(1)} %get-tuple-element.47), channel_id=1, source_target_pairs={{0,4},{2,6},{4,0},{6,2},{8,12},{10,14},{12,8},{14,10},{16,20},{18,... | collective-permute-start | bytes 737288 | tf_op jit(solution)/shard_map/ppermute | solution.py:595
  6.1 49.7 %collective-permute-start.17 = (bf16[528,1024]{1,0:T(8,128)(2,1)S(1)}, bf16[528,1024]{1,0:T(8,128)(2,1)S(1)}, u32[]{:S(2)}, u32[]{:S(2)}) collective-permute-start(bf16[528,1024]{1,0:T(8,128)(2,1)S(1)} %get-tuple-element.62), channel_id=1, source_target_pairs={{0,1},{1,0},{2,3},{3,2},{4,5},{5,4},{6,7},{7,6},{8,9},{9,8},{10,11... | collective-permute-start | bytes 3244040 | tf_op jit(solution)/shard_map/ppermute | solution.py:598
  7.6 8.5 %collective-permute-start.5 = (bf16[320,384]{1,0:T(8,128)(2,1)S(1)}, bf16[320,384]{1,0:T(8,128)(2,1)S(1)}, u32[]{:S(2)}, u32[]{:S(2)}) collective-permute-start(bf16[320,384]{1,0:T(8,128)(2,1)S(1)} %get-tuple-element.48), channel_id=1, source_target_pairs={{0,6},{2,4},{4,2},{6,0},{8,14},{10,12},{12,10},{14,8},{16,22},{18,... | collective-permute-start | bytes 737288 | tf_op jit(solution)/shard_map/ppermute | solution.py:595
  7.7 11.4 %collective-permute-start.6 = (bf16[320,384]{1,0:T(8,128)(2,1)S(1)}, bf16[320,384]{1,0:T(8,128)(2,1)S(1)}, u32[]{:S(2)}, u32[]{:S(2)}) collective-permute-start(bf16[320,384]{1,0:T(8,128)(2,1)S(1)} %get-tuple-element.41.after_ref.refs_4_), channel_id=1, source_target_pairs={{0,8},{2,10},{4,12},{6,14},{8,16},{10,18},{12,20},{14,22},{16,24},... | collective-permute-start | bytes 737288 | tf_op jit(solution)/shard_map/ppermute | solution.py:605
  9.2 14.3 %collective-permute-start.7 = (bf16[320,384]{1,0:T(8,128)(2,1)S(1)}, bf16[320,384]{1,0:T(8,128)(2,1)S(1)}, u32[]{:S(2)}, u32[]{:S(2)}) collective-permute-start(bf16[320,384]{1,0:T(8,128)(2,1)S(1)} %collective-permute-done.3.refs_5_), channel_id=1, source_target_pairs={{0,8},{2,10},{4,12},{6,14},{8,16},{10,18},{12,20},{14,22},{16,24},... | collective-permute-start | bytes 737288 | tf_op jit(solution)/shard_map/ppermute | solution.py:605
  11.4 17.4 %collective-permute-start.8 = (bf16[320,384]{1,0:T(8,128)(2,1)S(1)}, bf16[320,384]{1,0:T(8,128)(2,1)S(1)}, u32[]{:S(2)}, u32[]{:S(2)}) collective-permute-start(bf16[320,384]{1,0:T(8,128)(2,1)S(1)} %collective-permute-done.4.refs_6_), channel_id=1, source_target_pairs={{0,8},{2,10},{4,12},{6,14},{8,16},{10,18},{12,20},{14,22},{16,24},... | collective-permute-start | bytes 737288 | tf_op jit(solution)/shard_map/ppermute | solution.py:605
  16.1 17.7 %collective-permute-start.9 = (bf16[320,384]{1,0:T(8,128)(2,1)S(1)}, bf16[320,384]{1,0:T(8,128)(2,1)S(1)}, u32[]{:S(2)}, u32[]{:S(2)}) collective-permute-start(bf16[320,384]{1,0:T(8,128)(2,1)S(1)} %collective-permute-done.5.refs_7_.refs_4_), channel_id=1, source_target_pairs={{0,8},{2,10},{4,12},{6,14},{8,16},{10,18},{12,20},{14,22},{16,24},... | collective-permute-start | bytes 737288 | tf_op jit(solution)/shard_map/ppermute | solution.py:605
  19.0 15.3 %collective-permute-start = (bf16[240,384]{1,0:T(8,128)(2,1)S(1)}, bf16[240,384]{1,0:T(8,128)(2,1)S(1)}, u32[]{:S(2)}, u32[]{:S(2)}) collective-permute-start(bf16[240,384]{1,0:T(8,128)(2,1)S(1)} %get-tuple-element.43), channel_id=1, source_target_pairs={{0,2},{2,0},{4,6},{6,4},{8,10},{10,8},{12,14},{14,12},{16,18},{18,... | collective-permute-start | bytes 552968 | tf_op jit(solution)/shard_map/ppermute | solution.py:595
  23.6 10.9 %collective-permute-start.1 = (bf16[240,384]{1,0:T(8,128)(2,1)S(1)}, bf16[240,384]{1,0:T(8,128)(2,1)S(1)}, u32[]{:S(2)}, u32[]{:S(2)}) collective-permute-start(bf16[240,384]{1,0:T(8,128)(2,1)S(1)} %get-tuple-element.44), channel_id=1, source_target_pairs={{0,4},{2,6},{4,0},{6,2},{8,12},{10,14},{12,8},{14,10},{16,20},{18,... | collective-permute-start | bytes 552968 | tf_op jit(solution)/shard_map/ppermute | solution.py:595
  28.8 6.9 %collective-permute-start.2 = (bf16[240,384]{1,0:T(8,128)(2,1)S(1)}, bf16[240,384]{1,0:T(8,128)(2,1)S(1)}, u32[]{:S(2)}, u32[]{:S(2)}) collective-permute-start(bf16[240,384]{1,0:T(8,128)(2,1)S(1)} %get-tuple-element.45), channel_id=1, source_target_pairs={{0,6},{2,4},{4,2},{6,0},{8,14},{10,12},{12,10},{14,8},{16,22},{18,... | collective-permute-start | bytes 552968 | tf_op jit(solution)/shard_map/ppermute | solution.py:595
  33.8 22.0 %collective-permute-start.24 = (bf16[704,512]{1,0:T(8,128)(2,1)S(1)}, bf16[704,512]{1,0:T(8,128)(2,1)S(1)}, u32[]{:S(2)}, u32[]{:S(2)}) collective-permute-start(bf16[704,512]{1,0:T(8,128)(2,1)S(1)} %get-tuple-element.74), channel_id=1, source_target_pairs={{0,1},{1,0},{2,3},{3,2},{4,5},{5,4},{6,7},{7,6},{8,9},{9,8},{10,11... | collective-permute-start | bytes 2162696 | tf_op jit(solution)/shard_map/ppermute | solution.py:598
  34.4 10.7 %collective-permute-start.10 = (bf16[320,384]{1,0:T(8,128)(2,1)S(1)}, bf16[320,384]{1,0:T(8,128)(2,1)S(1)}, u32[]{:S(2)}, u32[]{:S(2)}) collective-permute-start(bf16[320,384]{1,0:T(8,128)(2,1)S(1)} %shard_map.111), channel_id=1, source_target_pairs={{0,8},{2,10},{4,12},{6,14},{8,16},{10,18},{12,20},{14,22},{16,24},... | collective-permute-start | bytes 737288 | tf_op jit(solution)/shard_map/ppermute | solution.py:605
  34.5 15.9 %collective-permute-start.11 = (bf16[320,384]{1,0:T(8,128)(2,1)S(1)}, bf16[320,384]{1,0:T(8,128)(2,1)S(1)}, u32[]{:S(2)}, u32[]{:S(2)}) collective-permute-start(bf16[320,384]{1,0:T(8,128)(2,1)S(1)} %shard_map.112), channel_id=1, source_target_pairs={{0,8},{2,10},{4,12},{6,14},{8,16},{10,18},{12,20},{14,22},{16,24},... | collective-permute-start | bytes 737288 | tf_op jit(solution)/shard_map/ppermute | solution.py:605
  39.4 14.8 %collective-permute-start.12 = (bf16[320,384]{1,0:T(8,128)(2,1)S(1)}, bf16[320,384]{1,0:T(8,128)(2,1)S(1)}, u32[]{:S(2)}, u32[]{:S(2)}) collective-permute-start(bf16[320,384]{1,0:T(8,128)(2,1)S(1)} %shard_map.114), channel_id=1, source_target_pairs={{0,8},{2,10},{4,12},{6,14},{8,16},{10,18},{12,20},{14,22},{16,24},... | collective-permute-start | bytes 737288 | tf_op jit(solution)/shard_map/ppermute | solution.py:605
  55.7 28.1 %collective-permute-start.18 = (bf16[528,1024]{1,0:T(8,128)(2,1)S(1)}, bf16[528,1024]{1,0:T(8,128)(2,1)S(1)}, u32[]{:S(2)}, u32[]{:S(2)}) collective-permute-start(bf16[528,1024]{1,0:T(8,128)(2,1)S(1)} %collective-permute-done.17.refs_2_.refs_5_), channel_id=1, source_target_pairs={{0,2},{2,0},{4,6},{6,4},{8,10},{10,8},{12,14},{14,12},{16,18},{18,... | collective-permute-start | bytes 3244040 | tf_op jit(solution)/shard_map/ppermute | solution.py:595
  55.8 30.9 %collective-permute-start.25 = (bf16[704,512]{1,0:T(8,128)(2,1)S(1)}, bf16[704,512]{1,0:T(8,128)(2,1)S(1)}, u32[]{:S(2)}, u32[]{:S(2)}) collective-permute-start(bf16[704,512]{1,0:T(8,128)(2,1)S(1)} %collective-permute-done.24.refs_0_), channel_id=1, source_target_pairs={{0,4},{2,6},{4,0},{6,2},{8,12},{10,14},{12,8},{14,10},{16,20},{18,... | collective-permute-start | bytes 2162696 | tf_op jit(solution)/shard_map/ppermute | solution.py:595
  57.4 4.1 %collective-permute-start.19 = (bf16[192,128]{1,0:T(8,128)(2,1)S(1)}, bf16[192,128]{1,0:T(8,128)(2,1)S(1)}, u32[]{:S(2)}, u32[]{:S(2)}) collective-permute-start(bf16[192,128]{1,0:T(8,128)(2,1)S(1)} %get-tuple-element.70), channel_id=1, source_target_pairs={{0,1},{1,0},{2,3},{3,2},{4,5},{5,4},{6,7},{7,6},{8,9},{9,8},{10,11... | collective-permute-start | bytes 147464 | tf_op jit(solution)/shard_map/ppermute | solution.py:598
  58.9 6.8 %collective-permute-start.13 = (bf16[384,128]{1,0:T(8,128)(2,1)S(1)}, bf16[384,128]{1,0:T(8,128)(2,1)S(1)}, u32[]{:S(2)}, u32[]{:S(2)}) collective-permute-start(bf16[384,128]{1,0:T(8,128)(2,1)S(1)} %get-tuple-element.58), channel_id=1, source_target_pairs={{0,2},{2,0},{4,6},{6,4},{8,10},{10,8},{12,14},{14,12},{16,18},{18,... | collective-permute-start | bytes 294920 | tf_op jit(solution)/shard_map/ppermute | solution.py:595
  58.9 18.1 %collective-permute-start.14 = (bf16[384,128]{1,0:T(8,128)(2,1)S(1)}, bf16[384,128]{1,0:T(8,128)(2,1)S(1)}, u32[]{:S(2)}, u32[]{:S(2)}) collective-permute-start(bf16[384,128]{1,0:T(8,128)(2,1)S(1)} %get-tuple-element.59), channel_id=1, source_target_pairs={{0,4},{2,6},{4,0},{6,2},{8,12},{10,14},{12,8},{14,10},{16,20},{18,... | collective-permute-start | bytes 294920 | tf_op jit(solution)/shard_map/ppermute | solution.py:595
  61.5 18.0 %collective-permute-start.15 = (bf16[384,128]{1,0:T(8,128)(2,1)S(1)}, bf16[384,128]{1,0:T(8,128)(2,1)S(1)}, u32[]{:S(2)}, u32[]{:S(2)}) collective-permute-start(bf16[384,128]{1,0:T(8,128)(2,1)S(1)} %get-tuple-element.60), channel_id=1, source_target_pairs={{0,6},{2,4},{4,2},{6,0},{8,14},{10,12},{12,10},{14,8},{16,22},{18,... | collective-permute-start | bytes 294920 | tf_op jit(solution)/shard_map/ppermute | solution.py:595
  65.6 15.8 %collective-permute-start.20 = (bf16[192,128]{1,0:T(8,128)(2,1)S(1)}, bf16[192,128]{1,0:T(8,128)(2,1)S(1)}, u32[]{:S(2)}, u32[]{:S(2)}) collective-permute-start(bf16[192,128]{1,0:T(8,128)(2,1)S(1)} %get-tuple-element.71), channel_id=1, source_target_pairs={{0,3},{1,2},{2,1},{3,0},{4,7},{5,6},{6,5},{7,4},{8,11},{9,10},{10,... | collective-permute-start | bytes 147464 | tf_op jit(solution)/shard_map/ppermute | solution.py:602
  77.0 5.0 %collective-permute-start.21 = (bf16[192,128]{1,0:T(8,128)(2,1)S(1)}, bf16[192,128]{1,0:T(8,128)(2,1)S(1)}, u32[]{:S(2)}, u32[]{:S(2)}) collective-permute-start(bf16[192,128]{1,0:T(8,128)(2,1)S(1)} %get-tuple-element.72), channel_id=1, source_target_pairs={{0,5},{1,4},{2,7},{3,6},{4,1},{5,0},{6,3},{7,2},{8,13},{9,12},{10,... | collective-permute-start | bytes 147464 | tf_op jit(solution)/shard_map/ppermute | solution.py:602
  79.4 4.4 %collective-permute-start.22 = (bf16[192,128]{1,0:T(8,128)(2,1)S(1)}, bf16[192,128]{1,0:T(8,128)(2,1)S(1)}, u32[]{:S(2)}, u32[]{:S(2)}) collective-permute-start(bf16[192,128]{1,0:T(8,128)(2,1)S(1)} %get-tuple-element.73), channel_id=1, source_target_pairs={{0,7},{1,6},{2,5},{3,4},{4,3},{5,2},{6,1},{7,0},{8,15},{9,14},{10,... | collective-permute-start | bytes 147464 | tf_op jit(solution)/shard_map/ppermute | solution.py:602
  80.4 3.4 %copy-start = (f32[2048]{0:T(1024)S(1)}, f32[2048]{0:T(1024)}, u32[]{:S(2)}) copy-start(f32[2048]{0:T(1024)} %param.16) | copy-start | bytes 24580
  83.9 11.3 %copy-start.1 = (s32[192,1]{0,1:T(1,128)S(1)}, s32[192,1]{0,1:T(1,128)}, u32[]{:S(2)}) copy-start(s32[192,1]{0,1:T(1,128)} %param.17) | copy-start | bytes 2308
  86.7 11.9 %collective-permute-start.26 = (bf16[704,512]{1,0:T(8,128)(2,1)S(1)}, bf16[704,512]{1,0:T(8,128)(2,1)S(1)}, u32[]{:S(2)}, u32[]{:S(2)}) collective-permute-start(bf16[704,512]{1,0:T(8,128)(2,1)S(1)} %collective-permute-done.24.refs_0_), channel_id=1, source_target_pairs={{0,2},{2,0},{4,6},{6,4},{8,10},{10,8},{12,14},{14,12},{16,18},{18,... | collective-permute-start | bytes 2162696 | tf_op jit(solution)/shard_map/ppermute | solution.py:595
  86.8 11.9 %collective-permute-start.27 = (bf16[704,512]{1,0:T(8,128)(2,1)S(1)}, bf16[704,512]{1,0:T(8,128)(2,1)S(1)}, u32[]{:S(2)}, u32[]{:S(2)}) collective-permute-start(bf16[704,512]{1,0:T(8,128)(2,1)S(1)} %collective-permute-done.25.refs_2_), channel_id=1, source_target_pairs={{0,2},{2,0},{4,6},{6,4},{8,10},{10,8},{12,14},{14,12},{16,18},{18,... | collective-permute-start | bytes 2162696 | tf_op jit(solution)/shard_map/ppermute | solution.py:595
  87.3 7.8 %collective-permute-start.16 = (bf16[768,128]{1,0:T(8,128)(2,1)S(1)}, bf16[768,128]{1,0:T(8,128)(2,1)S(1)}, u32[]{:S(2)}, u32[]{:S(2)}) collective-permute-start(bf16[768,128]{1,0:T(8,128)(2,1)S(1)} %own_tokens.1), channel_id=1, source_target_pairs={{0,1},{1,0},{2,3},{3,2},{4,5},{5,4},{6,7},{7,6},{8,9},{9,8},{10,11... | collective-permute-start | bytes 589832 | tf_op jit(solution)/shard_map/ppermute | solution.py:598
  88.3 10.4 %collective-permute-start.23 = (bf16[792,128]{1,0:T(8,128)(2,1)S(1)}, bf16[792,128]{1,0:T(8,128)(2,1)S(1)}, u32[]{:S(2)}, u32[]{:S(2)}) collective-permute-start(bf16[792,128]{1,0:T(8,128)(2,1)S(1)} %hidden_peer.1), channel_id=1, source_target_pairs={{0,1},{1,0},{2,3},{3,2},{4,5},{5,4},{6,7},{7,6},{8,9},{9,8},{10,11... | collective-permute-start | bytes 608264 | tf_op jit(solution)/shard_map/ppermute | solution.py:598
  95.1 3.5 %copy-start.2 = (f32[192,1]{0,1:T(1,128)S(1)}, f32[192,1]{0,1:T(1,128)}, u32[]{:S(2)}) copy-start(f32[192,1]{0,1:T(1,128)} %param.18) | copy-start | bytes 2308

commit v3 on v2

--- a/solution.py
+++ b/solution.py
@@ -89,44 +89,72 @@
     )(in_hbm(k), in_hbm(v))
 
 
-def cut_kernel(group, w_ref, down_ref, ids_ref, after_ref, w_out, down_out, ids_buf, sem):
+def cut_kernel(group, w_ref, down_ref, ids_ref, after_ref, w1_out, w2_out, down_out, ids_buf, sem):
     seq = lax.axis_index("seq")
     own = seq % group
-    width, quarter = w_out.shape[1], down_out.shape[1]
+    rows, width = w_ref.shape[0], w1_out.shape[1]
+    quarter = down_out.shape[1]
+    first = (seq % 2) * (8 * width)
+    outer = first + (seq // 2 % 2) * (7 * width)
     ids_load = pltpu.make_async_copy(ids_ref, ids_buf, sem.at[0])
     copies = [
         pltpu.make_async_copy(
-            down_ref.at[0, :, pl.ds(pl.multiple_of(own * quarter, 128), quarter)], down_out, sem.at[1]
+            w_ref.at[:, pl.ds(pl.multiple_of(outer, 128), width)], w1_out.at[:rows, :], sem.at[1]
         ),
         pltpu.make_async_copy(
-            w_ref.at[:, pl.ds(pl.multiple_of((seq % 2) * width, 128), width)],
-            w_out.at[: w_ref.shape[0], :],
-            sem.at[2],
+            down_ref.at[0, :, pl.ds(pl.multiple_of(own * quarter, 128), quarter)], down_out, sem.at[2]
+        ),
+        pltpu.make_async_copy(
+            w_ref.at[:, pl.ds(pl.multiple_of(first + width, 128), 6 * width)], w2_out, sem.at[3]
         ),
     ]
     for copy in [ids_load] + copies:
         copy.start()
     ids_load.wait()
     ids = jnp.broadcast_to(ids_buf[...].astype(F32), (EXTRA, ids_buf.shape[1]))
-    w_out[w_ref.shape[0] :, : ids_buf.shape[1]] = ids.astype(BF16)
+    columns = jnp.concatenate([ids, jnp.zeros((EXTRA, 2 * width - ids.shape[1]), F32)], axis=1)
+    w1_out[rows : rows + EXTRA, :] = columns[:, :width].astype(BF16)
+    w1_out[rows + EXTRA :, :] = columns[:, width:].astype(BF16)
     for copy in copies:
         copy.wait()
 
 
 def cut(w, down, ids, earlier, group):
+    width = w.shape[1] // 16
     return pl.pallas_call(
         functools.partial(cut_kernel, group),
         out_shape=[
-            pltpu.VMEM((w.shape[0] + EXTRA, w.shape[1] // 2), BF16),
+            pltpu.VMEM((w.shape[0] + 2 * EXTRA, width), BF16),
+            pltpu.VMEM((w.shape[0], 6 * width), BF16),
             pltpu.VMEM((down.shape[1], down.shape[2] // group), BF16),
         ],
         in_specs=[anywhere()] * 4,
-        out_specs=[vmem()] * 2,
-        scratch_shapes=[pltpu.VMEM(ids.shape, jnp.int32), pltpu.SemaphoreType.DMA((3,))],
+        out_specs=[vmem()] * 3,
+        scratch_shapes=[pltpu.VMEM(ids.shape, jnp.int32), pltpu.SemaphoreType.DMA((4,))],
         compiler_params=params(8),
         cost_estimate=pl.CostEstimate(flops=1 << 20, transcendentals=0, bytes_accessed=1 << 20),
         name="cut",
     )(in_hbm(w), in_hbm(down), in_hbm(ids), earlier)
+
+
+def join_outer_kernel(own_ref, other_ref, out_ref):
+    width = own_ref.shape[1]
+    far = lax.axis_index("seq") // 2 % 2
+    rows = out_ref.shape[0]
+    out_ref[:, pl.ds(pl.multiple_of(far * width, 128), width)] = own_ref[:rows, :]
+    out_ref[:, pl.ds(pl.multiple_of((1 - far) * width, 128), width)] = other_ref[:rows, :]
+
+
+def join_outer(own, other):
+    return pl.pallas_call(
+        join_outer_kernel,
+        out_shape=pltpu.VMEM((own.shape[0] - 2 * EXTRA, 2 * own.shape[1]), BF16),
+        in_specs=[vmem()] * 2,
+        out_specs=vmem(),
+        compiler_params=params(8),
+        cost_estimate=pl.CostEstimate(flops=1 << 20, transcendentals=0, bytes_accessed=1 << 20),
+        name="join_outer",
+    )(own, other)
 
 
 def stage_kernel(*refs):
@@ -469,8 +497,8 @@
 def hidden_kernel(group, mine, eps, *refs):
     count = 1 if mine else group
     partial_out, pieces, refs = refs[0], refs[1 : 1 + count], refs[1 + count :]
-    w_same, w_swap, gain, gate_w, up_w = refs[:5]
-    refs = refs[5:]
+    outer, outer_core, inner, inner_core, ids_row, gain, gate_w, up_w = refs[:8]
+    refs = refs[8:]
     if mine:
         ids, down_own, attended_ref, partial_ref, place_ref, ctx, att = refs
     else:
@@ -485,10 +513,11 @@
     for d in range(group):
         piece = pieces[0][d * rows_here : (d + 1) * rows_here, :] if mine else pieces[d][...]
         ctx[:, pl.ds(pl.multiple_of((own ^ d) * VD, VD), VD)] = piece
-    width = att.shape[1] // 2
-    for at, ref in ((side, w_same), (1 - side, w_swap)):
-        cols = pl.ds(pl.multiple_of(at * width, 128), width)
-        att[:, cols] = partial_out[rows, cols] + jnp.dot(ctx[...], ref[:half, :], preferred_element_type=F32)
+    width = att.shape[1] // 16
+    for at, edges, middle in ((side, outer, inner), (1 - side, outer_core, inner_core)):
+        for begin, ref in ((0, edges.at[:, :width]), (1, middle), (7, edges.at[:, width:])):
+            cols = pl.ds(pl.multiple_of((8 * at + begin) * width, 128), ref.shape[1])
+            att[:, cols] = partial_out[rows, cols] + jnp.dot(ctx[...], ref[...], preferred_element_type=F32)
     attended = att[...]
     rescale = lax.rsqrt(jnp.mean(attended * attended, axis=1, keepdims=True) + F32(eps))
     normed = (attended * rescale * gain[...]).astype(BF16)
@@ -503,19 +532,20 @@
         away = jnp.where(ids[...] == part, F32(0.0), F32(1.0))
         place_ref[...] = slots_of(away, place_ref.shape[1]).T.astype(BF16)
     else:
-        arriving = w_same[half : half + 1, :rows_here].astype(F32)
+        arriving = jnp.concatenate([ids_row[half : half + 1, :], ids_row[half + EXTRA : half + EXTRA + 1, :]], axis=1)
+        arriving = arriving[:, :rows_here].astype(F32)
         member = jnp.where(arriving == part.astype(F32), F32(1.0), F32(0.0))
         place = slots_of(member, capacity_of(rows_here)).astype(BF16)
         chosen = lax.dot_general(place, hidden, across, preferred_element_type=F32)
         pack_columns(hidden_ref, chosen)
 
 
-def hidden_part(group, partial_out, pieces, w_same, w_swap, gain, gate_w, up_w, *extra):
+def hidden_part(group, partial_out, pieces, w_parts, gain, gate_w, up_w, *extra):
     mine = bool(extra)
     rows = partial_out.shape[0] // 2
     width = partial_out.shape[1]
     inner = gate_w.shape[1]
-    inputs = [partial_out] + list(pieces) + [w_same, w_swap, gain, gate_w, up_w] + list(extra)
+    inputs = [partial_out] + list(pieces) + list(w_parts) + [gain, gate_w, up_w] + list(extra)
     if mine:
         outs = [pltpu.VMEM((rows, width), F32)] * 2 + [pltpu.VMEM((rows, capacity_of(rows)), BF16)]
     else:
@@ -601,8 +631,11 @@
         pairs = [(2 * i + e, 2 * (i ^ d) + 1 - e) for i in range(peers) for e in range(2)]
         return lax.ppermute(array, ("seq", "exp"), pairs)
 
-    def forward(array):
-        return lax.ppermute(array, "seq", [(i, (i + group) % peers) for i in range(peers)])
+    def forward(array, final):
+        pairs = [(i, (i + group) % peers) for i in range(peers)]
+        if final:
+            pairs = [(i, i + group) for i in range((phases - 2) * group, peers - group)]
+        return lax.ppermute(array, "seq", pairs)
 
     def needed(hop):
         return [
@@ -613,12 +646,14 @@
 
     ids = expert_ids.reshape(1, -1)
     kv = pack_kv(key_heads, value_heads, group)
-    w_part, down_part = cut(out_weight, down_weight, ids, kv[0], group)
+    w1_part, w2_part, down_part = cut(out_weight, down_weight, ids, kv[0], group)
     held = [kv[0]] + [swap(kv[d], d) for d in range(1, group)]
     qs = pack_q(queries, block_layout, kv[0], group, phases)
     qs = [qs[0]] + [swap(qs[d], d) for d in range(1, group)]
     down0 = across(down_part)
-    w_same = across(w_part)
+    w1 = across(w1_part)
+    w2 = across(w2_part)
+    outer = join_outer(w1, swap(w1, 2))
 
     tables = tuple((1, (tuple(g ^ d for g in range(group)),)) for d in range(group))
     early = group // 2
@@ -645,7 +680,8 @@
                 (1, (tuple(chains[g][k][2][g] for g in range(group)),)) for k in range(len(wanted))
             )
             parts = [gather(group, plan, parts[:early] if k == 0 else parts)[0] for k, plan in enumerate(plans)]
-        parts = [forward(part) for part in parts]
+        final = len(parts) - 1 if hop == phases - 1 else -1
+        parts = [forward(part, at == final) for at, part in enumerate(parts)]
 
         def seen(those):
             highest = max(max(table[c]) for count, table in those for c in range(count))
@@ -676,15 +712,16 @@
                 shards_seen=late,
                 finish=late,
             )
-    (w_same,) = after((w_same,), context[0])
-    w_swap = swap(w_same, 1)
+    outer_core = swap(outer, 1)
     whole, first = context[:group], context[group : 2 * group]
     same = [whole[0]] + [swap(whole[d], d) for d in range(1, group)]
     other = [across(first[0])] + [swap_across(first[d], d) for d in range(1, group)]
+    (w2,) = after((w2,), same[1])
+    w2_core = swap(w2, 1)
     mine = [across(own_tokens(same))]
     gain = norm_gain.reshape(1, -1)
     partial_out = half_out(same, out_now)
-    weights = (w_same, w_swap, gain, gate_now, up_now)
+    weights = ((outer, outer_core, w2, w2_core, w1), gain, gate_now, up_now)
     (hid_out,) = hidden_part(group, partial_out, other, *weights)
     hid_peer = across(hid_out)
     down0, down2 = after((down0, down2), hid_out)

time: 101 us -> 111 us (1.099)
  waiting for transfers between devices: 42.6 us -> 52 us
    ppermute x13 -> x15, waiting for transfers between devices: 12.7 us -> 22.7 us  [swap(): return lax.ppermute(array, 'seq', [(i, i ^ d) for i in range(peers)])]
    ppermute x7, waiting for transfers between devices: 19.7 us -> 11.2 us  [forward(): return lax.ppermute(array, 'seq', pairs)]
    ppermute x5 -> x6, waiting for transfers between devices: 7.78 us -> 15.5 us  [across(): return lax.ppermute(array, 'exp', [(0, 1), (1, 0)])]
    ppermute x13 -> x15, starting transfers between devices: 8.45 us -> 10.4 us  [swap(): return lax.ppermute(array, 'seq', [(i, i ^ d) for i in range(peers)])]
    ppermute x3, starting transfers between devices: 5.26 us -> 3.6 us  [swap_across(): return lax.ppermute(array, ('seq', 'exp'), pairs)]
    ppermute x5 -> x6, starting transfers between devices: 5.7 us -> 6.94 us  [across(): return lax.ppermute(array, 'exp', [(0, 1), (1, 0)])]
  transfers between devices with their start and end apart: 28 -> 31, of which waited for: 13 -> 13; matrix products, arithmetic and copies ran while one was open for 0% -> 0% of each run, Pallas kernels for 25% -> 23%
where the time goes in v3:
time: 111 us
  waiting for transfers between devices  52 us (47%)
  starting transfers between devices  30.1 us (27%)
  Pallas kernels  28.5 us (26%)
    ppermute x15, waiting for transfers between devices, swap(): return lax.ppermute(array, 'seq', [(i, i ^ d) for i in range(peers)])  22.7 us
    ppermute x6, waiting for transfers between devices, across(): return lax.ppermute(array, 'exp', [(0, 1), (1, 0)])  15.5 us
    ppermute x7, waiting for transfers between devices, forward(): return lax.ppermute(array, 'seq', pairs)  11.2 us
    pallas_call x4, Pallas kernels, attend(): pl.pallas_call(functools.partial(attend_kernel, group, tables, phase, fir...  10.6 us
    ppermute x15, starting transfers between devices, swap(): return lax.ppermute(array, 'seq', [(i, i ^ d) for i in range(peers)])  10.4 us
    ppermute x7, starting transfers between devices, forward(): return lax.ppermute(array, 'seq', pairs)  9.25 us
    ppermute x6, starting transfers between devices, across(): return lax.ppermute(array, 'exp', [(0, 1), (1, 0)])  6.94 us
    pallas_call x2, Pallas kernels, hidden_part(): pl.pallas_call(functools.partial(hidden_kernel, group, mine, 1e-06), out_...  6.5 us
  transfers between devices with their start and end apart: 31, of which 13 were waited for; matrix products, arithmetic and copies ran while one was open for 0% of the time, Pallas kernels for 23%

profile of v3, /device:TPU:0, one launch (start us, length us, event | category | flops | bytes accessed | tf_op | source)
XLA Modules:
  0.0 111.0 jit_solution(7745098675629422380)
XLA Ops:
  0.0 1.4 %pack_kv.1 = (bf16[320,384]{1,0:T(8,128)(2,1)S(1)}, bf16[320,384]{1,0:T(8,128)(2,1)S(1)}, bf16[320,384]{1,0:T(8,128)(2,1)S(1)}, bf16[320,384]{1,0:T(8,128)(2,1)S(1)}) custom-call(bf16[384,768]{1,0:T(8,128)(2,1)} %k_ref.1, bf16[384,512]{1,0:T(8,128)(2,1)} %v_ref.1), custom_call_target="tpu_custom_call" | custom-call | flops 1048576 | bytes 1048576 | tf_op jit(solution)/shard_map/pack_kv/pallas_call | solution.py:76
  1.5 0.6 collective-permute-start.3
  2.0 2.6 %collective-permute-start.4 = (bf16[320,384]{1,0:T(8,128)(2,1)S(1)}, bf16[320,384]{1,0:T(8,128)(2,1)S(1)}, u32[]{:S(2)}, u32[]{:S(2)}) collective-permute-start(bf16[320,384]{1,0:T(8,128)(2,1)S(1)} %get-tuple-element.48), channel_id=1, source_target_pairs={{0,4},{2,6},{4,0},{6,2},{8,12},{10,14},{12,8},{14,10},{16,20},{18,... | collective-permute-start | bytes 737288 | tf_op jit(solution)/shard_map/ppermute | solution.py:625
  4.6 0.0 collective-permute-start.5
  4.6 1.8 %collective-permute-start.6 = (bf16[320,384]{1,0:T(8,128)(2,1)S(1)}, bf16[320,384]{1,0:T(8,128)(2,1)S(1)}, u32[]{:S(2)}, u32[]{:S(2)}) collective-permute-start(bf16[320,384]{1,0:T(8,128)(2,1)S(1)} %get-tuple-element.42.after_ref.refs_4_), channel_id=1, source_target_pairs={{0,8},{2,10},{4,12},{6,14},{8,16},{10,18},{12,20},{14,22},{16,24},... | collective-permute-start | bytes 737288 | tf_op jit(solution)/shard_map/ppermute | solution.py:638
  6.4 1.6 %collective-permute-start.7 = (bf16[320,384]{1,0:T(8,128)(2,1)S(1)}, bf16[320,384]{1,0:T(8,128)(2,1)S(1)}, u32[]{:S(2)}, u32[]{:S(2)}) collective-permute-start(bf16[320,384]{1,0:T(8,128)(2,1)S(1)} %collective-permute-done.3.refs_5_), channel_id=1, source_target_pairs={{0,8},{2,10},{4,12},{6,14},{8,16},{10,18},{12,20},{14,22},{16,24},... | collective-permute-start | bytes 737288 | tf_op jit(solution)/shard_map/ppermute | solution.py:638
  8.0 3.4 %collective-permute-done.4.refs_6_ = bf16[320,384]{1,0:T(8,128)(2,1)S(1)} collective-permute-done((bf16[320,384]{1,0:T(8,128)(2,1)S(1)}, bf16[320,384]{1,0:T(8,128)(2,1)S(1)}, u32[]{:S(2)}, u32[]{:S(2)}) %collective-permute-start.4) | collective-permute-done | bytes 245792 | tf_op jit(solution)/shard_map/ppermute | solution.py:625
  11.4 2.1 %collective-permute-start.8 = (bf16[320,384]{1,0:T(8,128)(2,1)S(1)}, bf16[320,384]{1,0:T(8,128)(2,1)S(1)}, u32[]{:S(2)}, u32[]{:S(2)}) collective-permute-start(bf16[320,384]{1,0:T(8,128)(2,1)S(1)} %collective-permute-done.4.refs_6_), channel_id=1, source_target_pairs={{0,8},{2,10},{4,12},{6,14},{8,16},{10,18},{12,20},{14,22},{16,24},... | collective-permute-start | bytes 737288 | tf_op jit(solution)/shard_map/ppermute | solution.py:638
  13.5 2.6 %collective-permute-done.5.refs_7_.refs_4_ = bf16[320,384]{1,0:T(8,128)(2,1)S(1)} collective-permute-done((bf16[320,384]{1,0:T(8,128)(2,1)S(1)}, bf16[320,384]{1,0:T(8,128)(2,1)S(1)}, u32[]{:S(2)}, u32[]{:S(2)}) %collective-permute-start.5) | collective-permute-done | bytes 245792 | tf_op jit(solution)/shard_map/ppermute | solution.py:625
  16.1 1.5 %collective-permute-start.9 = (bf16[320,384]{1,0:T(8,128)(2,1)S(1)}, bf16[320,384]{1,0:T(8,128)(2,1)S(1)}, u32[]{:S(2)}, u32[]{:S(2)}) collective-permute-start(bf16[320,384]{1,0:T(8,128)(2,1)S(1)} %collective-permute-done.5.refs_7_.refs_4_), channel_id=1, source_target_pairs={{0,8},{2,10},{4,12},{6,14},{8,16},{10,18},{12,20},{14,22},{16,24},... | collective-permute-start | bytes 737288 | tf_op jit(solution)/shard_map/ppermute | solution.py:638
  17.7 1.3 %pack_q.1 = (bf16[240,384]{1,0:T(8,128)(2,1)S(1)}, bf16[240,384]{1,0:T(8,128)(2,1)S(1)}, bf16[240,384]{1,0:T(8,128)(2,1)S(1)}, bf16[240,384]{1,0:T(8,128)(2,1)S(1)}) custom-call(s32[3,16]{1,0:T(4,128)} %layout_hbm.1, bf16[384,768]{1,0:T(8,128)(2,1)} %q_ref.1, bf16[320,384]{1,0:T(8,128)(2,1)S(1)} %get-tuple-element.42.after_ref.refs_4_), custom_call_target="tpu_custom_call" | custom-call | flops 1048576 | bytes 1048576 | tf_op jit(solution)/shard_map/pack_q/pallas_call | solution.py:224
  19.0 0.4 collective-permute-start
  19.5 0.0 collective-permute-done.6.refs_3_.refs_0_
  19.5 1.5 %collective-permute-start.1 = (bf16[240,384]{1,0:T(8,128)(2,1)S(1)}, bf16[240,384]{1,0:T(8,128)(2,1)S(1)}, u32[]{:S(2)}, u32[]{:S(2)}) collective-permute-start(bf16[240,384]{1,0:T(8,128)(2,1)S(1)} %get-tuple-element.45), channel_id=1, source_target_pairs={{0,4},{2,6},{4,0},{6,2},{8,12},{10,14},{12,8},{14,10},{16,20},{18,... | collective-permute-start | bytes 552968 | tf_op jit(solution)/shard_map/ppermute | solution.py:625
  20.9 0.0 collective-permute-done.7.refs_4_.refs_1_
  21.0 0.0 collective-permute-start.2
  21.0 1.5 %cut.1 = (bf16[544,128]{1,0:T(8,128)(2,1)S(1)}, bf16[512,768]{1,0:T(8,128)(2,1)S(1)}, bf16[704,512]{1,0:T(8,128)(2,1)S(1)}) custom-call(bf16[512,2048]{1,0:T(8,128)(2,1)} %w_ref.1, bf16[1,704,2048]{2,1,0:T(8,128)(2,1)} %down_ref.1, s32[1,192]{1,0:T(1,128)} %bitcast.7, bf16[320,384]{1,0:T(8,128)(2,1)S(1)} %get-tuple-element.42.after_ref.refs_4_), custom_call_target="tpu_custom_call" | custom-call | flops 1048576 | bytes 1048576 | tf_op jit(solution)/shard_map/cut/pallas_call | solution.py:124
  22.4 3.4 %collective-permute-done.8.refs_5_.refs_2_ = bf16[320,384]{1,0:T(8,128)(2,1)S(1)} collective-permute-done((bf16[320,384]{1,0:T(8,128)(2,1)S(1)}, bf16[320,384]{1,0:T(8,128)(2,1)S(1)}, u32[]{:S(2)}, u32[]{:S(2)}) %collective-permute-start.8) | collective-permute-done | bytes 245792 | tf_op jit(solution)/shard_map/ppermute | solution.py:638
  25.8 1.7 %collective-permute-start.20 = (bf16[512,768]{1,0:T(8,128)(2,1)S(1)}, bf16[512,768]{1,0:T(8,128)(2,1)S(1)}, u32[]{:S(2)}, u32[]{:S(2)}) collective-permute-start(bf16[512,768]{1,0:T(8,128)(2,1)S(1)} %get-tuple-element.64), channel_id=1, source_target_pairs={{0,1},{1,0},{2,3},{3,2},{4,5},{5,4},{6,7},{7,6},{8,9},{9,8},{10,11... | collective-permute-start | bytes 2359304 | tf_op jit(solution)/shard_map/ppermute | solution.py:628
  27.6 3.2 %collective-permute-done.9.refs_6_.refs_3_ = bf16[320,384]{1,0:T(8,128)(2,1)S(1)} collective-permute-done((bf16[320,384]{1,0:T(8,128)(2,1)S(1)}, bf16[320,384]{1,0:T(8,128)(2,1)S(1)}, u32[]{:S(2)}, u32[]{:S(2)}) %collective-permute-start.9) | collective-permute-done | bytes 245792 | tf_op jit(solution)/shard_map/ppermute | solution.py:638
  30.7 1.5 %collective-permute-start.27 = (bf16[704,512]{1,0:T(8,128)(2,1)S(1)}, bf16[704,512]{1,0:T(8,128)(2,1)S(1)}, u32[]{:S(2)}, u32[]{:S(2)}) collective-permute-start(bf16[704,512]{1,0:T(8,128)(2,1)S(1)} %get-tuple-element.76), channel_id=1, source_target_pairs={{0,1},{1,0},{2,3},{3,2},{4,5},{5,4},{6,7},{7,6},{8,9},{9,8},{10,11... | collective-permute-start | bytes 2162696 | tf_op jit(solution)/shard_map/ppermute | solution.py:628
  32.3 0.0 collective-permute-done.refs_1_
  32.3 0.1 collective-permute-start.10
  32.4 0.0 collective-permute-done.1.refs_2_
  32.4 1.3 %collective-permute-start.11 = (bf16[320,384]{1,0:T(8,128)(2,1)S(1)}, bf16[320,384]{1,0:T(8,128)(2,1)S(1)}, u32[]{:S(2)}, u32[]{:S(2)}) collective-permute-start(bf16[320,384]{1,0:T(8,128)(2,1)S(1)} %shard_map.112), channel_id=1, source_target_pairs={{0,8},{2,10},{4,12},{6,14},{8,16},{10,18},{12,20},{14,22},{16,24},... | collective-permute-start | bytes 737288 | tf_op jit(solution)/shard_map/ppermute | solution.py:638
  33.7 0.0 collective-permute-done.2.refs_3_
  33.7 3.6 %shard_map.109 = (bf16[1536,256]{1,0:T(8,128)(2,1)S(1)}, f32[1536,128]{1,0:T(8,128)S(1)}, f32[1536,256]{1,0:T(8,128)S(1)}) custom-call(bf16[240,384]{1,0:T(8,128)(2,1)S(1)} %get-tuple-element.43.refs_0_, bf16[240,384]{1,0:T(8,128)(2,1)S(1)} %collective-permute-done.refs_1_, bf16[240,384]{1,0:T(8,128)(2,1)S(1)} %collective-permute-done.1.refs_2_, ...), custom_call_target="tpu_custom_call" | custom-call | flops 2415919104 | bytes 1048576 | tf_op jit(solution)/shard_map/pallas_call | solution.py:378
  37.2 0.1 shard_map.114
  37.3 0.9 collective-permute-start.12
  38.2 3.7 %shard_map.110 = (f32[1536,128]{1,0:T(8,128)S(1)}, f32[1536,256]{1,0:T(8,128)S(1)}) custom-call(bf16[1536,256]{1,0:T(8,128)(2,1)S(1)} %get-tuple-element.50.refs_0_, f32[1536,128]{1,0:T(8,128)S(1)} %get-tuple-element.51.refs_1_, f32[1536,256]{1,0:T(8,128)S(1)} %get-tuple-element.52.refs_2_, ...), custom_call_target="tpu_custom_call", output_to_operand_aliasing={{0}: (1, {}), {1}: (2, {})} | custom-call | flops 2415919104 | bytes 1048576 | tf_op jit(solution)/shard_map/pallas_call | solution.py:378
  41.9 1.1 collective-permute-done.10.refs_3_
  43.0 3.6 %collective-permute-done.11.refs_4_ = bf16[320,384]{1,0:T(8,128)(2,1)S(1)} collective-permute-done((bf16[320,384]{1,0:T(8,128)(2,1)S(1)}, bf16[320,384]{1,0:T(8,128)(2,1)S(1)}, u32[]{:S(2)}, u32[]{:S(2)}) %collective-permute-start.11) | collective-permute-done | bytes 245792 | tf_op jit(solution)/shard_map/ppermute | solution.py:638
  46.6 1.8 %shard_map.113 = (f32[1536,128]{1,0:T(8,128)S(1)}, f32[1536,256]{1,0:T(8,128)S(1)}, bf16[1536,128]{1,0:T(8,128)(2,1)S(1)}) custom-call(bf16[1536,256]{1,0:T(8,128)(2,1)S(1)} %get-tuple-element.50.refs_0_, f32[1536,128]{1,0:T(8,128)S(1)} %get-tuple-element.53.refs_1_, ...), custom_call_target="tpu_custom_call", output_to_operand_aliasing={{0}: (1, {}), {1}: (2, {})} | custom-call | flops 905969664 | bytes 1048576 | tf_op jit(solution)/shard_map/pallas_call | solution.py:378
  48.3 1.5 %shard_map.115 = (bf16[384,128]{1,0:T(8,128)(2,1)S(1)}, bf16[384,128]{1,0:T(8,128)(2,1)S(1)}, bf16[384,128]{1,0:T(8,128)(2,1)S(1)}, bf16[384,128]{1,0:T(8,128)(2...) custom-call(bf16[1536,256]{1,0:T(8,128)(2,1)S(1)} %get-tuple-element, ...), custom_call_target="tpu_custom_call", output_to_operand_aliasing={{8}: (3, {})} | custom-call | flops 301989888 | bytes 1048576 | tf_op jit(solution)/shard_map/pallas_call | solution.py:378
  49.9 0.1 collective-permute-start.13
  50.0 1.3 %collective-permute-done.13.refs_1_ = bf16[384,128]{1,0:T(8,128)(2,1)S(1)} collective-permute-done((bf16[384,128]{1,0:T(8,128)(2,1)S(1)}, bf16[384,128]{1,0:T(8,128)(2,1)S(1)}, u32[]{:S(2)}, u32[]{:S(2)}) %collective-permute-start.13) | collective-permute-done | bytes 98336 | tf_op jit(solution)/shard_map/ppermute | solution.py:625
  51.3 0.2 collective-permute-start.21
  51.4 0.7 collective-permute-start.17
  52.1 9.5 %collective-permute-done.27.refs_0_ = bf16[704,512]{1,0:T(8,128)(2,1)S(1)} collective-permute-done((bf16[704,512]{1,0:T(8,128)(2,1)S(1)}, bf16[704,512]{1,0:T(8,128)(2,1)S(1)}, u32[]{:S(2)}, u32[]{:S(2)}) %collective-permute-start.27) | collective-permute-done | bytes 720928 | tf_op jit(solution)/shard_map/ppermute | solution.py:628
  61.6 1.3 %collective-permute-start.28 = (bf16[704,512]{1,0:T(8,128)(2,1)S(1)}, bf16[704,512]{1,0:T(8,128)(2,1)S(1)}, u32[]{:S(2)}, u32[]{:S(2)}) collective-permute-start(bf16[704,512]{1,0:T(8,128)(2,1)S(1)} %collective-permute-done.27.refs_0_), channel_id=1, source_target_pairs={{0,4},{2,6},{4,0},{6,2},{8,12},{10,14},{12,8},{14,10},{16,20},{18,... | collective-permute-start | bytes 2162696 | tf_op jit(solution)/shard_map/ppermute | solution.py:625
  62.9 0.2 collective-permute-done.17.own_ref.refs_6_.refs_9_
  63.1 1.3 %collective-permute-start.18 = (bf16[544,128]{1,0:T(8,128)(2,1)S(1)}, bf16[544,128]{1,0:T(8,128)(2,1)S(1)}, u32[]{:S(2)}, u32[]{:S(2)}) collective-permute-start(bf16[544,128]{1,0:T(8,128)(2,1)S(1)} %collective-permute-done.17.own_ref.refs_6_.refs_9_), channel_id=1, source_target_pairs={{0,4},{2,6},{4,0},{6,2},{8,12},{10,14},{12,8},{14,10},{16,20},{18,... | collective-permute-start | bytes 417800 | tf_op jit(solution)/shard_map/ppermute | solution.py:625
  64.4 15.4 %collective-permute-done.18.other_ref = bf16[544,128]{1,0:T(8,128)(2,1)S(1)} collective-permute-done((bf16[544,128]{1,0:T(8,128)(2,1)S(1)}, bf16[544,128]{1,0:T(8,128)(2,1)S(1)}, u32[]{:S(2)}, u32[]{:S(2)}) %collective-permute-start.18) | collective-permute-done | bytes 139296 | tf_op jit(solution)/shard_map/ppermute | solution.py:625
  79.8 0.1 join_outer.1.refs_2_.refs_5_
  79.9 0.1 collective-permute-start.19
  79.9 0.9 collective-permute-start.14
  80.8 0.9 collective-permute-start.15
  81.8 0.9 collective-permute-start.22
  82.7 4.2 %stage.1 = (bf16[1,704,2048]{2,1,0:T(8,128)(2,1)S(1)}, bf16[1,704,2048]{2,1,0:T(8,128)(2,1)S(1)}, bf16[512,2048]{1,0:T(8,128)(2,1)S(1)}, bf16[1,704,2048]{2,1,0:T(8,128)(2,1)S(1)}) custom-call(bf16[1,704,2048]{2,1,0:T(8,128)(2,1)} %bitcast.10, bf16[1,704,2048]{2,1,0:T(8,128)(2,1)} %bitcast.11, bf16[512,2048]{1,0:T(8,128)(2,1)} %w_ref.1, ...), custom_call_target="tpu_custom_call" | custom-call | flops 1048576 | bytes 1048576 | tf_op jit(solution)/shard_map/stage/pallas_call | solution.py:173
  86.8 0.0 copy-start
  86.8 0.9 collective-permute-start.23
  87.8 1.8 %collective-permute-start.24 = (bf16[192,128]{1,0:T(8,128)(2,1)S(1)}, bf16[192,128]{1,0:T(8,128)(2,1)S(1)}, u32[]{:S(2)}, u32[]{:S(2)}) collective-permute-start(bf16[192,128]{1,0:T(8,128)(2,1)S(1)} %get-tuple-element.74), channel_id=1, source_target_pairs={{0,5},{1,4},{2,7},{3,6},{4,1},{5,0},{6,3},{7,2},{8,13},{9,12},{10,... | collective-permute-start | bytes 147464 | tf_op jit(solution)/shard_map/ppermute | solution.py:632
  89.6 0.9 collective-permute-start.25
  90.5 1.0 half_out.1.refs_0_
  91.5 1.3 %collective-permute-done.24.refs_3_ = bf16[192,128]{1,0:T(8,128)(2,1)S(1)} collective-permute-done((bf16[192,128]{1,0:T(8,128)(2,1)S(1)}, bf16[192,128]{1,0:T(8,128)(2,1)S(1)}, u32[]{:S(2)}, u32[]{:S(2)}) %collective-permute-start.24) | collective-permute-done | bytes 49184 | tf_op jit(solution)/shard_map/ppermute | solution.py:632
  92.8 1.4 %collective-permute-done.25.refs_4_ = bf16[192,128]{1,0:T(8,128)(2,1)S(1)} collective-permute-done((bf16[192,128]{1,0:T(8,128)(2,1)S(1)}, bf16[192,128]{1,0:T(8,128)(2,1)S(1)}, u32[]{:S(2)}, u32[]{:S(2)}) %collective-permute-start.25) | collective-permute-done | bytes 49184 | tf_op jit(solution)/shard_map/ppermute | solution.py:632
  94.2 2.9 %hidden_peer.1 = bf16[792,128]{1,0:T(8,128)(2,1)S(1)} custom-call(f32[384,2048]{1,0:T(8,128)S(1)} %half_out.1.refs_0_, bf16[192,128]{1,0:T(8,128)(2,1)S(1)} %collective-permute-done.22.refs_1_, bf16[192,128]{1,0:T(8,128)(2,1)S(1)} %collective-permute-done.23.refs_2_, bf16[192,128]{1,0:T(8,128)(2,1)S(1)} %collective-permute-done.24.refs_3_, ...), custom_call_target="tpu_custom_call" | custom-call | flops 1912602624 | bytes 1048576 | tf_op jit(solution)/shard_map/hidden_peer/pallas_call | solution.py:553
  97.1 0.2 collective-permute-start.29
  97.3 0.4 collective-permute-start.30
  97.7 0.6 collective-permute-start.16
  98.3 1.5 %collective-permute-start.26 = (bf16[792,128]{1,0:T(8,128)(2,1)S(1)}, bf16[792,128]{1,0:T(8,128)(2,1)S(1)}, u32[]{:S(2)}, u32[]{:S(2)}) collective-permute-start(bf16[792,128]{1,0:T(8,128)(2,1)S(1)} %hidden_peer.1), channel_id=1, source_target_pairs={{0,1},{1,0},{2,3},{3,2},{4,5},{5,4},{6,7},{7,6},{8,9},{9,8},{10,11... | collective-permute-start | bytes 608264 | tf_op jit(solution)/shard_map/ppermute | solution.py:628
  99.8 5.7 %collective-permute-done.16.refs_1_ = bf16[768,128]{1,0:T(8,128)(2,1)S(1)} collective-permute-done((bf16[768,128]{1,0:T(8,128)(2,1)S(1)}, bf16[768,128]{1,0:T(8,128)(2,1)S(1)}, u32[]{:S(2)}, u32[]{:S(2)}) %collective-permute-start.16) | collective-permute-done | bytes 196640 | tf_op jit(solution)/shard_map/ppermute | solution.py:628
  105.5 3.6 %hidden_own.1 = (f32[192,2048]{1,0:T(8,128)S(1)}, f32[192,2048]{1,0:T(8,128)S(1)}, bf16[192,144]{1,0:T(8,128)(2,1)S(1)}) custom-call(f32[384,2048]{1,0:T(8,128)S(1)} %half_out.1.refs_0_, bf16[768,128]{1,0:T(8,128)(2,1)S(1)} %collective-permute-done.16.refs_1_, bf16[512,256]{1,0:T(8,128)(2,1)S(1)} %join_outer.1.refs_2_.refs_5_, ...), custom_call_target="tpu_custom_call" | custom-call | flops 1912602624 | bytes 1048576 | tf_op jit(solution)/shard_map/hidden_own/pallas_call | solution.py:553
  109.2 1.7 %combine.1 = bf16[192,2048]{1,0:T(8,128)(2,1)} custom-call(f32[192,2048]{1,0:T(8,128)S(1)} %get-tuple-element.69.attended, f32[192,2048]{1,0:T(8,128)S(1)} %get-tuple-element.70.partial, bf16[192,144]{1,0:T(8,128)(2,1)S(1)} %get-tuple-element.71.place, bf16[792,128]{1,0:T(8,128)(2,1)S(1)} %collective-permute-done.26.hid_peer, f32[1,192]{1,0:T(1,128)S(1)} %bitcast.9, ...), custom_call_target="tpu_custom_call" | custom-call | flops 1048576 | bytes 1048576 | tf_op jit(solution)/shard_map/combine/pallas_call | solution.py:589
  (21 shorter events, 0.1 us)
Async XLA Ops:
  1.5 5.0 %collective-permute-start.3 = (bf16[320,384]{1,0:T(8,128)(2,1)S(1)}, bf16[320,384]{1,0:T(8,128)(2,1)S(1)}, u32[]{:S(2)}, u32[]{:S(2)}) collective-permute-start(bf16[320,384]{1,0:T(8,128)(2,1)S(1)} %get-tuple-element.47), channel_id=1, source_target_pairs={{0,2},{2,0},{4,6},{6,4},{8,10},{10,8},{12,14},{14,12},{16,18},{18,... | collective-permute-start | bytes 737288 | tf_op jit(solution)/shard_map/ppermute | solution.py:625
  2.0 9.4 %collective-permute-start.4 = (bf16[320,384]{1,0:T(8,128)(2,1)S(1)}, bf16[320,384]{1,0:T(8,128)(2,1)S(1)}, u32[]{:S(2)}, u32[]{:S(2)}) collective-permute-start(bf16[320,384]{1,0:T(8,128)(2,1)S(1)} %get-tuple-element.48), channel_id=1, source_target_pairs={{0,4},{2,6},{4,0},{6,2},{8,12},{10,14},{12,8},{14,10},{16,20},{18,... | collective-permute-start | bytes 737288 | tf_op jit(solution)/shard_map/ppermute | solution.py:625
  4.6 11.6 %collective-permute-start.5 = (bf16[320,384]{1,0:T(8,128)(2,1)S(1)}, bf16[320,384]{1,0:T(8,128)(2,1)S(1)}, u32[]{:S(2)}, u32[]{:S(2)}) collective-permute-start(bf16[320,384]{1,0:T(8,128)(2,1)S(1)} %get-tuple-element.49), channel_id=1, source_target_pairs={{0,6},{2,4},{4,2},{6,0},{8,14},{10,12},{12,10},{14,8},{16,22},{18,... | collective-permute-start | bytes 737288 | tf_op jit(solution)/shard_map/ppermute | solution.py:625
  4.6 14.8 %collective-permute-start.6 = (bf16[320,384]{1,0:T(8,128)(2,1)S(1)}, bf16[320,384]{1,0:T(8,128)(2,1)S(1)}, u32[]{:S(2)}, u32[]{:S(2)}) collective-permute-start(bf16[320,384]{1,0:T(8,128)(2,1)S(1)} %get-tuple-element.42.after_ref.refs_4_), channel_id=1, source_target_pairs={{0,8},{2,10},{4,12},{6,14},{8,16},{10,18},{12,20},{14,22},{16,24},... | collective-permute-start | bytes 737288 | tf_op jit(solution)/shard_map/ppermute | solution.py:638
  6.4 14.5 %collective-permute-start.7 = (bf16[320,384]{1,0:T(8,128)(2,1)S(1)}, bf16[320,384]{1,0:T(8,128)(2,1)S(1)}, u32[]{:S(2)}, u32[]{:S(2)}) collective-permute-start(bf16[320,384]{1,0:T(8,128)(2,1)S(1)} %collective-permute-done.3.refs_5_), channel_id=1, source_target_pairs={{0,8},{2,10},{4,12},{6,14},{8,16},{10,18},{12,20},{14,22},{16,24},... | collective-permute-start | bytes 737288 | tf_op jit(solution)/shard_map/ppermute | solution.py:638
  11.4 14.4 %collective-permute-start.8 = (bf16[320,384]{1,0:T(8,128)(2,1)S(1)}, bf16[320,384]{1,0:T(8,128)(2,1)S(1)}, u32[]{:S(2)}, u32[]{:S(2)}) collective-permute-start(bf16[320,384]{1,0:T(8,128)(2,1)S(1)} %collective-permute-done.4.refs_6_), channel_id=1, source_target_pairs={{0,8},{2,10},{4,12},{6,14},{8,16},{10,18},{12,20},{14,22},{16,24},... | collective-permute-start | bytes 737288 | tf_op jit(solution)/shard_map/ppermute | solution.py:638
  16.1 14.6 %collective-permute-start.9 = (bf16[320,384]{1,0:T(8,128)(2,1)S(1)}, bf16[320,384]{1,0:T(8,128)(2,1)S(1)}, u32[]{:S(2)}, u32[]{:S(2)}) collective-permute-start(bf16[320,384]{1,0:T(8,128)(2,1)S(1)} %collective-permute-done.5.refs_7_.refs_4_), channel_id=1, source_target_pairs={{0,8},{2,10},{4,12},{6,14},{8,16},{10,18},{12,20},{14,22},{16,24},... | collective-permute-start | bytes 737288 | tf_op jit(solution)/shard_map/ppermute | solution.py:638
  19.0 13.3 %collective-permute-start = (bf16[240,384]{1,0:T(8,128)(2,1)S(1)}, bf16[240,384]{1,0:T(8,128)(2,1)S(1)}, u32[]{:S(2)}, u32[]{:S(2)}) collective-permute-start(bf16[240,384]{1,0:T(8,128)(2,1)S(1)} %get-tuple-element.44), channel_id=1, source_target_pairs={{0,2},{2,0},{4,6},{6,4},{8,10},{10,8},{12,14},{14,12},{16,18},{18,... | collective-permute-start | bytes 552968 | tf_op jit(solution)/shard_map/ppermute | solution.py:625
  19.5 12.9 %collective-permute-start.1 = (bf16[240,384]{1,0:T(8,128)(2,1)S(1)}, bf16[240,384]{1,0:T(8,128)(2,1)S(1)}, u32[]{:S(2)}, u32[]{:S(2)}) collective-permute-start(bf16[240,384]{1,0:T(8,128)(2,1)S(1)} %get-tuple-element.45), channel_id=1, source_target_pairs={{0,4},{2,6},{4,0},{6,2},{8,12},{10,14},{12,8},{14,10},{16,20},{18,... | collective-permute-start | bytes 552968 | tf_op jit(solution)/shard_map/ppermute | solution.py:625
  21.0 12.7 %collective-permute-start.2 = (bf16[240,384]{1,0:T(8,128)(2,1)S(1)}, bf16[240,384]{1,0:T(8,128)(2,1)S(1)}, u32[]{:S(2)}, u32[]{:S(2)}) collective-permute-start(bf16[240,384]{1,0:T(8,128)(2,1)S(1)} %get-tuple-element.46), channel_id=1, source_target_pairs={{0,6},{2,4},{4,2},{6,0},{8,14},{10,12},{12,10},{14,8},{16,22},{18,... | collective-permute-start | bytes 552968 | tf_op jit(solution)/shard_map/ppermute | solution.py:625
  25.8 24.2 %collective-permute-start.20 = (bf16[512,768]{1,0:T(8,128)(2,1)S(1)}, bf16[512,768]{1,0:T(8,128)(2,1)S(1)}, u32[]{:S(2)}, u32[]{:S(2)}) collective-permute-start(bf16[512,768]{1,0:T(8,128)(2,1)S(1)} %get-tuple-element.64), channel_id=1, source_target_pairs={{0,1},{1,0},{2,3},{3,2},{4,5},{5,4},{6,7},{7,6},{8,9},{9,8},{10,11... | collective-permute-start | bytes 2359304 | tf_op jit(solution)/shard_map/ppermute | solution.py:628
  30.7 30.9 %collective-permute-start.27 = (bf16[704,512]{1,0:T(8,128)(2,1)S(1)}, bf16[704,512]{1,0:T(8,128)(2,1)S(1)}, u32[]{:S(2)}, u32[]{:S(2)}) collective-permute-start(bf16[704,512]{1,0:T(8,128)(2,1)S(1)} %get-tuple-element.76), channel_id=1, source_target_pairs={{0,1},{1,0},{2,3},{3,2},{4,5},{5,4},{6,7},{7,6},{8,9},{9,8},{10,11... | collective-permute-start | bytes 2162696 | tf_op jit(solution)/shard_map/ppermute | solution.py:628
  32.3 10.7 %collective-permute-start.10 = (bf16[320,384]{1,0:T(8,128)(2,1)S(1)}, bf16[320,384]{1,0:T(8,128)(2,1)S(1)}, u32[]{:S(2)}, u32[]{:S(2)}) collective-permute-start(bf16[320,384]{1,0:T(8,128)(2,1)S(1)} %shard_map.111), channel_id=1, source_target_pairs={{0,8},{2,10},{4,12},{6,14},{8,16},{10,18},{12,20},{14,22},{16,24},... | collective-permute-start | bytes 737288 | tf_op jit(solution)/shard_map/ppermute | solution.py:638
  32.4 14.2 %collective-permute-start.11 = (bf16[320,384]{1,0:T(8,128)(2,1)S(1)}, bf16[320,384]{1,0:T(8,128)(2,1)S(1)}, u32[]{:S(2)}, u32[]{:S(2)}) collective-permute-start(bf16[320,384]{1,0:T(8,128)(2,1)S(1)} %shard_map.112), channel_id=1, source_target_pairs={{0,8},{2,10},{4,12},{6,14},{8,16},{10,18},{12,20},{14,22},{16,24},... | collective-permute-start | bytes 737288 | tf_op jit(solution)/shard_map/ppermute | solution.py:638
  37.3 11.0 %collective-permute-start.12 = (bf16[320,384]{1,0:T(8,128)(2,1)S(1)}, bf16[320,384]{1,0:T(8,128)(2,1)S(1)}, u32[]{:S(2)}, u32[]{:S(2)}) collective-permute-start(bf16[320,384]{1,0:T(8,128)(2,1)S(1)} %shard_map.114), channel_id=1, source_target_pairs={{8,16},{10,18},{12,20},{14,22},{16,24},{18,26},{20,28},{22,30},{9,... | collective-permute-start | bytes 737288 | tf_op jit(solution)/shard_map/ppermute | solution.py:638
  49.9 1.4 %collective-permute-start.13 = (bf16[384,128]{1,0:T(8,128)(2,1)S(1)}, bf16[384,128]{1,0:T(8,128)(2,1)S(1)}, u32[]{:S(2)}, u32[]{:S(2)}) collective-permute-start(bf16[384,128]{1,0:T(8,128)(2,1)S(1)} %get-tuple-element.59), channel_id=1, source_target_pairs={{0,2},{2,0},{4,6},{6,4},{8,10},{10,8},{12,14},{14,12},{16,18},{18,... | collective-permute-start | bytes 294920 | tf_op jit(solution)/shard_map/ppermute | solution.py:625
  51.3 42.9 %collective-permute-start.21 = (bf16[512,768]{1,0:T(8,128)(2,1)S(1)}, bf16[512,768]{1,0:T(8,128)(2,1)S(1)}, u32[]{:S(2)}, u32[]{:S(2)}) collective-permute-start(bf16[512,768]{1,0:T(8,128)(2,1)S(1)} %collective-permute-done.20.refs_4_.refs_7_), channel_id=1, source_target_pairs={{0,2},{2,0},{4,6},{6,4},{8,10},{10,8},{12,14},{14,12},{16,18},{18,... | collective-permute-start | bytes 2359304 | tf_op jit(solution)/shard_map/ppermute | solution.py:625
  51.4 11.7 %collective-permute-start.17 = (bf16[544,128]{1,0:T(8,128)(2,1)S(1)}, bf16[544,128]{1,0:T(8,128)(2,1)S(1)}, u32[]{:S(2)}, u32[]{:S(2)}) collective-permute-start(bf16[544,128]{1,0:T(8,128)(2,1)S(1)} %get-tuple-element.63), channel_id=1, source_target_pairs={{0,1},{1,0},{2,3},{3,2},{4,5},{5,4},{6,7},{7,6},{8,9},{9,8},{10,11... | collective-permute-start | bytes 417800 | tf_op jit(solution)/shard_map/ppermute | solution.py:628
  61.6 35.4 %collective-permute-start.28 = (bf16[704,512]{1,0:T(8,128)(2,1)S(1)}, bf16[704,512]{1,0:T(8,128)(2,1)S(1)}, u32[]{:S(2)}, u32[]{:S(2)}) collective-permute-start(bf16[704,512]{1,0:T(8,128)(2,1)S(1)} %collective-permute-done.27.refs_0_), channel_id=1, source_target_pairs={{0,4},{2,6},{4,0},{6,2},{8,12},{10,14},{12,8},{14,10},{16,20},{18,... | collective-permute-start | bytes 2162696 | tf_op jit(solution)/shard_map/ppermute | solution.py:625
  63.1 16.6 %collective-permute-start.18 = (bf16[544,128]{1,0:T(8,128)(2,1)S(1)}, bf16[544,128]{1,0:T(8,128)(2,1)S(1)}, u32[]{:S(2)}, u32[]{:S(2)}) collective-permute-start(bf16[544,128]{1,0:T(8,128)(2,1)S(1)} %collective-permute-done.17.own_ref.refs_6_.refs_9_), channel_id=1, source_target_pairs={{0,4},{2,6},{4,0},{6,2},{8,12},{10,14},{12,8},{14,10},{16,20},{18,... | collective-permute-start | bytes 417800 | tf_op jit(solution)/shard_map/ppermute | solution.py:625
  79.9 1.9 %collective-permute-start.19 = (bf16[512,256]{1,0:T(8,128)(2,1)S(1)}, bf16[512,256]{1,0:T(8,128)(2,1)S(1)}, u32[]{:S(2)}, u32[]{:S(2)}) collective-permute-start(bf16[512,256]{1,0:T(8,128)(2,1)S(1)} %join_outer.1.refs_2_.refs_5_), channel_id=1, source_target_pairs={{0,2},{2,0},{4,6},{6,4},{8,10},{10,8},{12,14},{14,12},{16,18},{18,... | collective-permute-start | bytes 786440 | tf_op jit(solution)/shard_map/ppermute | solution.py:625
  79.9 7.8 %collective-permute-start.14 = (bf16[384,128]{1,0:T(8,128)(2,1)S(1)}, bf16[384,128]{1,0:T(8,128)(2,1)S(1)}, u32[]{:S(2)}, u32[]{:S(2)}) collective-permute-start(bf16[384,128]{1,0:T(8,128)(2,1)S(1)} %get-tuple-element.60), channel_id=1, source_target_pairs={{0,4},{2,6},{4,0},{6,2},{8,12},{10,14},{12,8},{14,10},{16,20},{18,... | collective-permute-start | bytes 294920 | tf_op jit(solution)/shard_map/ppermute | solution.py:625
  80.8 8.7 %collective-permute-start.15 = (bf16[384,128]{1,0:T(8,128)(2,1)S(1)}, bf16[384,128]{1,0:T(8,128)(2,1)S(1)}, u32[]{:S(2)}, u32[]{:S(2)}) collective-permute-start(bf16[384,128]{1,0:T(8,128)(2,1)S(1)} %get-tuple-element.61), channel_id=1, source_target_pairs={{0,6},{2,4},{4,2},{6,0},{8,14},{10,12},{12,10},{14,8},{16,22},{18,... | collective-permute-start | bytes 294920 | tf_op jit(solution)/shard_map/ppermute | solution.py:625
  81.8 5.1 %collective-permute-start.22 = (bf16[192,128]{1,0:T(8,128)(2,1)S(1)}, bf16[192,128]{1,0:T(8,128)(2,1)S(1)}, u32[]{:S(2)}, u32[]{:S(2)}) collective-permute-start(bf16[192,128]{1,0:T(8,128)(2,1)S(1)} %get-tuple-element.72), channel_id=1, source_target_pairs={{0,1},{1,0},{2,3},{3,2},{4,5},{5,4},{6,7},{7,6},{8,9},{9,8},{10,11... | collective-permute-start | bytes 147464 | tf_op jit(solution)/shard_map/ppermute | solution.py:628
  86.8 7.3 %copy-start = (f32[2048]{0:T(1024)S(1)}, f32[2048]{0:T(1024)}, u32[]{:S(2)}) copy-start(f32[2048]{0:T(1024)} %param.16) | copy-start | bytes 24580
  86.8 4.6 %collective-permute-start.23 = (bf16[192,128]{1,0:T(8,128)(2,1)S(1)}, bf16[192,128]{1,0:T(8,128)(2,1)S(1)}, u32[]{:S(2)}, u32[]{:S(2)}) collective-permute-start(bf16[192,128]{1,0:T(8,128)(2,1)S(1)} %get-tuple-element.73), channel_id=1, source_target_pairs={{0,3},{1,2},{2,1},{3,0},{4,7},{5,6},{6,5},{7,4},{8,11},{9,10},{10,... | collective-permute-start | bytes 147464 | tf_op jit(solution)/shard_map/ppermute | solution.py:632
  87.8 5.0 %collective-permute-start.24 = (bf16[192,128]{1,0:T(8,128)(2,1)S(1)}, bf16[192,128]{1,0:T(8,128)(2,1)S(1)}, u32[]{:S(2)}, u32[]{:S(2)}) collective-permute-start(bf16[192,128]{1,0:T(8,128)(2,1)S(1)} %get-tuple-element.74), channel_id=1, source_target_pairs={{0,5},{1,4},{2,7},{3,6},{4,1},{5,0},{6,3},{7,2},{8,13},{9,12},{10,... | collective-permute-start | bytes 147464 | tf_op jit(solution)/shard_map/ppermute | solution.py:632
  89.6 4.6 %collective-permute-start.25 = (bf16[192,128]{1,0:T(8,128)(2,1)S(1)}, bf16[192,128]{1,0:T(8,128)(2,1)S(1)}, u32[]{:S(2)}, u32[]{:S(2)}) collective-permute-start(bf16[192,128]{1,0:T(8,128)(2,1)S(1)} %get-tuple-element.75), channel_id=1, source_target_pairs={{0,7},{1,6},{2,5},{3,4},{4,3},{5,2},{6,1},{7,0},{8,15},{9,14},{10,... | collective-permute-start | bytes 147464 | tf_op jit(solution)/shard_map/ppermute | solution.py:632
  94.2 11.4 %copy-start.1 = (s32[192,1]{0,1:T(1,128)S(1)}, s32[192,1]{0,1:T(1,128)}, u32[]{:S(2)}) copy-start(s32[192,1]{0,1:T(1,128)} %param.17) | copy-start | bytes 2308
  97.1 12.1 %collective-permute-start.29 = (bf16[704,512]{1,0:T(8,128)(2,1)S(1)}, bf16[704,512]{1,0:T(8,128)(2,1)S(1)}, u32[]{:S(2)}, u32[]{:S(2)}) collective-permute-start(bf16[704,512]{1,0:T(8,128)(2,1)S(1)} %collective-permute-done.27.refs_0_), channel_id=1, source_target_pairs={{0,2},{2,0},{4,6},{6,4},{8,10},{10,8},{12,14},{14,12},{16,18},{18,... | collective-permute-start | bytes 2162696 | tf_op jit(solution)/shard_map/ppermute | solution.py:625
  97.3 11.9 %collective-permute-start.30 = (bf16[704,512]{1,0:T(8,128)(2,1)S(1)}, bf16[704,512]{1,0:T(8,128)(2,1)S(1)}, u32[]{:S(2)}, u32[]{:S(2)}) collective-permute-start(bf16[704,512]{1,0:T(8,128)(2,1)S(1)} %collective-permute-done.28.refs_2_), channel_id=1, source_target_pairs={{0,2},{2,0},{4,6},{6,4},{8,10},{10,8},{12,14},{14,12},{16,18},{18,... | collective-permute-start | bytes 2162696 | tf_op jit(solution)/shard_map/ppermute | solution.py:625
  97.7 7.8 %collective-permute-start.16 = (bf16[768,128]{1,0:T(8,128)(2,1)S(1)}, bf16[768,128]{1,0:T(8,128)(2,1)S(1)}, u32[]{:S(2)}, u32[]{:S(2)}) collective-permute-start(bf16[768,128]{1,0:T(8,128)(2,1)S(1)} %own_tokens.1), channel_id=1, source_target_pairs={{0,1},{1,0},{2,3},{3,2},{4,5},{5,4},{6,7},{7,6},{8,9},{9,8},{10,11... | collective-permute-start | bytes 589832 | tf_op jit(solution)/shard_map/ppermute | solution.py:628
  98.3 10.9 %collective-permute-start.26 = (bf16[792,128]{1,0:T(8,128)(2,1)S(1)}, bf16[792,128]{1,0:T(8,128)(2,1)S(1)}, u32[]{:S(2)}, u32[]{:S(2)}) collective-permute-start(bf16[792,128]{1,0:T(8,128)(2,1)S(1)} %hidden_peer.1), channel_id=1, source_target_pairs={{0,1},{1,0},{2,3},{3,2},{4,5},{5,4},{6,7},{7,6},{8,9},{9,8},{10,11... | collective-permute-start | bytes 608264 | tf_op jit(solution)/shard_map/ppermute | solution.py:628
  105.5 3.7 %copy-start.2 = (f32[192,1]{0,1:T(1,128)S(1)}, f32[192,1]{0,1:T(1,128)}, u32[]{:S(2)}) copy-start(f32[192,1]{0,1:T(1,128)} %param.18) | copy-start | bytes 2308
